TPU v7x, 128 devices: a whole 4x4x4 slice. The times are simulated.
128 devices in a mesh: rows: 16 (over y, x), cols: 8 (over z, core).
Axes of the slice: x: 4, y: 4, z: 4, core: 2. Of those that a mesh axis runs over, the one named last changes fastest.
Arguments:
- fmap1: bfloat16 [2, 512, 512, 256], P(None, 'rows', 'cols'), may hold values from -6 to 6
- fmap2: bfloat16 [2, 512, 512, 256], P(None, 'rows', 'cols'), may hold values from -6 to 6
- target_owner: int32 [2, 8192, 1], P(None, ('rows', 'cols')), may hold values from 0 to 127; in each aligned block of 64 rows (0 to 63, 64 to 127, ..., all dimensions but the last counted through in order) at most 2 rows name the same one
- target_tile: int32 [2, 8192], P(None, ('rows', 'cols')), may hold values from 0 to 31
Outputs:
- corr: float32 [2, 81, 524288], P(None, None, ('rows', 'cols'))
Inputs may be any that keep to these rules, and one draw needn't show every extreme that they name: `target_owner`: at each level, the 64 query blocks of one region (aligned blocks of rows) name any one owner at most 2 times, a bound that some block reaches. `target_tile`: tile of the owner's region in the query block's frame, numbered row-major; level l uses it modulo that level's tile count.
All inputs are finite; a program needn't handle non-finite values.
Results may differ from a plain program's by a relative error of at most 0.0013.
Values may be sent and summed in bfloat16 or wider, within the bound.
No kernel may reach another device: no remote copies, remote signals or barrier semaphores. Data moves between devices by JAX's collectives and lax.ppermute only.
A program may use at most 128 MiB of HBM per device.

v0:
```python
import jax
import jax.numpy as jnp
from jax import lax
from jax.experimental import pallas as pl
from jax.experimental.pallas import tpu as pltpu
from jax.sharding import PartitionSpec as P


RADIUS = 4
LEVELS = 2
SIDE = 2 * RADIUS
SPAN = 4 * RADIUS
WIN = 2 * RADIUS + 1
WINDOW = WIN * WIN
QUERIES = SIDE * SIDE
SLOTS = 2
LANES = SLOTS * QUERIES
REPLY_ROWS = -(-LEVELS * (WINDOW + 1) // 8) * 8
PEERS_A_STEP = 4
LABELS = 64
FULL = 32767.0
AXES = ("rows", "cols")


def halo(block, axis, dim, width):
    count = lax.axis_size(axis)
    forward = [(i, i + 1) for i in range(count - 1)]
    backward = [(target, source) for source, target in forward]
    low = lax.ppermute(
        lax.slice_in_dim(block, block.shape[dim] - width, None, axis=dim), axis, forward
    )
    high = lax.ppermute(lax.slice_in_dim(block, 0, width, axis=dim), axis, backward)
    return jnp.concatenate([low, block, high], axis=dim)


def pool_level(level_map):
    frame_count, rows_in, cols_in, channels = level_map.shape
    pooled = level_map.astype(jnp.float32).reshape(
        frame_count, rows_in // 2, 2, cols_in // 2, 2, channels
    )
    return jnp.mean(pooled, axis=(2, 4)).astype(jnp.bfloat16)


def window_strips(padded):
    frames, rows, cols, channels = padded.shape
    across = (cols - SIDE) // SIDE
    strips = [
        lax.slice_in_dim(padded, t * SIDE, t * SIDE + SPAN, axis=2) for t in range(across)
    ]
    return jnp.stack(strips).reshape(across * frames * rows, SPAN, channels)


def build_body(peers, blocks, tiles_of, per_frame, across, band_rows):
    def kernel(owner, tile, fmap, send, codes, count, sems):
        def clear(i, carry):
            count[i] = 0
            return carry

        lax.fori_loop(0, LEVELS * peers, clear, 0, unroll=8)

        def source(k):
            frame = k // per_frame
            rest = k % per_frame
            row = frame * band_rows + rest // across * SIDE
            return fmap.at[pl.ds(row, SIDE), rest % across]

        def place(k, carry):
            for level in range(LEVELS):
                own = owner[level * blocks + k]
                seen = count[level * peers + own]
                count[level * peers + own] = seen + 1
                label = k // per_frame * tiles_of[level] + lax.rem(
                    tile[level * blocks + k], tiles_of[level]
                )
                slot = (own * LEVELS + level) * SLOTS + seen
                codes[level * blocks + k] = slot * LABELS + label
                pltpu.make_async_copy(
                    source(k), send.at[slot], sems.at[level * blocks + k]
                ).start()
            return carry

        lax.fori_loop(0, blocks, place, 0)

        def finish(k, carry):
            for level in range(LEVELS):
                slot = codes[level * blocks + k] // LABELS
                pltpu.make_async_copy(
                    source(k), send.at[slot], sems.at[level * blocks + k]
                ).wait()
            return carry

        lax.fori_loop(0, blocks, finish, 0)

    return kernel


def serve_body(rows_of, across_of, tiles_of, frames):
    def kernel(labels, queries, strips0, strips1, reply, flat):
        step = pl.program_id(0)
        lane = lax.broadcasted_iota(jnp.int32, (1, LANES), 1)
        first = lane < QUERIES
        i_part = lane % QUERIES // SIDE
        j_part = lane % SIDE
        row_id = lax.broadcasted_iota(jnp.int32, (REPLY_ROWS, LANES), 0)
        flat[...] = jnp.zeros_like(flat)

        def start_of(label, level):
            label = jnp.maximum(label, 0)
            frame = label // tiles_of[level]
            tile = label % tiles_of[level]
            column = tile % across_of[level]
            return (column * frames + frame) * rows_of[level] + tile // across_of[level] * SIDE

        def table_of(peer, level, strips):
            at = ((step * PEERS_A_STEP + peer) * LEVELS + level) * SLOTS
            query = queries[peer, level * LANES : (level + 1) * LANES]
            tables = []
            for slot in range(SLOTS):
                cells = strips[pl.ds(start_of(labels[at + slot], level), SPAN)]
                tables.append(
                    lax.dot_general(
                        cells.reshape(SPAN * SPAN, -1),
                        query,
                        (((1,), (1,)), ((), ())),
                        preferred_element_type=jnp.float32,
                    )
                )
            table = jnp.where(first, tables[0], tables[1])
            table = table.reshape(SPAN, SPAN, LANES)
            for bit in (4, 2, 1):
                left = table.shape[0] - bit
                table = jnp.where(i_part & bit != 0, table[bit:], table[:left])
            table = table.reshape(WIN * SPAN, LANES)
            for bit in (4, 2, 1):
                table = jnp.where(
                    j_part & bit != 0, pltpu.roll(table, WIN * SPAN - bit, 0), table
                )
            return table

        for peer in range(PEERS_A_STEP):
            powers = []
            for level, strips in enumerate((strips0, strips1)):
                table = table_of(peer, level, strips)
                base = level * WINDOW
                for a in range(WIN):
                    flat[peer, base + a * WIN : base + (a + 1) * WIN, :] = table[
                        a * SPAN : a * SPAN + WIN
                    ]
            values = flat[peer]
            size = jnp.abs(values)
            tops = [
                jnp.max(jnp.where(row_id < WINDOW, size, 0.0), axis=0, keepdims=True),
                jnp.max(jnp.where(row_id < WINDOW, 0.0, size), axis=0, keepdims=True),
            ]
            powers = [jnp.ceil(jnp.log2(jnp.maximum(top, 1e-30))) for top in tops]
            factors = [jnp.exp2(-power) * FULL for power in powers]
            coded = jnp.round(values * jnp.where(row_id < WINDOW, factors[0], factors[1]))
            coded = jnp.clip(coded, -FULL, FULL)
            for level in range(LEVELS):
                coded = jnp.where(row_id == LEVELS * WINDOW + level, powers[level], coded)
            reply[peer] = coded.astype(jnp.int32).astype(jnp.int16)

    return kernel


def finish_body(blocks, groups, scale):
    def kernel(slots, reply, out):
        step = pl.program_id(0)
        low = lax.broadcasted_iota(jnp.int32, (1, LANES), 1) < QUERIES
        for level in range(LEVELS):
            for group in range(groups):
                k = level * blocks + (step * groups + group) * 2
                halves = []
                for side in range(2):
                    slot = slots[k + side] // LABELS
                    block = reply[slot // (LEVELS * SLOTS)].astype(jnp.int32)
                    turned = pltpu.roll(block, QUERIES, 1)
                    halves.append(jnp.where(slot % SLOTS == side, block, turned))
                both = jnp.where(low, halves[0], halves[1]).astype(jnp.float32)
                power = both[LEVELS * WINDOW + level : LEVELS * WINDOW + level + 1]
                factor = jnp.exp2(power) * (scale / FULL)
                values = both[level * WINDOW : (level + 1) * WINDOW] * factor
                out[:, level, group * LANES : (group + 1) * LANES] = values

    return kernel


def steps(fmap1, fmap2, target_owner, target_tile):
    frames, band_rows, band_cols, channels = fmap1.shape
    peers = lax.axis_size("rows") * lax.axis_size("cols")
    across = band_cols // SIDE
    per_frame = band_rows // SIDE * across
    blocks = frames * per_frame
    across_of = [(band_cols >> l) // SIDE for l in range(LEVELS)]
    tiles_of = [((band_rows >> l) // SIDE) * across_of[l] for l in range(LEVELS)]
    per_peer = LEVELS * SLOTS

    smem = pl.BlockSpec(memory_space=pltpu.SMEM)
    hbm = pl.BlockSpec(memory_space=pl.ANY)
    send, codes = pl.pallas_call(
        build_body(peers, blocks, tiles_of, per_frame, across, band_rows),
        in_specs=[smem, smem, pl.BlockSpec(memory_space=pltpu.VMEM)],
        out_specs=[hbm, smem],
        out_shape=[
            jax.ShapeDtypeStruct((peers * per_peer, SIDE, SIDE, channels), jnp.bfloat16),
            jax.ShapeDtypeStruct((LEVELS * blocks,), jnp.int32),
        ],
        scratch_shapes=[
            pltpu.SMEM((LEVELS * peers,), jnp.int32),
            pltpu.SemaphoreType.DMA((LEVELS * blocks,)),
        ],
        name="build",
    )(
        target_owner.reshape(LEVELS * blocks),
        target_tile.reshape(LEVELS * blocks),
        fmap1.reshape(frames * band_rows, across, SIDE, channels),
    )

    def exchange(value):
        return lax.all_to_all(value, AXES, split_axis=0, concat_axis=0, tiled=True)

    arrived = exchange(send.reshape(peers, LEVELS * LANES, channels))

    every = lax.all_gather(codes, AXES)
    mine = lax.axis_index(AXES) * per_peer + jnp.arange(per_peer, dtype=jnp.int32)
    found = every[:, None, :] // LABELS == mine[None, :, None]
    labels = jnp.max(jnp.where(found, every[:, None, :] % LABELS, -1), axis=2).reshape(-1)

    tall = halo(fmap2, "rows", 1, SIDE)
    wide = halo(tall, "cols", 2, SIDE)
    maps = [wide[:, RADIUS:-RADIUS, RADIUS:-RADIUS], pool_level(wide)]
    strips = [window_strips(level_map) for level_map in maps]

    served = pl.pallas_call(
        serve_body([m.shape[1] for m in maps], across_of, tiles_of, frames),
        grid_spec=pltpu.PrefetchScalarGridSpec(
            num_scalar_prefetch=1,
            grid=(peers // PEERS_A_STEP,),
            in_specs=[
                pl.BlockSpec((PEERS_A_STEP, LEVELS * LANES, channels), lambda s, _: (s, 0, 0)),
                pl.BlockSpec(strips[0].shape, lambda s, _: (0, 0, 0)),
                pl.BlockSpec(strips[1].shape, lambda s, _: (0, 0, 0)),
            ],
            out_specs=pl.BlockSpec((PEERS_A_STEP, REPLY_ROWS, LANES), lambda s, _: (s, 0, 0)),
            scratch_shapes=[pltpu.VMEM((PEERS_A_STEP, REPLY_ROWS, LANES), jnp.float32)],
        ),
        out_shape=jax.ShapeDtypeStruct((peers, REPLY_ROWS, LANES), jnp.int16),
        name="serve",
    )(labels, arrived, *strips)
    reply = exchange(served)

    groups = 4
    width = groups * LANES
    out = pl.pallas_call(
        finish_body(blocks, groups, channels ** (-0.5)),
        grid_spec=pltpu.PrefetchScalarGridSpec(
            num_scalar_prefetch=1,
            grid=(blocks * QUERIES // width,),
            in_specs=[pl.BlockSpec((peers, REPLY_ROWS, LANES), lambda s, _: (0, 0, 0))],
            out_specs=pl.BlockSpec((WINDOW, LEVELS, width), lambda s, _: (0, 0, s)),
        ),
        out_shape=jax.ShapeDtypeStruct((WINDOW, LEVELS, blocks * QUERIES), jnp.float32),
        name="finish",
    )(codes, reply)
    return out.transpose(1, 0, 2)


def solution(mesh):
    in_specs = (
        P(None, "rows", "cols", None),
        P(None, "rows", "cols", None),
        P(None, AXES, None),
        P(None, AXES),
    )
    out_specs = P(None, None, AXES)
    return jax.shard_map(steps, mesh=mesh, in_specs=in_specs, out_specs=out_specs, check_vma=False)
```

profile of v0, /device:TPU:1, one launch (start us, length us, event | category | flops | bytes accessed | tf_op | source)
XLA Modules:
  0.0 455.4 jit_solution(7889125916328968047)
XLA Ops:
  0.0 0.5 broadcast.35
  0.5 1.3 reduce.3
  1.9 0.6 reshape.55.owner
  2.4 1.3 reshape.56.tile
  3.8 6.3 %build.1 = (bf16[512,8,8,256]{3,2,1,0:T(8,128)(2,1)}, s32[128]{0:T(128)}) custom-call(s32[128]{0:T(128)} %reshape.55.owner, s32[128]{0:T(128)} %reshape.56.tile, bf16[64,8,8,256]{3,2,1,0:T(8,128)(2,1)} %bitcast.52), custom_call_target="tpu_custom_call" | custom-call | tf_op jit(solution)/shard_map/build/pallas_call | solution.py:200
  10.1 0.0 copy-start.1
  10.1 12.0 %all-to-all-start = ((bf16[128,256,256]{2,1,0:T(8,128)(2,1)}), bf16[128,256,256]{2,1,0:T(8,128)(2,1)}, u32[]{:S(2)}, u32[]{:S(2)}) async-start(bf16[128,256,256]{2,1,0:T(8,128)(2,1)} %bitcast.50), calls=%async_computation | async-start | bytes 33554432 | tf_op jit(solution)/shard_map/all_to_all | solution.py:220
  22.1 0.0 copy-done.1
  22.1 0.9 fusion.13
  23.0 4.1 collective-permute-start
  27.0 1.3 collective-permute-start.1
  28.3 213.1 %collective-permute-done = bf16[2,8,64,256]{3,2,1,0:T(8,128)(2,1)} collective-permute-done((bf16[2,8,64,256]{3,2,1,0:T(8,128)(2,1)S(1)}, bf16[2,8,64,256]{3,2,1,0:T(8,128)(2,1)}, u32[]{:S(2)}, u32[]{:S(2)}) %collective-permute-start) | collective-permute-done | bytes 524320 | tf_op jit(solution)/shard_map/ppermute | solution.py:29
  241.5 1.1 constant_dynamic-update-slice_fusion.2
  242.6 0.0 copy-start.2
  242.6 1.7 constant_dynamic-update-slice_fusion.1
  244.3 5.6 %collective-permute-done.1 = bf16[2,8,64,256]{3,2,1,0:T(8,128)(2,1)} collective-permute-done((bf16[2,8,64,256]{3,2,1,0:T(8,128)(2,1)}, bf16[2,8,64,256]{3,2,1,0:T(8,128)(2,1)}, u32[]{:S(2)}, u32[]{:S(2)}) %collective-permute-start.1) | collective-permute-done | bytes 524320 | tf_op jit(solution)/shard_map/ppermute | solution.py:32
  249.9 1.1 constant_dynamic-update-slice_fusion
  250.9 1.0 fusion.12
  251.9 10.4 %collective-permute-start.2 = (bf16[2,48,8,256]{3,2,1,0:T(8,128)(2,1)}, bf16[2,48,8,256]{3,2,1,0:T(8,128)(2,1)}, u32[]{:S(2)}, u32[]{:S(2)}) collective-permute-start(bf16[2,48,8,256]{3,2,1,0:T(8,128)(2,1)} %get-tuple-element.10), channel_id=1, source_target_pairs={{0,1},{1,2},{2,3},{3,4},{4,5},{5,6},{6,7},{8,9},{9,10},{10,11},{11... | collective-permute-start | bytes 1179656 | tf_op jit(solution)/shard_map/ppermute | solution.py:29
  262.3 1.9 collective-permute-start.3
  264.2 0.0 copy-done.2
  264.2 36.4 %all-gather.1 = s32[128,1,128]{2,1,0:T(1,128)S(1)} all-gather(s32[1,1,128]{2,1,0:T(1,128)S(1)} %bitcast.54), channel_id=2, replica_groups=mesh['rows'=16,'cols'=8] {'rows','cols'}, dimensions={0}, use_global_device_ids=true | all-gather | bytes 66048 | tf_op jit(solution)/shard_map/all_gather | solution.py:224
  300.6 0.1 add_select_fusion.1
  300.7 0.2 select_reduce_fusion
  300.9 0.7 copy.5
  301.6 1.5 reshape.58.labels
  303.1 0.0 collective-permute-done.2
  303.1 0.0 collective-permute-done.3
  303.1 4.6 %maximum_convert_fusion = f32[2,48,80,256]{3,2,1,0:T(8,128)} fusion(bf16[2,48,8,256]{3,2,1,0:T(8,128)(2,1)S(1)} %collective-permute-done.3, bf16[2,48,64,256]{3,2,1,0:T(8,128)(2,1)S(1)} %constant_dynamic-update-slice_fusion, bf16[2,48,8,256]{3,2,1,0:T(8,128)(2,1)} %collective-permute-done.2), kind=kLoop, calls=%fused_computation | loop fusion | flops 11796480 | bytes 11796480 | tf_op jit(solution)/shard_map/convert_element_type | solution.py:38
  307.7 9.9 %reshape.62 = f32[2,24,2,40,2,256]{5,4,3,2,1,0:T(2,128)} reshape(f32[2,48,80,256]{3,2,1,0:T(8,128)} %maximum_convert_fusion) | data formatting | bytes 15728640 | tf_op jit(solution)/shard_map/convert_element_type | solution.py:38
  317.7 10.6 %reduce_sum.9 = f32[2,24,40,256]{3,2,1,0:T(8,128)} reduce(f32[2,24,2,40,2,256]{5,4,3,2,1,0:T(2,128)} %reshape.62, f32[]{:T(128)} %constant.47.clone.1), dimensions={2,4}, to_apply=%region_1.2 | reduce | flops 1474560 | bytes 9830404 | tf_op jit(solution)/shard_map/reduce_sum | solution.py:41
  328.3 2.1 fusion.9
  330.4 1.2 fusion.7
  331.5 1.2 fusion.6
  332.7 1.2 fusion.5
  333.9 1.1 fusion.4
  335.0 0.0 copy-start
  335.0 1.2 fusion.3
  336.2 1.2 fusion.2
  337.3 1.3 fusion.1
  338.6 0.0 copy-done
  338.6 0.2 multiply_convert_fusion
  338.8 0.2 slice_bitcast_fusion.9
  339.0 1.3 pad_maximum_fusion
  340.3 0.0 all-to-all-done.queries
  340.3 35.4 %serve.1 = s16[128,168,128]{2,1,0:T(8,128)(2,1)} custom-call(s32[512]{0:T(512)} %reshape.58.labels, bf16[128,256,256]{2,1,0:T(8,128)(2,1)} %all-to-all-done.queries, bf16[640,16,256]{2,1,0:T(8,128)(2,1)} %bitcast.12.strips0, bf16[192,16,256]{2,1,0:T(8,128)(2,1)} %bitcast.51), custom_call_target="tpu_custom_call" | custom-call | tf_op jit(solution)/shard_map/serve/pallas_call | solution.py:234
  375.7 71.6 %all_to_all.10.reply = s16[128,168,128]{2,1,0:T(8,128)(2,1)} all-to-all(s16[128,168,128]{2,1,0:T(8,128)(2,1)} %serve.1), channel_id=1, replica_groups=mesh['rows'=16,'cols'=8] {'rows','cols'}, dimensions={0} | all-to-all | bytes 11010048 | tf_op jit(solution)/shard_map/all_to_all | solution.py:220
  447.3 8.1 %finish.1 = f32[81,2,4096]{2,1,0:T(2,128)} custom-call(s32[128]{0:T(128)} %get-tuple-element.7.slots, s16[128,168,128]{2,1,0:T(8,128)(2,1)} %all_to_all.10.reply), custom_call_target="tpu_custom_call" | custom-call | tf_op jit(solution)/shard_map/finish/pallas_call | solution.py:254
  (1 shorter events, 0.0 us)
Async XLA Ops:
  10.1 12.0 %copy-start.1 = (bf16[2,32,64,256]{3,2,1,0:T(8,128)(2,1)S(1)}, bf16[2,32,64,256]{3,2,1,0:T(8,128)(2,1)}, u32[]{:S(2)}) copy-start(bf16[2,32,64,256]{3,2,1,0:T(8,128)(2,1)} %param.5) | copy-start | bytes 6291460
  10.1 330.2 %all-to-all-start = ((bf16[128,256,256]{2,1,0:T(8,128)(2,1)}), bf16[128,256,256]{2,1,0:T(8,128)(2,1)}, u32[]{:S(2)}, u32[]{:S(2)}) async-start(bf16[128,256,256]{2,1,0:T(8,128)(2,1)} %bitcast.50), calls=%async_computation | async-start | bytes 33554432 | tf_op jit(solution)/shard_map/all_to_all | solution.py:220
  23.0 218.5 %collective-permute-start = (bf16[2,8,64,256]{3,2,1,0:T(8,128)(2,1)S(1)}, bf16[2,8,64,256]{3,2,1,0:T(8,128)(2,1)}, u32[]{:S(2)}, u32[]{:S(2)}) collective-permute-start(bf16[2,8,64,256]{3,2,1,0:T(8,128)(2,1)S(1)} %get-tuple-element.12), channel_id=1, source_target_pairs={{0,8},{8,16},{16,24},{24,32},{32,40},{40,48},{48,56},{56,64},{64,7... | collective-permute-start | bytes 1572872 | tf_op jit(solution)/shard_map/ppermute | solution.py:29
  27.0 222.8 %collective-permute-start.1 = (bf16[2,8,64,256]{3,2,1,0:T(8,128)(2,1)}, bf16[2,8,64,256]{3,2,1,0:T(8,128)(2,1)}, u32[]{:S(2)}, u32[]{:S(2)}) collective-permute-start(bf16[2,8,64,256]{3,2,1,0:T(8,128)(2,1)} %get-tuple-element.11), channel_id=1, source_target_pairs={{8,0},{16,8},{24,16},{32,24},{40,32},{48,40},{56,48},{64,56},{72,6... | collective-permute-start | bytes 1572872 | tf_op jit(solution)/shard_map/ppermute | solution.py:32
  242.6 21.7 %copy-start.2 = (s32[128]{0:T(128)S(1)}, s32[128]{0:T(128)}, u32[]{:S(2)}) copy-start(s32[128]{0:T(128)} %get-tuple-element.7.slots) | copy-start | bytes 1540
  251.9 51.2 %collective-permute-start.2 = (bf16[2,48,8,256]{3,2,1,0:T(8,128)(2,1)}, bf16[2,48,8,256]{3,2,1,0:T(8,128)(2,1)}, u32[]{:S(2)}, u32[]{:S(2)}) collective-permute-start(bf16[2,48,8,256]{3,2,1,0:T(8,128)(2,1)} %get-tuple-element.10), channel_id=1, source_target_pairs={{0,1},{1,2},{2,3},{3,4},{4,5},{5,6},{6,7},{8,9},{9,10},{10,11},{11... | collective-permute-start | bytes 1179656 | tf_op jit(solution)/shard_map/ppermute | solution.py:29
  262.3 40.9 %collective-permute-start.3 = (bf16[2,48,8,256]{3,2,1,0:T(8,128)(2,1)}, bf16[2,48,8,256]{3,2,1,0:T(8,128)(2,1)S(1)}, u32[]{:S(2)}, u32[]{:S(2)}) collective-permute-start(bf16[2,48,8,256]{3,2,1,0:T(8,128)(2,1)} %get-tuple-element.9), channel_id=1, source_target_pairs={{1,0},{2,1},{3,2},{4,3},{5,4},{6,5},{7,6},{9,8},{10,9},{11,10},{12... | collective-permute-start | bytes 1179656 | tf_op jit(solution)/shard_map/ppermute | solution.py:32
  335.0 3.6 copy-start
where the time goes:
time: 457 us; the launch traced here: 455 us
  waiting for transfers between devices  219 us (48%)
  blocking collectives  108 us (24%)
  Pallas kernels  49.8 us (11%)
  starting transfers between devices  29.6 us (6%)
  local copies, waits for them, and re-layouts  27.4 us (6%)
  other arithmetic  21.7 us (5%)
    ppermute x2, waiting for transfers between devices, halo(): lax.ppermute(lax.slice_in_dim(block, block.shape[dim] - width, None, axis...  213 us
    all_to_all x1, blocking collectives, exchange(): return lax.all_to_all(value, AXES, split_axis=0, concat_axis=0, tiled=True)  71.6 us
    all_gather x1, blocking collectives, steps(): every = lax.all_gather(codes, AXES)  36.4 us
    pallas_call x1, Pallas kernels, steps(): pl.pallas_call(serve_body([m.shape[1] for m in maps], across_of, tiles_of...  35.4 us
    ppermute x2, starting transfers between devices, halo(): lax.ppermute(lax.slice_in_dim(block, block.shape[dim] - width, None, axis...  14.4 us
    all_to_all x1, starting transfers between devices, exchange(): return lax.all_to_all(value, AXES, split_axis=0, concat_axis=0, tiled=True)  12 us
    reduce_sum x1, other arithmetic, pool_level(): return jnp.mean(pooled, axis=(2, 4)).astype(jnp.bfloat16)  10.6 us
    unnamed x15, local copies, waits for them, and re-layouts  10.3 us
  transfers between devices with their start and end apart: 5, of which 2 were waited for; matrix products, arithmetic and copies ran while one was open for 10% of the time, Pallas kernels for 0%

commit v1 on v0

--- a/solution.py
+++ b/solution.py
@@ -16,21 +16,22 @@
 SLOTS = 2
 LANES = SLOTS * QUERIES
 REPLY_ROWS = -(-LEVELS * (WINDOW + 1) // 8) * 8
-PEERS_A_STEP = 4
-LABELS = 64
+PEERS_A_STEP = 16
+BENCHES = 4
 FULL = 32767.0
 AXES = ("rows", "cols")
 
 
-def halo(block, axis, dim, width):
+def swapped(upward, downward, axis):
     count = lax.axis_size(axis)
     forward = [(i, i + 1) for i in range(count - 1)]
     backward = [(target, source) for source, target in forward]
-    low = lax.ppermute(
-        lax.slice_in_dim(block, block.shape[dim] - width, None, axis=dim), axis, forward
-    )
-    high = lax.ppermute(lax.slice_in_dim(block, 0, width, axis=dim), axis, backward)
-    return jnp.concatenate([low, block, high], axis=dim)
+    return lax.ppermute(upward, axis, forward), lax.ppermute(downward, axis, backward)
+
+
+def neighbours(block, axis, dim, width):
+    tail = lax.slice_in_dim(block, block.shape[dim] - width, None, axis=dim)
+    return swapped(tail, lax.slice_in_dim(block, 0, width, axis=dim), axis)
 
 
 def pool_level(level_map):
@@ -51,12 +52,18 @@
 
 
 def build_body(peers, blocks, tiles_of, per_frame, across, band_rows):
-    def kernel(owner, tile, fmap, send, codes, count, sems):
+    def kernel(owner, tile, fmap, send, codes, count, labels, notes, sems, note_sem):
         def clear(i, carry):
             count[i] = 0
             return carry
 
         lax.fori_loop(0, LEVELS * peers, clear, 0, unroll=8)
+
+        def blank(i, carry):
+            labels[i] = 0
+            return carry
+
+        lax.fori_loop(0, LEVELS * SLOTS * peers, blank, 0, unroll=8)
 
         def source(k):
             frame = k // per_frame
@@ -64,59 +71,87 @@
             row = frame * band_rows + rest // across * SIDE
             return fmap.at[pl.ds(row, SIDE), rest % across]
 
+        def copy(k, level, slot):
+            own = slot // (LEVELS * SLOTS)
+            place = slot % (LEVELS * SLOTS)
+            return pltpu.make_async_copy(
+                source(k), send.at[own, pl.ds(place * SIDE, SIDE)], sems.at[level * blocks + k]
+            )
+
         def place(k, carry):
             for level in range(LEVELS):
-                own = owner[level * blocks + k]
+                own = owner[level, 0, k]
                 seen = count[level * peers + own]
                 count[level * peers + own] = seen + 1
-                label = k // per_frame * tiles_of[level] + lax.rem(
-                    tile[level * blocks + k], tiles_of[level]
+                slot = (own * LEVELS + level) * SLOTS + seen
+                codes[level * blocks + k] = slot
+                labels[slot] = k // per_frame * tiles_of[level] + lax.rem(
+                    tile[level, k], tiles_of[level]
                 )
-                slot = (own * LEVELS + level) * SLOTS + seen
-                codes[level * blocks + k] = slot * LABELS + label
-                pltpu.make_async_copy(
-                    source(k), send.at[slot], sems.at[level * blocks + k]
-                ).start()
+                copy(k, level, slot).start()
             return carry
 
         lax.fori_loop(0, blocks, place, 0)
+
+        lane = lax.broadcasted_iota(jnp.int32, notes.shape[1:], 1)
+
+        def note(peer, carry):
+            values = jnp.zeros(notes.shape[1:], jnp.int32)
+            for slot in range(LEVELS * SLOTS):
+                values = jnp.where(lane == slot, labels[peer * LEVELS * SLOTS + slot], values)
+            notes[peer] = values.astype(jnp.float32).astype(jnp.bfloat16)
+            return carry
+
+        lax.fori_loop(0, peers, note, 0, unroll=4)
+        noted = pltpu.make_async_copy(notes, send.at[:, LEVELS * SLOTS * SIDE], note_sem)
+        noted.start()
 
         def finish(k, carry):
             for level in range(LEVELS):
-                slot = codes[level * blocks + k] // LABELS
-                pltpu.make_async_copy(
-                    source(k), send.at[slot], sems.at[level * blocks + k]
-                ).wait()
+                copy(k, level, codes[level * blocks + k]).wait()
             return carry
 
         lax.fori_loop(0, blocks, finish, 0)
+        noted.wait()
 
     return kernel
 
 
-def serve_body(rows_of, across_of, tiles_of, frames):
-    def kernel(labels, queries, strips0, strips1, reply, flat):
+def serve_body(rows_of, across_of, tiles_of, frames, peers):
+    def kernel(notes, queries, strips0, strips1, reply, flat, lines, labels, sem):
         step = pl.program_id(0)
         lane = lax.broadcasted_iota(jnp.int32, (1, LANES), 1)
         first = lane < QUERIES
         i_part = lane % QUERIES // SIDE
         j_part = lane % SIDE
         row_id = lax.broadcasted_iota(jnp.int32, (REPLY_ROWS, LANES), 0)
-        flat[...] = jnp.zeros_like(flat)
+
+        @pl.when(step == 0)
+        def _():
+            flat[...] = jnp.zeros_like(flat)
+
+            def line(peer, carry):
+                values = notes[peer].astype(jnp.float32).astype(jnp.int32)
+                lines[pl.ds(peer, 1), :] = values[:1, : lines.shape[1]]
+                return carry
+
+            lax.fori_loop(0, peers, line, 0, unroll=8)
+            taken = pltpu.make_async_copy(lines, labels, sem)
+            taken.start()
+            taken.wait()
 
         def start_of(label, level):
-            label = jnp.maximum(label, 0)
             frame = label // tiles_of[level]
             tile = label % tiles_of[level]
             column = tile % across_of[level]
             return (column * frames + frame) * rows_of[level] + tile // across_of[level] * SIDE
 
         def table_of(peer, level, strips):
-            at = ((step * PEERS_A_STEP + peer) * LEVELS + level) * SLOTS
             query = queries[peer, level * LANES : (level + 1) * LANES]
             tables = []
             for slot in range(SLOTS):
-                cells = strips[pl.ds(start_of(labels[at + slot], level), SPAN)]
+                label = labels[step * PEERS_A_STEP + peer, level * SLOTS + slot]
+                cells = strips[pl.ds(start_of(label, level), SPAN)]
                 tables.append(
                     lax.dot_general(
                         cells.reshape(SPAN * SPAN, -1),
@@ -137,16 +172,15 @@
                 )
             return table
 
-        for peer in range(PEERS_A_STEP):
-            powers = []
+        def one(peer, bench):
             for level, strips in enumerate((strips0, strips1)):
                 table = table_of(peer, level, strips)
                 base = level * WINDOW
                 for a in range(WIN):
-                    flat[peer, base + a * WIN : base + (a + 1) * WIN, :] = table[
+                    flat[bench, base + a * WIN : base + (a + 1) * WIN, :] = table[
                         a * SPAN : a * SPAN + WIN
                     ]
-            values = flat[peer]
+            values = flat[bench]
             size = jnp.abs(values)
             tops = [
                 jnp.max(jnp.where(row_id < WINDOW, size, 0.0), axis=0, keepdims=True),
@@ -160,6 +194,13 @@
                 coded = jnp.where(row_id == LEVELS * WINDOW + level, powers[level], coded)
             reply[peer] = coded.astype(jnp.int32).astype(jnp.int16)
 
+        def turn(i, carry):
+            for bench in range(BENCHES):
+                one(i * BENCHES + bench, bench)
+            return carry
+
+        lax.fori_loop(0, PEERS_A_STEP // BENCHES, turn, 0)
+
     return kernel
 
 
@@ -172,7 +213,7 @@
                 k = level * blocks + (step * groups + group) * 2
                 halves = []
                 for side in range(2):
-                    slot = slots[k + side] // LABELS
+                    slot = slots[k + side]
                     block = reply[slot // (LEVELS * SLOTS)].astype(jnp.int32)
                     turned = pltpu.roll(block, QUERIES, 1)
                     halves.append(jnp.where(slot % SLOTS == side, block, turned))
@@ -193,8 +234,8 @@
     blocks = frames * per_frame
     across_of = [(band_cols >> l) // SIDE for l in range(LEVELS)]
     tiles_of = [((band_rows >> l) // SIDE) * across_of[l] for l in range(LEVELS)]
-    per_peer = LEVELS * SLOTS
-
+
+    parts = LEVELS * SLOTS * SIDE + 1
     smem = pl.BlockSpec(memory_space=pltpu.SMEM)
     hbm = pl.BlockSpec(memory_space=pl.ANY)
     send, codes = pl.pallas_call(
@@ -202,51 +243,59 @@
         in_specs=[smem, smem, pl.BlockSpec(memory_space=pltpu.VMEM)],
         out_specs=[hbm, smem],
         out_shape=[
-            jax.ShapeDtypeStruct((peers * per_peer, SIDE, SIDE, channels), jnp.bfloat16),
+            jax.ShapeDtypeStruct((peers, parts, SIDE, channels), jnp.bfloat16),
             jax.ShapeDtypeStruct((LEVELS * blocks,), jnp.int32),
         ],
         scratch_shapes=[
             pltpu.SMEM((LEVELS * peers,), jnp.int32),
+            pltpu.SMEM((LEVELS * SLOTS * peers,), jnp.int32),
+            pltpu.VMEM((peers, SIDE, channels), jnp.bfloat16),
             pltpu.SemaphoreType.DMA((LEVELS * blocks,)),
+            pltpu.SemaphoreType.DMA,
         ],
         name="build",
     )(
-        target_owner.reshape(LEVELS * blocks),
-        target_tile.reshape(LEVELS * blocks),
+        target_owner.transpose(0, 2, 1),
+        target_tile,
         fmap1.reshape(frames * band_rows, across, SIDE, channels),
     )
 
     def exchange(value):
         return lax.all_to_all(value, AXES, split_axis=0, concat_axis=0, tiled=True)
 
-    arrived = exchange(send.reshape(peers, LEVELS * LANES, channels))
-
-    every = lax.all_gather(codes, AXES)
-    mine = lax.axis_index(AXES) * per_peer + jnp.arange(per_peer, dtype=jnp.int32)
-    found = every[:, None, :] // LABELS == mine[None, :, None]
-    labels = jnp.max(jnp.where(found, every[:, None, :] % LABELS, -1), axis=2).reshape(-1)
-
-    tall = halo(fmap2, "rows", 1, SIDE)
-    wide = halo(tall, "cols", 2, SIDE)
+    arrived = exchange(send.reshape(peers, parts * SIDE, channels))
+
+    low, high = neighbours(fmap2, "rows", 1, SIDE)
+    edges = [
+        jnp.concatenate([lax.slice_in_dim(part, *span, axis=2) for part in (low, fmap2, high)], axis=1)
+        for span in ((0, SIDE), (band_cols - SIDE, band_cols))
+    ]
+    west, east = swapped(edges[1], edges[0], "cols")
+    tall = jnp.concatenate([low, fmap2, high], axis=1)
+    wide = jnp.concatenate([west, tall, east], axis=2)
     maps = [wide[:, RADIUS:-RADIUS, RADIUS:-RADIUS], pool_level(wide)]
     strips = [window_strips(level_map) for level_map in maps]
 
+    rows_sent = LEVELS * LANES
     served = pl.pallas_call(
-        serve_body([m.shape[1] for m in maps], across_of, tiles_of, frames),
-        grid_spec=pltpu.PrefetchScalarGridSpec(
-            num_scalar_prefetch=1,
-            grid=(peers // PEERS_A_STEP,),
-            in_specs=[
-                pl.BlockSpec((PEERS_A_STEP, LEVELS * LANES, channels), lambda s, _: (s, 0, 0)),
-                pl.BlockSpec(strips[0].shape, lambda s, _: (0, 0, 0)),
-                pl.BlockSpec(strips[1].shape, lambda s, _: (0, 0, 0)),
-            ],
-            out_specs=pl.BlockSpec((PEERS_A_STEP, REPLY_ROWS, LANES), lambda s, _: (s, 0, 0)),
-            scratch_shapes=[pltpu.VMEM((PEERS_A_STEP, REPLY_ROWS, LANES), jnp.float32)],
-        ),
+        serve_body([m.shape[1] for m in maps], across_of, tiles_of, frames, peers),
+        grid=(peers // PEERS_A_STEP,),
+        in_specs=[
+            pl.BlockSpec((peers, SIDE, channels), lambda s: (0, rows_sent // SIDE, 0)),
+            pl.BlockSpec((PEERS_A_STEP, rows_sent, channels), lambda s: (s, 0, 0)),
+            pl.BlockSpec(strips[0].shape, lambda s: (0, 0, 0)),
+            pl.BlockSpec(strips[1].shape, lambda s: (0, 0, 0)),
+        ],
+        out_specs=pl.BlockSpec((PEERS_A_STEP, REPLY_ROWS, LANES), lambda s: (s, 0, 0)),
+        scratch_shapes=[
+            pltpu.VMEM((BENCHES, REPLY_ROWS, LANES), jnp.float32),
+            pltpu.VMEM((peers, 128), jnp.int32),
+            pltpu.SMEM((peers, 128), jnp.int32),
+            pltpu.SemaphoreType.DMA,
+        ],
         out_shape=jax.ShapeDtypeStruct((peers, REPLY_ROWS, LANES), jnp.int16),
         name="serve",
-    )(labels, arrived, *strips)
+    )(arrived, arrived, *strips)
     reply = exchange(served)
 
     groups = 4

time: 457 us -> 436 us (0.954)
  blocking collectives: 108 us -> 83.5 us
  waiting for transfers between devices: 219 us -> 237 us
  local copies, waits for them, and re-layouts: 27.4 us -> 17.4 us
    all_gather x1 -> x0, blocking collectives: 36.4 us -> none  [steps(): every = lax.all_gather(codes, AXES)]
    ppermute x4, waiting for transfers between devices: 219 us -> 237 us  [the longest x2 234 us: swapped(): lax.ppermute(downward, axis, backward)]
    all_to_all x1, blocking collectives: 71.6 us -> 83.5 us  [exchange(): return lax.all_to_all(value, AXES, split_axis=0, concat_axis=0, tiled=True)]
    unnamed x15 -> x16, local copies, waits for them, and re-layouts: 10.3 us -> 7.14 us
  transfers between devices with their start and end apart: 5 -> 5, of which waited for: 2 -> 3; matrix products, arithmetic and copies ran while one was open for 10% -> 8% of each run, Pallas kernels for 0% -> 0%
where the time goes in v1:
time: 436 us; the launch traced here: 435 us
  waiting for transfers between devices  237 us (54%)
  blocking collectives  83.5 us (19%)
  Pallas kernels  48.6 us (11%)
  starting transfers between devices  29.3 us (7%)
  other arithmetic  19.1 us (4%)
  local copies, waits for them, and re-layouts  17.4 us (4%)
    ppermute x2, waiting for transfers between devices, swapped(): lax.ppermute(downward, axis, backward)  234 us
    all_to_all x1, blocking collectives, exchange(): return lax.all_to_all(value, AXES, split_axis=0, concat_axis=0, tiled=True)  83.5 us
    pallas_call x1, Pallas kernels, steps(): pl.pallas_call(serve_body([m.shape[1] for m in maps], across_of, tiles_of...  32.2 us
    ppermute x2, starting transfers between devices, swapped(): lax.ppermute(upward, axis, forward)  14.1 us
    all_to_all x1, starting transfers between devices, exchange(): return lax.all_to_all(value, AXES, split_axis=0, concat_axis=0, tiled=True)  11.9 us
    reduce_sum x1, other arithmetic, pool_level(): return jnp.mean(pooled, axis=(2, 4)).astype(jnp.bfloat16)  10.6 us
    convert_element_type x1, local copies, waits for them, and re-layouts, pool_level(): level_map.astype(jnp.float32)  9.89 us
  transfers between devices with their start and end apart: 5, of which 3 were waited for; matrix products, arithmetic and copies ran while one was open for 8% of the time, Pallas kernels for 0%

profile of v1, /device:TPU:1, one launch (start us, length us, event | category | flops | bytes accessed | tf_op | source)
XLA Modules:
  0.0 434.9 jit_solution(11429331270859740878)
XLA Ops:
  0.0 8.4 %build.1 = (bf16[128,33,8,256]{3,2,1,0:T(8,128)(2,1)}, s32[128]{0:T(128)}) custom-call(s32[2,1,64]{2,1,0:T(1,128)} %bitcast.53, s32[2,64]{1,0:T(2,128)} %tile.1, bf16[64,8,8,256]{3,2,1,0:T(8,128)(2,1)} %bitcast.52), custom_call_target="tpu_custom_call" | custom-call | tf_op jit(solution)/shard_map/build/pallas_call | solution.py:241
  8.4 0.0 copy-start.1
  8.4 11.9 %all-to-all-start = ((bf16[128,264,256]{2,1,0:T(8,128)(2,1)}), bf16[128,264,256]{2,1,0:T(8,128)(2,1)}, u32[]{:S(2)}, u32[]{:S(2)}) async-start(bf16[128,264,256]{2,1,0:T(8,128)(2,1)} %bitcast.50), calls=%async_computation | async-start | bytes 34603008 | tf_op jit(solution)/shard_map/all_to_all | solution.py:264
  20.3 0.0 copy-done.1
  20.3 0.0 copy-start.2
  20.3 0.1 fusion.11
  20.4 1.4 collective-permute-start.1
  21.9 4.0 collective-permute-start
  25.9 229.9 %collective-permute-done.1 = bf16[2,8,64,256]{3,2,1,0:T(8,128)(2,1)S(1)} collective-permute-done((bf16[2,8,64,256]{3,2,1,0:T(8,128)(2,1)S(1)}, bf16[2,8,64,256]{3,2,1,0:T(8,128)(2,1)S(1)}, u32[]{:S(2)}, u32[]{:S(2)}) %collective-permute-start.1) | collective-permute-done | bytes 524320 | tf_op jit(solution)/shard_map/ppermute | solution.py:29
  255.8 0.0 collective-permute-done
  255.9 0.1 pad_maximum_fusion.3
  255.9 10.0 %collective-permute-start.2 = (bf16[2,48,8,256]{3,2,1,0:T(8,128)(2,1)S(1)}, bf16[2,48,8,256]{3,2,1,0:T(8,128)(2,1)S(1)}, u32[]{:S(2)}, u32[]{:S(2)}) collective-permute-start(bf16[2,48,8,256]{3,2,1,0:T(8,128)(2,1)S(1)} %pad_maximum_fusion.3), channel_id=1, source_target_pairs={{0,1},{1,2},{2,3},{3,4},{4,5},{5,6},{6,7},{8,9},{9,10},{10,11},{11... | collective-permute-start | bytes 1179656 | tf_op jit(solution)/shard_map/ppermute | solution.py:29
  266.0 0.1 pad_maximum_fusion.4
  266.0 1.9 collective-permute-start.3
  268.0 0.0 copy-done.2
  268.0 0.1 constant_dynamic-update-slice_fusion.1
  268.2 2.5 collective-permute-done.2
  270.7 0.0 copy-start.3
  270.7 4.5 %collective-permute-done.3 = bf16[2,48,8,256]{3,2,1,0:T(8,128)(2,1)S(1)} collective-permute-done((bf16[2,48,8,256]{3,2,1,0:T(8,128)(2,1)S(1)}, bf16[2,48,8,256]{3,2,1,0:T(8,128)(2,1)S(1)}, u32[]{:S(2)}, u32[]{:S(2)}) %collective-permute-start.3) | collective-permute-done | bytes 393248 | tf_op jit(solution)/shard_map/ppermute | solution.py:29
  275.1 0.0 copy-done.3
  275.1 3.5 maximum_convert_fusion
  278.7 9.9 %reshape.20 = f32[2,24,2,40,2,256]{5,4,3,2,1,0:T(2,128)} reshape(f32[2,48,80,256]{3,2,1,0:T(8,128)} %maximum_convert_fusion) | data formatting | bytes 15728640 | tf_op jit(solution)/shard_map/convert_element_type | solution.py:39
  288.6 10.6 %reduce_sum.9 = f32[2,24,40,256]{3,2,1,0:T(8,128)} reduce(f32[2,24,2,40,2,256]{5,4,3,2,1,0:T(2,128)} %reshape.20, f32[]{:T(128)} %constant.1.clone.1), dimensions={2,4}, to_apply=%region_0.0 | reduce | flops 1474560 | bytes 9830404 | tf_op jit(solution)/shard_map/reduce_sum | solution.py:42
  299.2 2.1 fusion.9
  301.3 1.2 fusion.7
  302.4 1.2 fusion.6
  303.6 1.2 fusion.5
  304.8 1.2 fusion.4
  305.9 0.0 copy-start
  305.9 1.1 fusion.3
  307.1 1.1 fusion.2
  308.2 1.2 fusion.1
  309.5 0.0 copy-done
  309.5 0.2 multiply_convert_fusion
  309.6 0.2 slice_bitcast_fusion.9
  309.8 1.3 pad_maximum_fusion
  311.2 0.0 all-to-all-done.notes.queries
  311.2 32.2 %serve.1 = s16[128,168,128]{2,1,0:T(8,128)(2,1)} custom-call(bf16[128,264,256]{2,1,0:T(8,128)(2,1)} %all-to-all-done.notes.queries, bf16[128,264,256]{2,1,0:T(8,128)(2,1)} %all-to-all-done.notes.queries, bf16[640,16,256]{2,1,0:T(8,128)(2,1)} %bitcast.12.strips0, bf16[192,16,256]{2,1,0:T(8,128)(2,1)} %bitcast.51), custom_call_target="tpu_custom_call" | custom-call | tf_op jit(solution)/shard_map/serve/pallas_call | solution.py:280
  343.4 83.5 %all_to_all.10.reply = s16[128,168,128]{2,1,0:T(8,128)(2,1)} all-to-all(s16[128,168,128]{2,1,0:T(8,128)(2,1)} %serve.1), channel_id=1, replica_groups=mesh['rows'=16,'cols'=8] {'rows','cols'}, dimensions={0} | all-to-all | bytes 11010048 | tf_op jit(solution)/shard_map/all_to_all | solution.py:264
  426.8 8.1 %finish.1 = f32[81,2,4096]{2,1,0:T(2,128)} custom-call(s32[128]{0:T(128)} %get-tuple-element.7.slots, s16[128,168,128]{2,1,0:T(8,128)(2,1)} %all_to_all.10.reply), custom_call_target="tpu_custom_call" | custom-call | tf_op jit(solution)/shard_map/finish/pallas_call | solution.py:303
  (5 shorter events, 0.1 us)
Async XLA Ops:
  8.4 11.9 %copy-start.1 = (bf16[2,32,64,256]{3,2,1,0:T(8,128)(2,1)S(1)}, bf16[2,32,64,256]{3,2,1,0:T(8,128)(2,1)}, u32[]{:S(2)}) copy-start(bf16[2,32,64,256]{3,2,1,0:T(8,128)(2,1)} %param.5) | copy-start | bytes 6291460
  8.4 302.8 %all-to-all-start = ((bf16[128,264,256]{2,1,0:T(8,128)(2,1)}), bf16[128,264,256]{2,1,0:T(8,128)(2,1)}, u32[]{:S(2)}, u32[]{:S(2)}) async-start(bf16[128,264,256]{2,1,0:T(8,128)(2,1)} %bitcast.50), calls=%async_computation | async-start | bytes 34603008 | tf_op jit(solution)/shard_map/all_to_all | solution.py:264
  20.3 247.7 %copy-start.2 = (bf16[2,32,64,256]{3,2,1,0:T(8,128)(2,1)S(1)}, bf16[2,32,64,256]{3,2,1,0:T(8,128)(2,1)}, u32[]{:S(2)}) copy-start(bf16[2,32,64,256]{3,2,1,0:T(8,128)(2,1)} %param.5) | copy-start | bytes 6291460
  20.4 235.4 %collective-permute-start.1 = (bf16[2,8,64,256]{3,2,1,0:T(8,128)(2,1)S(1)}, bf16[2,8,64,256]{3,2,1,0:T(8,128)(2,1)S(1)}, u32[]{:S(2)}, u32[]{:S(2)}) collective-permute-start(bf16[2,8,64,256]{3,2,1,0:T(8,128)(2,1)S(1)} %get-tuple-element.11), channel_id=1, source_target_pairs={{8,0},{16,8},{24,16},{32,24},{40,32},{48,40},{56,48},{64,56},{72,6... | collective-permute-start | bytes 1572872 | tf_op jit(solution)/shard_map/ppermute | solution.py:29
  21.9 234.0 %collective-permute-start = (bf16[2,8,64,256]{3,2,1,0:T(8,128)(2,1)S(1)}, bf16[2,8,64,256]{3,2,1,0:T(8,128)(2,1)S(1)}, u32[]{:S(2)}, u32[]{:S(2)}) collective-permute-start(bf16[2,8,64,256]{3,2,1,0:T(8,128)(2,1)S(1)} %get-tuple-element.12), channel_id=1, source_target_pairs={{0,8},{8,16},{16,24},{24,32},{32,40},{40,48},{48,56},{56,64},{64,7... | collective-permute-start | bytes 1572872 | tf_op jit(solution)/shard_map/ppermute | solution.py:29
  255.9 14.7 %collective-permute-start.2 = (bf16[2,48,8,256]{3,2,1,0:T(8,128)(2,1)S(1)}, bf16[2,48,8,256]{3,2,1,0:T(8,128)(2,1)S(1)}, u32[]{:S(2)}, u32[]{:S(2)}) collective-permute-start(bf16[2,48,8,256]{3,2,1,0:T(8,128)(2,1)S(1)} %pad_maximum_fusion.3), channel_id=1, source_target_pairs={{0,1},{1,2},{2,3},{3,4},{4,5},{5,6},{6,7},{8,9},{9,10},{10,11},{11... | collective-permute-start | bytes 1179656 | tf_op jit(solution)/shard_map/ppermute | solution.py:29
  266.0 9.1 %collective-permute-start.3 = (bf16[2,48,8,256]{3,2,1,0:T(8,128)(2,1)S(1)}, bf16[2,48,8,256]{3,2,1,0:T(8,128)(2,1)S(1)}, u32[]{:S(2)}, u32[]{:S(2)}) collective-permute-start(bf16[2,48,8,256]{3,2,1,0:T(8,128)(2,1)S(1)} %pad_maximum_fusion.4), channel_id=1, source_target_pairs={{1,0},{2,1},{3,2},{4,3},{5,4},{6,5},{7,6},{9,8},{10,9},{11,10},{12... | collective-permute-start | bytes 1179656 | tf_op jit(solution)/shard_map/ppermute | solution.py:29
  270.7 4.5 %copy-start.3 = (bf16[2,48,8,256]{3,2,1,0:T(8,128)(2,1)}, bf16[2,48,8,256]{3,2,1,0:T(8,128)(2,1)S(1)}, u32[]{:S(2)}) copy-start(bf16[2,48,8,256]{3,2,1,0:T(8,128)(2,1)S(1)} %collective-permute-done.2) | copy-start | bytes 1179652
  305.9 3.5 copy-start

commit v2 on v1

v2 whole, which is shorter than its diff:
```python
import jax
import jax.numpy as jnp
from jax import lax
from jax.experimental import pallas as pl
from jax.experimental.pallas import tpu as pltpu
from jax.sharding import PartitionSpec as P


RADIUS = 4
LEVELS = 2
SIDE = 2 * RADIUS
SPAN = 4 * RADIUS
WIN = 2 * RADIUS + 1
WINDOW = WIN * WIN
QUERIES = SIDE * SIDE
SLOTS = 2
LANES = SLOTS * QUERIES
REPLY_ROWS = -(-(WINDOW + 1) // 8) * 8
PEERS_A_STEP = 16
BENCHES = 4
FULL = 32767.0
AXES = ("rows", "cols")


def swapped(upward, downward, axis):
    count = lax.axis_size(axis)
    forward = [(i, i + 1) for i in range(count - 1)]
    backward = [(target, source) for source, target in forward]
    return lax.ppermute(upward, axis, forward), lax.ppermute(downward, axis, backward)


def neighbours(block, axis, dim, width):
    tail = lax.slice_in_dim(block, block.shape[dim] - width, None, axis=dim)
    return swapped(tail, lax.slice_in_dim(block, 0, width, axis=dim), axis)


def pool_level(level_map):
    frame_count, rows_in, cols_in, channels = level_map.shape
    pooled = level_map.astype(jnp.float32).reshape(
        frame_count, rows_in // 2, 2, cols_in // 2, 2, channels
    )
    return jnp.mean(pooled, axis=(2, 4)).astype(jnp.bfloat16)


def window_strips(padded):
    frames, rows, cols, channels = padded.shape
    across = (cols - SIDE) // SIDE
    strips = [
        lax.slice_in_dim(padded, t * SIDE, t * SIDE + SPAN, axis=2) for t in range(across)
    ]
    return jnp.stack(strips).reshape(across * frames * rows, SPAN, channels)


def tile_copy(fmap, send, sems, per_frame, across, band_rows):
    def copy(k, slot):
        frame = k // per_frame
        rest = k % per_frame
        row = frame * band_rows + rest // across * SIDE
        return pltpu.make_async_copy(
            fmap.at[pl.ds(row, SIDE), rest % across],
            send.at[slot // SLOTS, pl.ds(slot % SLOTS * SIDE, SIDE)],
            sems.at[k],
        )

    return copy


def first_body(peers, blocks, tiles_of, per_frame, across, band_rows):
    last = LEVELS - 1

    def kernel(owner, tile, fmap, send, slots, count, labels, notes, sems, note_sem):
        copy = tile_copy(fmap, send, sems, per_frame, across, band_rows)

        def clear(i, carry):
            count[i] = 0
            return carry

        lax.fori_loop(0, LEVELS * peers, clear, 0, unroll=8)

        def blank(i, carry):
            labels[i] = 0
            return carry

        lax.fori_loop(0, LEVELS * SLOTS * peers, blank, 0, unroll=8)

        def place(k, carry):
            for level in reversed(range(LEVELS)):
                own = owner[level, 0, k]
                seen = count[level * peers + own]
                count[level * peers + own] = seen + 1
                slot = own * SLOTS + seen
                slots[level * blocks + k] = slot
                labels[level * SLOTS * peers + slot] = k // per_frame * tiles_of[level] + lax.rem(
                    tile[level, k], tiles_of[level]
                )
                if level == last:
                    copy(k, slot).start()
            return carry

        lax.fori_loop(0, blocks, place, 0)

        lane = lax.broadcasted_iota(jnp.int32, notes.shape[1:], 1)

        def note(peer, carry):
            values = jnp.zeros(notes.shape[1:], jnp.int32)
            for level in range(LEVELS):
                for seen in range(SLOTS):
                    label = labels[(level * peers + peer) * SLOTS + seen]
                    values = jnp.where(lane == level * SLOTS + seen, label, values)
            notes[peer] = values.astype(jnp.float32).astype(jnp.bfloat16)
            return carry

        lax.fori_loop(0, peers, note, 0, unroll=4)
        noted = pltpu.make_async_copy(notes, send.at[:, SLOTS * SIDE], note_sem)
        noted.start()

        def finish(k, carry):
            copy(k, slots[last * blocks + k]).wait()
            return carry

        lax.fori_loop(0, blocks, finish, 0)
        noted.wait()

    return kernel


def second_body(blocks, per_frame, across, band_rows):
    def kernel(slots, fmap, send, sems):
        copy = tile_copy(fmap, send, sems, per_frame, across, band_rows)

        def place(k, carry):
            copy(k, slots[k]).start()
            return carry

        def finish(k, carry):
            copy(k, slots[k]).wait()
            return carry

        lax.fori_loop(0, blocks, place, 0)
        lax.fori_loop(0, blocks, finish, 0)

    return kernel


def serve_body(level, rows, across, tiles, frames, peers):
    def kernel(notes, queries, strips, reply, flat, lines, labels, sem):
        step = pl.program_id(0)
        lane = lax.broadcasted_iota(jnp.int32, (1, LANES), 1)
        first = lane < QUERIES
        i_part = lane % QUERIES // SIDE
        j_part = lane % SIDE
        row_id = lax.broadcasted_iota(jnp.int32, (REPLY_ROWS, LANES), 0)

        @pl.when(step == 0)
        def _():
            flat[...] = jnp.zeros_like(flat)

            def line(peer, carry):
                values = notes[peer].astype(jnp.float32).astype(jnp.int32)
                lines[pl.ds(peer, 1), :] = values[:1, : lines.shape[1]]
                return carry

            lax.fori_loop(0, peers, line, 0, unroll=8)
            taken = pltpu.make_async_copy(lines, labels, sem)
            taken.start()
            taken.wait()

        def start_of(label):
            tile = label % tiles
            column = tile % across
            return (column * frames + label // tiles) * rows + tile // across * SIDE

        def one(peer, bench):
            query = queries[peer]
            tables = []
            for slot in range(SLOTS):
                label = labels[step * PEERS_A_STEP + peer, level * SLOTS + slot]
                cells = strips[pl.ds(start_of(label), SPAN)]
                tables.append(
                    lax.dot_general(
                        cells.reshape(SPAN * SPAN, -1),
                        query,
                        (((1,), (1,)), ((), ())),
                        preferred_element_type=jnp.float32,
                    )
                )
            table = jnp.where(first, tables[0], tables[1])
            table = table.reshape(SPAN, SPAN, LANES)
            for bit in (4, 2, 1):
                left = table.shape[0] - bit
                table = jnp.where(i_part & bit != 0, table[bit:], table[:left])
            table = table.reshape(WIN * SPAN, LANES)
            for bit in (4, 2, 1):
                table = jnp.where(
                    j_part & bit != 0, pltpu.roll(table, WIN * SPAN - bit, 0), table
                )
            for a in range(WIN):
                flat[bench, a * WIN : (a + 1) * WIN, :] = table[a * SPAN : a * SPAN + WIN]
            values = flat[bench]
            top = jnp.max(jnp.abs(values), axis=0, keepdims=True)
            power = jnp.ceil(jnp.log2(jnp.maximum(top, 1e-30)))
            coded = jnp.round(values * (jnp.exp2(-power) * FULL))
            coded = jnp.clip(coded, -FULL, FULL)
            coded = jnp.where(row_id == WINDOW, power, coded)
            reply[peer] = coded.astype(jnp.int32).astype(jnp.int16)

        def turn(i, carry):
            for bench in range(BENCHES):
                one(i * BENCHES + bench, bench)
            return carry

        lax.fori_loop(0, PEERS_A_STEP // BENCHES, turn, 0)

    return kernel


def finish_body(blocks, groups, scale):
    def kernel(slots, reply0, reply1, out):
        step = pl.program_id(0)
        low = lax.broadcasted_iota(jnp.int32, (1, LANES), 1) < QUERIES
        for level, reply in enumerate((reply0, reply1)):
            for group in range(groups):
                k = level * blocks + (step * groups + group) * 2
                halves = []
                for side in range(2):
                    slot = slots[k + side]
                    block = reply[slot // SLOTS].astype(jnp.int32)
                    turned = pltpu.roll(block, QUERIES, 1)
                    halves.append(jnp.where(slot % SLOTS == side, block, turned))
                both = jnp.where(low, halves[0], halves[1]).astype(jnp.float32)
                factor = jnp.exp2(both[WINDOW : WINDOW + 1]) * (scale / FULL)
                out[:, level, group * LANES : (group + 1) * LANES] = both[:WINDOW] * factor

    return kernel


def steps(fmap1, fmap2, target_owner, target_tile):
    frames, band_rows, band_cols, channels = fmap1.shape
    peers = lax.axis_size("rows") * lax.axis_size("cols")
    across = band_cols // SIDE
    per_frame = band_rows // SIDE * across
    blocks = frames * per_frame
    across_of = [(band_cols >> l) // SIDE for l in range(LEVELS)]
    tiles_of = [((band_rows >> l) // SIDE) * across_of[l] for l in range(LEVELS)]

    smem = pl.BlockSpec(memory_space=pltpu.SMEM)
    vmem = pl.BlockSpec(memory_space=pltpu.VMEM)
    hbm = pl.BlockSpec(memory_space=pl.ANY)
    tiles = fmap1.reshape(frames * band_rows, across, SIDE, channels)

    def send_shape(parts):
        return jax.ShapeDtypeStruct((peers, parts, SIDE, channels), jnp.bfloat16)

    send1, slots = pl.pallas_call(
        first_body(peers, blocks, tiles_of, per_frame, across, band_rows),
        in_specs=[smem, smem, vmem],
        out_specs=[hbm, smem],
        out_shape=[
            send_shape(SLOTS * SIDE + 1),
            jax.ShapeDtypeStruct((LEVELS * blocks,), jnp.int32),
        ],
        scratch_shapes=[
            pltpu.SMEM((LEVELS * peers,), jnp.int32),
            pltpu.SMEM((LEVELS * SLOTS * peers,), jnp.int32),
            pltpu.VMEM((peers, SIDE, channels), jnp.bfloat16),
            pltpu.SemaphoreType.DMA((blocks,)),
            pltpu.SemaphoreType.DMA,
        ],
        name="build1",
    )(target_owner.transpose(0, 2, 1), target_tile, tiles)
    send0 = pl.pallas_call(
        second_body(blocks, per_frame, across, band_rows),
        in_specs=[smem, vmem],
        out_specs=hbm,
        out_shape=send_shape(SLOTS * SIDE),
        scratch_shapes=[pltpu.SemaphoreType.DMA((blocks,))],
        name="build0",
    )(slots, tiles)

    def exchange(value):
        return lax.all_to_all(value, AXES, split_axis=0, concat_axis=0, tiled=True)

    arrived = [exchange(send.reshape(peers, -1, channels)) for send in (send0, send1)]

    low, high = neighbours(fmap2, "rows", 1, SIDE)
    edges = [
        jnp.concatenate([lax.slice_in_dim(part, *span, axis=2) for part in (low, fmap2, high)], axis=1)
        for span in ((0, SIDE), (band_cols - SIDE, band_cols))
    ]
    west, east = swapped(edges[1], edges[0], "cols")
    tall = jnp.concatenate([low, fmap2, high], axis=1)
    wide = jnp.concatenate([west, tall, east], axis=2)
    maps = [wide[:, RADIUS:-RADIUS, RADIUS:-RADIUS], pool_level(wide)]

    replies = []
    for level in range(LEVELS):
        strips = window_strips(maps[level])
        served = pl.pallas_call(
            serve_body(level, maps[level].shape[1], across_of[level], tiles_of[level], frames, peers),
            grid=(peers // PEERS_A_STEP,),
            in_specs=[
                pl.BlockSpec((peers, SIDE, channels), lambda s: (0, LANES // SIDE, 0)),
                pl.BlockSpec((PEERS_A_STEP, LANES, channels), lambda s: (s, 0, 0)),
                pl.BlockSpec(strips.shape, lambda s: (0, 0, 0)),
            ],
            out_specs=pl.BlockSpec((PEERS_A_STEP, REPLY_ROWS, LANES), lambda s: (s, 0, 0)),
            scratch_shapes=[
                pltpu.VMEM((BENCHES, REPLY_ROWS, LANES), jnp.float32),
                pltpu.VMEM((peers, 128), jnp.int32),
                pltpu.SMEM((peers, 128), jnp.int32),
                pltpu.SemaphoreType.DMA,
            ],
            out_shape=jax.ShapeDtypeStruct((peers, REPLY_ROWS, LANES), jnp.int16),
        )(arrived[1], arrived[level], strips)
        replies.append(exchange(served))

    groups = 4
    width = groups * LANES
    whole = pl.BlockSpec((peers, REPLY_ROWS, LANES), lambda s, _: (0, 0, 0))
    out = pl.pallas_call(
        finish_body(blocks, groups, channels ** (-0.5)),
        grid_spec=pltpu.PrefetchScalarGridSpec(
            num_scalar_prefetch=1,
            grid=(blocks * QUERIES // width,),
            in_specs=[whole, whole],
            out_specs=pl.BlockSpec((WINDOW, LEVELS, width), lambda s, _: (0, 0, s)),
        ),
        out_shape=jax.ShapeDtypeStruct((WINDOW, LEVELS, blocks * QUERIES), jnp.float32),
        name="finish",
    )(slots, *replies)
    return out.transpose(1, 0, 2)


def solution(mesh):
    in_specs = (
        P(None, "rows", "cols", None),
        P(None, "rows", "cols", None),
        P(None, AXES, None),
        P(None, AXES),
    )
    out_specs = P(None, None, AXES)
    return jax.shard_map(steps, mesh=mesh, in_specs=in_specs, out_specs=out_specs, check_vma=False)
```

time: 436 us -> 402 us (0.922)
  waiting for transfers between devices: 237 us -> 108 us
  blocking collectives: 83.5 us -> 158 us
  Pallas kernels: 48.6 us -> 62.7 us
  starting transfers between devices: 29.3 us -> 35.7 us
    ppermute x2, waiting for transfers between devices: 234 us -> 106 us  [swapped(): lax.ppermute(downward, axis, backward)]
    all_to_all x1 -> x2, blocking collectives: 83.5 us -> 158 us  [exchange(): return lax.all_to_all(value, AXES, split_axis=0, concat_axis=0, tiled=True)]
    pallas_call x2 -> x4, Pallas kernels: 40.6 us -> 54.6 us  [the longest x2 42.7 us: steps(): pl.pallas_call(serve_body(level, maps[level].shape[1], across_of[level],...]
    all_to_all x1 -> x2, starting transfers between devices: 11.9 us -> 18.5 us  [exchange(): return lax.all_to_all(value, AXES, split_axis=0, concat_axis=0, tiled=True)]
  transfers between devices with their start and end apart: 5 -> 6, of which waited for: 3 -> 2; matrix products, arithmetic and copies ran while one was open for 8% -> 9% of each run, Pallas kernels for 0% -> 5%
where the time goes in v2:
time: 402 us; the launch traced here: 401 us
  blocking collectives  158 us (39%)
  waiting for transfers between devices  108 us (27%)
  Pallas kernels  62.7 us (16%)
  starting transfers between devices  35.7 us (9%)
  local copies, waits for them, and re-layouts  18.3 us (5%)
  other arithmetic  17.8 us (4%)
    all_to_all x2, blocking collectives, exchange(): return lax.all_to_all(value, AXES, split_axis=0, concat_axis=0, tiled=True)  158 us
    ppermute x2, waiting for transfers between devices, swapped(): lax.ppermute(downward, axis, backward)  106 us
    pallas_call x2, Pallas kernels, steps(): pl.pallas_call(serve_body(level, maps[level].shape[1], across_of[level],...  42.7 us
    all_to_all x2, starting transfers between devices, exchange(): return lax.all_to_all(value, AXES, split_axis=0, concat_axis=0, tiled=True)  18.5 us
    ppermute x2, starting transfers between devices, swapped(): lax.ppermute(upward, axis, forward)  13.8 us
    convert_element_type x1, local copies, waits for them, and re-layouts, pool_level(): level_map.astype(jnp.float32)  9.98 us
    reduce_sum x1, other arithmetic, pool_level(): return jnp.mean(pooled, axis=(2, 4)).astype(jnp.bfloat16)  9.35 us
    pallas_call x1, Pallas kernels, steps(): pl.pallas_call(finish_body(blocks, groups, channels ** (-0.5)), grid_spec...  8.15 us
  transfers between devices with their start and end apart: 6, of which 2 were waited for; matrix products, arithmetic and copies ran while one was open for 9% of the time, Pallas kernels for 5%

profile of v2, /device:TPU:1, one launch (start us, length us, event | category | flops | bytes accessed | tf_op | source)
XLA Modules:
  0.0 401.5 jit_solution(11202554442414523266)
XLA Ops:
  0.0 7.5 %build1.1 = (bf16[128,17,8,256]{3,2,1,0:T(8,128)(2,1)}, s32[128]{0:T(128)}) custom-call(s32[2,1,64]{2,1,0:T(1,128)} %bitcast.56, s32[2,64]{1,0:T(2,128)} %tile.1, bf16[64,8,8,256]{3,2,1,0:T(8,128)(2,1)} %bitcast.53), custom_call_target="tpu_custom_call" | custom-call | tf_op jit(solution)/shard_map/build1/pallas_call | solution.py:254
  7.5 4.4 %build0.1 = bf16[128,16,8,256]{3,2,1,0:T(8,128)(2,1)} custom-call(s32[128]{0:T(128)} %get-tuple-element.7.slots, bf16[64,8,8,256]{3,2,1,0:T(8,128)(2,1)} %bitcast.54), custom_call_target="tpu_custom_call" | custom-call | tf_op jit(solution)/shard_map/build0/pallas_call | solution.py:271
  11.9 110.2 %all_to_all.20.queries = bf16[128,128,256]{2,1,0:T(8,128)(2,1)} all-to-all(bf16[128,128,256]{2,1,0:T(8,128)(2,1)} %bitcast.51), channel_id=1, replica_groups=mesh['rows'=16,'cols'=8] {'rows','cols'}, dimensions={0} | all-to-all | bytes 16777216 | tf_op jit(solution)/shard_map/all_to_all | solution.py:281
  122.1 0.0 copy-start
  122.1 7.8 %all-to-all-start = ((bf16[128,136,256]{2,1,0:T(8,128)(2,1)}), bf16[128,136,256]{2,1,0:T(8,128)(2,1)}, u32[]{:S(2)}, u32[]{:S(2)}) async-start(bf16[128,136,256]{2,1,0:T(8,128)(2,1)} %bitcast.52), calls=%async_computation | async-start | bytes 17825792 | tf_op jit(solution)/shard_map/all_to_all | solution.py:281
  129.9 0.0 copy-done
  130.0 0.0 copy-start.1
  130.0 0.1 fusion.11
  130.1 1.4 collective-permute-start.1
  131.5 4.0 %collective-permute-start = (bf16[2,8,64,256]{3,2,1,0:T(8,128)(2,1)S(1)}, bf16[2,8,64,256]{3,2,1,0:T(8,128)(2,1)S(1)}, u32[]{:S(2)}, u32[]{:S(2)}) collective-permute-start(bf16[2,8,64,256]{3,2,1,0:T(8,128)(2,1)S(1)} %get-tuple-element.12), channel_id=1, source_target_pairs={{0,8},{8,16},{16,24},{24,32},{32,40},{40,48},{48,56},{56,64},{64,7... | collective-permute-start | bytes 1572872 | tf_op jit(solution)/shard_map/ppermute | solution.py:29
  135.6 105.8 %collective-permute-done.1 = bf16[2,8,64,256]{3,2,1,0:T(8,128)(2,1)S(1)} collective-permute-done((bf16[2,8,64,256]{3,2,1,0:T(8,128)(2,1)S(1)}, bf16[2,8,64,256]{3,2,1,0:T(8,128)(2,1)S(1)}, u32[]{:S(2)}, u32[]{:S(2)}) %collective-permute-start.1) | collective-permute-done | bytes 524320 | tf_op jit(solution)/shard_map/ppermute | solution.py:29
  241.4 0.0 collective-permute-done
  241.4 0.1 pad_maximum_fusion.3
  241.5 9.8 %collective-permute-start.2 = (bf16[2,48,8,256]{3,2,1,0:T(8,128)(2,1)S(1)}, bf16[2,48,8,256]{3,2,1,0:T(8,128)(2,1)S(1)}, u32[]{:S(2)}, u32[]{:S(2)}) collective-permute-start(bf16[2,48,8,256]{3,2,1,0:T(8,128)(2,1)S(1)} %pad_maximum_fusion.3), channel_id=1, source_target_pairs={{0,1},{1,2},{2,3},{3,4},{4,5},{5,6},{6,7},{8,9},{9,10},{10,11},{11... | collective-permute-start | bytes 1179656 | tf_op jit(solution)/shard_map/ppermute | solution.py:29
  251.3 0.1 pad_maximum_fusion.4
  251.3 1.9 collective-permute-start.3
  253.3 0.0 copy-done.1
  253.3 0.1 constant_dynamic-update-slice_fusion.1
  253.5 2.5 collective-permute-done.2
  256.0 1.1 fusion.9
  257.1 1.2 fusion.7
  258.3 1.2 fusion.6
  259.4 1.1 fusion.5
  260.6 1.2 fusion.4
  261.8 1.2 fusion.3
  263.0 1.1 fusion.2
  264.1 0.0 collective-permute-done.3
  264.1 0.0 copy-start.2
  264.1 0.7 copy-done.2
  264.9 1.3 fusion.1
  266.1 0.0 all-to-all-done.notes.queries
  266.1 21.9 %shard_map.46 = s16[128,88,128]{2,1,0:T(8,128)(2,1)} custom-call(bf16[128,136,256]{2,1,0:T(8,128)(2,1)} %all-to-all-done.notes.queries, bf16[128,128,256]{2,1,0:T(8,128)(2,1)} %all_to_all.20.queries, bf16[640,16,256]{2,1,0:T(8,128)(2,1)} %bitcast.13.strips), custom_call_target="tpu_custom_call" | custom-call | tf_op jit(solution)/shard_map/pallas_call | solution.py:298
  288.0 10.7 %all-to-all-start.2 = ((s16[128,88,128]{2,1,0:T(8,128)(2,1)}), s16[128,88,128]{2,1,0:T(8,128)(2,1)}, u32[]{:S(2)}, u32[]{:S(2)}) async-start(s16[128,88,128]{2,1,0:T(8,128)(2,1)} %shard_map.46), calls=%async_computation.2 | async-start | bytes 5767168 | tf_op jit(solution)/shard_map/all_to_all | solution.py:281
  298.7 4.5 %maximum_convert_fusion = f32[2,48,80,256]{3,2,1,0:T(8,128)} fusion(bf16[2,48,8,256]{3,2,1,0:T(8,128)(2,1)} %copy-done.2, bf16[2,48,64,256]{3,2,1,0:T(8,128)(2,1)S(1)} %constant_dynamic-update-slice_fusion, bf16[2,48,8,256]{3,2,1,0:T(8,128)(2,1)S(1)} %collective-permute-done.2), kind=kLoop, calls=%fused_computation | loop fusion | flops 11796480 | bytes 11796480 | tf_op jit(solution)/shard_map/convert_element_type | solution.py:39
  303.2 10.0 %reshape.24 = f32[2,24,2,40,2,256]{5,4,3,2,1,0:T(2,128)} reshape(f32[2,48,80,256]{3,2,1,0:T(8,128)} %maximum_convert_fusion) | data formatting | bytes 15728640 | tf_op jit(solution)/shard_map/convert_element_type | solution.py:39
  313.2 9.4 %reduce_sum.9 = f32[2,24,40,256]{3,2,1,0:T(8,128)S(1)} reduce(f32[2,24,2,40,2,256]{5,4,3,2,1,0:T(2,128)} %reshape.24, f32[]{:T(128)} %constant.1.clone.1), dimensions={2,4}, to_apply=%region_0.0 | reduce | flops 1474560 | bytes 9830404 | tf_op jit(solution)/shard_map/reduce_sum | solution.py:42
  322.6 0.2 multiply_convert_fusion
  322.8 0.2 slice_bitcast_fusion.9
  322.9 1.3 pad_maximum_fusion
  324.3 20.8 %shard_map.47 = s16[128,88,128]{2,1,0:T(8,128)(2,1)} custom-call(bf16[128,136,256]{2,1,0:T(8,128)(2,1)} %all-to-all-done.notes.queries, bf16[128,136,256]{2,1,0:T(8,128)(2,1)} %all-to-all-done.notes.queries, bf16[192,16,256]{2,1,0:T(8,128)(2,1)} %bitcast.55), custom_call_target="tpu_custom_call" | custom-call | tf_op jit(solution)/shard_map/pallas_call | solution.py:298
  345.1 0.0 all-to-all-done.2.reply0
  345.1 48.3 %all_to_all.21.reply1 = s16[128,88,128]{2,1,0:T(8,128)(2,1)} all-to-all(s16[128,88,128]{2,1,0:T(8,128)(2,1)} %shard_map.47), channel_id=1, replica_groups=mesh['rows'=16,'cols'=8] {'rows','cols'}, dimensions={0} | all-to-all | bytes 5767168 | tf_op jit(solution)/shard_map/all_to_all | solution.py:281
  393.4 8.1 %finish.1 = f32[81,2,4096]{2,1,0:T(2,128)} custom-call(s32[128]{0:T(128)} %get-tuple-element.7.slots, s16[128,88,128]{2,1,0:T(8,128)(2,1)} %all-to-all-done.2.reply0, s16[128,88,128]{2,1,0:T(8,128)(2,1)} %all_to_all.21.reply1), custom_call_target="tpu_custom_call" | custom-call | tf_op jit(solution)/shard_map/finish/pallas_call | solution.py:320
  (5 shorter events, 0.1 us)
Async XLA Ops:
  122.1 7.8 %copy-start = (bf16[2,32,64,256]{3,2,1,0:T(8,128)(2,1)S(1)}, bf16[2,32,64,256]{3,2,1,0:T(8,128)(2,1)}, u32[]{:S(2)}) copy-start(bf16[2,32,64,256]{3,2,1,0:T(8,128)(2,1)} %param.5) | copy-start | bytes 6291460
  122.1 144.0 %all-to-all-start = ((bf16[128,136,256]{2,1,0:T(8,128)(2,1)}), bf16[128,136,256]{2,1,0:T(8,128)(2,1)}, u32[]{:S(2)}, u32[]{:S(2)}) async-start(bf16[128,136,256]{2,1,0:T(8,128)(2,1)} %bitcast.52), calls=%async_computation | async-start | bytes 17825792 | tf_op jit(solution)/shard_map/all_to_all | solution.py:281
  130.0 123.4 %copy-start.1 = (bf16[2,32,64,256]{3,2,1,0:T(8,128)(2,1)S(1)}, bf16[2,32,64,256]{3,2,1,0:T(8,128)(2,1)}, u32[]{:S(2)}) copy-start(bf16[2,32,64,256]{3,2,1,0:T(8,128)(2,1)} %param.5) | copy-start | bytes 6291460
  130.1 111.3 %collective-permute-start.1 = (bf16[2,8,64,256]{3,2,1,0:T(8,128)(2,1)S(1)}, bf16[2,8,64,256]{3,2,1,0:T(8,128)(2,1)S(1)}, u32[]{:S(2)}, u32[]{:S(2)}) collective-permute-start(bf16[2,8,64,256]{3,2,1,0:T(8,128)(2,1)S(1)} %get-tuple-element.11), channel_id=1, source_target_pairs={{8,0},{16,8},{24,16},{32,24},{40,32},{48,40},{56,48},{64,56},{72,6... | collective-permute-start | bytes 1572872 | tf_op jit(solution)/shard_map/ppermute | solution.py:29
  131.5 109.9 %collective-permute-start = (bf16[2,8,64,256]{3,2,1,0:T(8,128)(2,1)S(1)}, bf16[2,8,64,256]{3,2,1,0:T(8,128)(2,1)S(1)}, u32[]{:S(2)}, u32[]{:S(2)}) collective-permute-start(bf16[2,8,64,256]{3,2,1,0:T(8,128)(2,1)S(1)} %get-tuple-element.12), channel_id=1, source_target_pairs={{0,8},{8,16},{16,24},{24,32},{32,40},{40,48},{48,56},{56,64},{64,7... | collective-permute-start | bytes 1572872 | tf_op jit(solution)/shard_map/ppermute | solution.py:29
  241.5 14.5 %collective-permute-start.2 = (bf16[2,48,8,256]{3,2,1,0:T(8,128)(2,1)S(1)}, bf16[2,48,8,256]{3,2,1,0:T(8,128)(2,1)S(1)}, u32[]{:S(2)}, u32[]{:S(2)}) collective-permute-start(bf16[2,48,8,256]{3,2,1,0:T(8,128)(2,1)S(1)} %pad_maximum_fusion.3), channel_id=1, source_target_pairs={{0,1},{1,2},{2,3},{3,4},{4,5},{5,6},{6,7},{8,9},{9,10},{10,11},{11... | collective-permute-start | bytes 1179656 | tf_op jit(solution)/shard_map/ppermute | solution.py:29
  251.3 12.8 %collective-permute-start.3 = (bf16[2,48,8,256]{3,2,1,0:T(8,128)(2,1)S(1)}, bf16[2,48,8,256]{3,2,1,0:T(8,128)(2,1)S(1)}, u32[]{:S(2)}, u32[]{:S(2)}) collective-permute-start(bf16[2,48,8,256]{3,2,1,0:T(8,128)(2,1)S(1)} %pad_maximum_fusion.4), channel_id=1, source_target_pairs={{1,0},{2,1},{3,2},{4,3},{5,4},{6,5},{7,6},{9,8},{10,9},{11,10},{12... | collective-permute-start | bytes 1179656 | tf_op jit(solution)/shard_map/ppermute | solution.py:29
  264.1 0.7 copy-start.2
  288.0 57.1 %all-to-all-start.2 = ((s16[128,88,128]{2,1,0:T(8,128)(2,1)}), s16[128,88,128]{2,1,0:T(8,128)(2,1)}, u32[]{:S(2)}, u32[]{:S(2)}) async-start(s16[128,88,128]{2,1,0:T(8,128)(2,1)} %shard_map.46), calls=%async_computation.2 | async-start | bytes 5767168 | tf_op jit(solution)/shard_map/all_to_all | solution.py:281

commit v3 on v2

--- a/solution.py
+++ b/solution.py
@@ -17,21 +17,35 @@
 LANES = SLOTS * QUERIES
 REPLY_ROWS = -(-(WINDOW + 1) // 8) * 8
 PEERS_A_STEP = 16
-BENCHES = 4
+BENCHES = 8
 FULL = 32767.0
 AXES = ("rows", "cols")
 
 
-def swapped(upward, downward, axis):
-    count = lax.axis_size(axis)
-    forward = [(i, i + 1) for i in range(count - 1)]
-    backward = [(target, source) for source, target in forward]
-    return lax.ppermute(upward, axis, forward), lax.ppermute(downward, axis, backward)
-
-
-def neighbours(block, axis, dim, width):
-    tail = lax.slice_in_dim(block, block.shape[dim] - width, None, axis=dim)
-    return swapped(tail, lax.slice_in_dim(block, 0, width, axis=dim), axis)
+def halo(block, width):
+    sizes = [lax.axis_size(axis) for axis in AXES]
+    rows, cols = block.shape[1:3]
+
+    def side(step, extent):
+        return {0: (0, extent), 1: (extent - width, extent), -1: (0, width)}[step]
+
+    def from_neighbour(down, right):
+        piece = block[:, slice(*side(down, rows)), slice(*side(right, cols))]
+        pairs = [
+            (r * sizes[1] + c, (r + down) * sizes[1] + c + right)
+            for r in range(sizes[0])
+            for c in range(sizes[1])
+            if 0 <= r + down < sizes[0] and 0 <= c + right < sizes[1]
+        ]
+        return lax.ppermute(piece, AXES, pairs)
+
+    bands = []
+    for down in (1, 0, -1):
+        band = [
+            block if down == right == 0 else from_neighbour(down, right) for right in (1, 0, -1)
+        ]
+        bands.append(jnp.concatenate(band, axis=2))
+    return jnp.concatenate(bands, axis=1)
 
 
 def pool_level(level_map):
@@ -221,13 +235,14 @@
         for level, reply in enumerate((reply0, reply1)):
             for group in range(groups):
                 k = level * blocks + (step * groups + group) * 2
-                halves = []
-                for side in range(2):
-                    slot = slots[k + side]
-                    block = reply[slot // SLOTS].astype(jnp.int32)
-                    turned = pltpu.roll(block, QUERIES, 1)
-                    halves.append(jnp.where(slot % SLOTS == side, block, turned))
-                both = jnp.where(low, halves[0], halves[1]).astype(jnp.float32)
+                slot = [slots[k + side] for side in range(2)]
+                block = [reply[at // SLOTS].astype(jnp.int32) for at in slot]
+                straight = jnp.where(low, block[0], block[1])
+                turned = pltpu.roll(jnp.where(low, block[1], block[0]), QUERIES, 1)
+                kept = [slot[side] % SLOTS == side for side in range(2)]
+                left = jnp.where(kept[0], straight, turned)
+                right = jnp.where(kept[1], straight, turned)
+                both = jnp.where(low, left, right).astype(jnp.float32)
                 factor = jnp.exp2(both[WINDOW : WINDOW + 1]) * (scale / FULL)
                 out[:, level, group * LANES : (group + 1) * LANES] = both[:WINDOW] * factor
 
@@ -282,14 +297,7 @@
 
     arrived = [exchange(send.reshape(peers, -1, channels)) for send in (send0, send1)]
 
-    low, high = neighbours(fmap2, "rows", 1, SIDE)
-    edges = [
-        jnp.concatenate([lax.slice_in_dim(part, *span, axis=2) for part in (low, fmap2, high)], axis=1)
-        for span in ((0, SIDE), (band_cols - SIDE, band_cols))
-    ]
-    west, east = swapped(edges[1], edges[0], "cols")
-    tall = jnp.concatenate([low, fmap2, high], axis=1)
-    wide = jnp.concatenate([west, tall, east], axis=2)
+    wide = halo(fmap2, SIDE)
     maps = [wide[:, RADIUS:-RADIUS, RADIUS:-RADIUS], pool_level(wide)]
 
     replies = []

time: 402 us -> 407 us (1.012)
  starting transfers between devices: 35.7 us -> 43.4 us
  Pallas kernels: 62.7 us -> 56.1 us
  waiting for transfers between devices: 108 us -> 114 us
    pallas_call x2, Pallas kernels: 42.7 us -> 36 us  [steps(): pl.pallas_call(serve_body(level, maps[level].shape[1], across_of[level],...]
    ppermute x4 -> x8, waiting for transfers between devices: 108 us -> 114 us  [from_neighbour(): return lax.ppermute(piece, AXES, pairs)]
    ppermute x4 -> x8, starting transfers between devices: 17.2 us -> 22.8 us  [from_neighbour(): return lax.ppermute(piece, AXES, pairs)]
    convert_element_type x1 -> x0, other arithmetic: 4.5 us -> none  [pool_level(): level_map.astype(jnp.float32)]
    unnamed x14 -> x13, local copies, waits for them, and re-layouts: 7.96 us -> 8.14 us
  transfers between devices with their start and end apart: 6 -> 10, of which waited for: 2 -> 4; matrix products, arithmetic and copies ran while one was open for 9% -> 8% of each run, Pallas kernels for 5% -> 4%
where the time goes in v3:
time: 407 us; the launch traced here: 406 us
  blocking collectives  158 us (39%)
  waiting for transfers between devices  114 us (28%)
  Pallas kernels  56.1 us (14%)
  starting transfers between devices  43.4 us (11%)
  local copies, waits for them, and re-layouts  19 us (5%)
  other arithmetic  14.5 us (4%)
    all_to_all x2, blocking collectives, exchange(): return lax.all_to_all(value, AXES, split_axis=0, concat_axis=0, tiled=True)  158 us
    ppermute x8, waiting for transfers between devices, from_neighbour(): return lax.ppermute(piece, AXES, pairs)  114 us
    pallas_call x2, Pallas kernels, steps(): pl.pallas_call(serve_body(level, maps[level].shape[1], across_of[level],...  36 us
    ppermute x8, starting transfers between devices, from_neighbour(): return lax.ppermute(piece, AXES, pairs)  22.8 us
    all_to_all x2, starting transfers between devices, exchange(): return lax.all_to_all(value, AXES, split_axis=0, concat_axis=0, tiled=True)  20.7 us
    reduce_sum x1, other arithmetic, pool_level(): return jnp.mean(pooled, axis=(2, 4)).astype(jnp.bfloat16)  10.6 us
    convert_element_type x1, local copies, waits for them, and re-layouts, pool_level(): level_map.astype(jnp.float32)  9.41 us
    unnamed x13, local copies, waits for them, and re-layouts  8.14 us
  transfers between devices with their start and end apart: 10, of which 4 were waited for; matrix products, arithmetic and copies ran while one was open for 8% of the time, Pallas kernels for 4%

profile of v3, /device:TPU:1, one launch (start us, length us, event | category | flops | bytes accessed | tf_op | source)
XLA Modules:
  0.0 405.6 jit_solution(402743113542649677)
XLA Ops:
  0.0 7.5 %build1.1 = (bf16[128,17,8,256]{3,2,1,0:T(8,128)(2,1)}, s32[128]{0:T(128)}) custom-call(s32[2,1,64]{2,1,0:T(1,128)} %bitcast.56, s32[2,64]{1,0:T(2,128)} %tile.1, bf16[64,8,8,256]{3,2,1,0:T(8,128)(2,1)} %bitcast.53), custom_call_target="tpu_custom_call" | custom-call | tf_op jit(solution)/shard_map/build1/pallas_call | solution.py:269
  7.5 4.5 %build0.1 = bf16[128,16,8,256]{3,2,1,0:T(8,128)(2,1)} custom-call(s32[128]{0:T(128)} %get-tuple-element.7.slots, bf16[64,8,8,256]{3,2,1,0:T(8,128)(2,1)} %bitcast.54), custom_call_target="tpu_custom_call" | custom-call | tf_op jit(solution)/shard_map/build0/pallas_call | solution.py:286
  12.0 110.2 %all_to_all.20.queries = bf16[128,128,256]{2,1,0:T(8,128)(2,1)} all-to-all(bf16[128,128,256]{2,1,0:T(8,128)(2,1)} %bitcast.51), channel_id=1, replica_groups=mesh['rows'=16,'cols'=8] {'rows','cols'}, dimensions={0} | all-to-all | bytes 16777216 | tf_op jit(solution)/shard_map/all_to_all | solution.py:296
  122.1 0.0 copy-start.2
  122.1 7.8 %all-to-all-start = ((bf16[128,136,256]{2,1,0:T(8,128)(2,1)}), bf16[128,136,256]{2,1,0:T(8,128)(2,1)}, u32[]{:S(2)}, u32[]{:S(2)}) async-start(bf16[128,136,256]{2,1,0:T(8,128)(2,1)} %bitcast.52), calls=%async_computation | async-start | bytes 17825792 | tf_op jit(solution)/shard_map/all_to_all | solution.py:296
  130.0 0.0 copy-done.2
  130.0 0.1 fusion.9
  130.1 1.3 collective-permute-start.6
  131.4 4.0 collective-permute-start.1
  135.4 1.3 collective-permute-start.7
  136.8 3.6 collective-permute-start.4
  140.4 2.5 collective-permute-start.3
  142.9 106.9 %collective-permute-done.7 = bf16[2,8,8,256]{3,2,1,0:T(8,128)(2,1)S(1)} collective-permute-done((bf16[2,8,8,256]{3,2,1,0:T(8,128)(2,1)S(1)}, bf16[2,8,8,256]{3,2,1,0:T(8,128)(2,1)S(1)}, u32[]{:S(2)}, u32[]{:S(2)}) %collective-permute-start.7) | collective-permute-done | bytes 65568 | tf_op jit(solution)/shard_map/ppermute | solution.py:40
  249.8 1.3 collective-permute-start.5
  251.1 4.4 %collective-permute-done.5 = bf16[2,8,8,256]{3,2,1,0:T(8,128)(2,1)S(1)} collective-permute-done((bf16[2,8,8,256]{3,2,1,0:T(8,128)(2,1)S(1)}, bf16[2,8,8,256]{3,2,1,0:T(8,128)(2,1)S(1)}, u32[]{:S(2)}, u32[]{:S(2)}) %collective-permute-start.5) | collective-permute-done | bytes 65568 | tf_op jit(solution)/shard_map/ppermute | solution.py:40
  255.5 1.7 collective-permute-start.2
  257.2 1.3 collective-permute-done.2
  258.5 7.0 %collective-permute-start = (bf16[2,8,8,256]{3,2,1,0:T(8,128)(2,1)S(1)}, bf16[2,8,8,256]{3,2,1,0:T(8,128)(2,1)S(1)}, u32[]{:S(2)}, u32[]{:S(2)}) collective-permute-start(bf16[2,8,8,256]{3,2,1,0:T(8,128)(2,1)S(1)} %get-tuple-element.9), channel_id=1, source_target_pairs={{0,9},{1,10},{2,11},{3,12},{4,13},{5,14},{6,15},{8,17},{9,18},{10,... | collective-permute-start | bytes 196616 | tf_op jit(solution)/shard_map/ppermute | solution.py:40
  265.5 1.3 collective-permute-done
  266.9 0.0 collective-permute-done.4
  266.9 0.0 collective-permute-done.3
  266.9 0.0 collective-permute-done.6
  266.9 0.0 collective-permute-done.1
  266.9 0.8 maximum_maximum_fusion
  267.7 0.0 copy-start
  267.7 1.3 fusion.7
  268.9 1.1 fusion.6
  270.1 1.1 fusion.5
  271.2 1.1 fusion.4
  272.3 1.2 fusion.3
  273.5 1.1 fusion.2
  274.7 1.2 fusion.1
  275.8 0.0 copy-done
  275.8 1.2 fusion
  277.0 0.0 all-to-all-done.notes.queries
  277.0 18.5 %shard_map.46 = s16[128,88,128]{2,1,0:T(8,128)(2,1)} custom-call(bf16[128,136,256]{2,1,0:T(8,128)(2,1)} %all-to-all-done.notes.queries, bf16[128,128,256]{2,1,0:T(8,128)(2,1)} %all_to_all.20.queries, bf16[640,16,256]{2,1,0:T(8,128)(2,1)} %bitcast.13.strips), custom_call_target="tpu_custom_call" | custom-call | tf_op jit(solution)/shard_map/pallas_call | solution.py:306
  295.5 12.9 %all-to-all-start.2 = ((s16[128,88,128]{2,1,0:T(8,128)(2,1)}), s16[128,88,128]{2,1,0:T(8,128)(2,1)S(1)}, u32[]{:S(2)}, u32[]{:S(2)}) async-start(s16[128,88,128]{2,1,0:T(8,128)(2,1)} %shard_map.46), calls=%async_computation.2 | async-start | bytes 5767168 | tf_op jit(solution)/shard_map/all_to_all | solution.py:296
  308.4 9.4 %reshape.24 = f32[2,24,2,40,2,256]{5,4,3,2,1,0:T(2,128)} reshape(bf16[2,48,80,256]{3,2,1,0:T(8,128)(2,1)} %copy-done) | data formatting | bytes 11796480 | tf_op jit(solution)/shard_map/convert_element_type | solution.py:53
  317.8 10.6 %reduce_sum.9 = f32[2,24,40,256]{3,2,1,0:T(8,128)} reduce(f32[2,24,2,40,2,256]{5,4,3,2,1,0:T(2,128)} %reshape.24, f32[]{:T(128)} %constant.1.clone.1), dimensions={2,4}, to_apply=%region_0.0 | reduce | flops 1474560 | bytes 9830404 | tf_op jit(solution)/shard_map/reduce_sum | solution.py:56
  328.4 1.7 multiply_convert_fusion
  330.2 0.2 slice_bitcast_fusion.11
  330.3 1.3 pad_maximum_fusion
  331.7 17.5 %shard_map.47 = s16[128,88,128]{2,1,0:T(8,128)(2,1)} custom-call(bf16[128,136,256]{2,1,0:T(8,128)(2,1)} %all-to-all-done.notes.queries, bf16[128,136,256]{2,1,0:T(8,128)(2,1)} %all-to-all-done.notes.queries, bf16[192,16,256]{2,1,0:T(8,128)(2,1)} %bitcast.55), custom_call_target="tpu_custom_call" | custom-call | tf_op jit(solution)/shard_map/pallas_call | solution.py:306
  349.2 0.0 all-to-all-done.2.reply0
  349.2 0.0 copy-start.1
  349.2 48.3 %all_to_all.21.reply1 = s16[128,88,128]{2,1,0:T(8,128)(2,1)} all-to-all(s16[128,88,128]{2,1,0:T(8,128)(2,1)} %shard_map.47), channel_id=1, replica_groups=mesh['rows'=16,'cols'=8] {'rows','cols'}, dimensions={0} | all-to-all | bytes 5767168 | tf_op jit(solution)/shard_map/all_to_all | solution.py:296
  397.5 0.0 copy-done.1
  397.5 8.1 %finish.1 = f32[81,2,4096]{2,1,0:T(2,128)} custom-call(s32[128]{0:T(128)} %get-tuple-element.7.slots, s16[128,88,128]{2,1,0:T(8,128)(2,1)} %copy-done.1, s16[128,88,128]{2,1,0:T(8,128)(2,1)} %all_to_all.21.reply1), custom_call_target="tpu_custom_call" | custom-call | tf_op jit(solution)/shard_map/finish/pallas_call | solution.py:328
  (2 shorter events, 0.1 us)
Async XLA Ops:
  122.1 7.8 %copy-start.2 = (bf16[2,32,64,256]{3,2,1,0:T(8,128)(2,1)S(1)}, bf16[2,32,64,256]{3,2,1,0:T(8,128)(2,1)}, u32[]{:S(2)}) copy-start(bf16[2,32,64,256]{3,2,1,0:T(8,128)(2,1)} %param.5) | copy-start | bytes 6291460
  122.1 154.8 %all-to-all-start = ((bf16[128,136,256]{2,1,0:T(8,128)(2,1)}), bf16[128,136,256]{2,1,0:T(8,128)(2,1)}, u32[]{:S(2)}, u32[]{:S(2)}) async-start(bf16[128,136,256]{2,1,0:T(8,128)(2,1)} %bitcast.52), calls=%async_computation | async-start | bytes 17825792 | tf_op jit(solution)/shard_map/all_to_all | solution.py:296
  130.1 136.8 %collective-permute-start.6 = (bf16[2,8,64,256]{3,2,1,0:T(8,128)(2,1)S(1)}, bf16[2,8,64,256]{3,2,1,0:T(8,128)(2,1)S(1)}, u32[]{:S(2)}, u32[]{:S(2)}) collective-permute-start(bf16[2,8,64,256]{3,2,1,0:T(8,128)(2,1)S(1)} %get-tuple-element.14), channel_id=1, source_target_pairs={{8,0},{9,1},{10,2},{11,3},{12,4},{13,5},{14,6},{15,7},{16,8},{17,9... | collective-permute-start | bytes 1572872 | tf_op jit(solution)/shard_map/ppermute | solution.py:40
  131.4 135.5 %collective-permute-start.1 = (bf16[2,8,64,256]{3,2,1,0:T(8,128)(2,1)S(1)}, bf16[2,8,64,256]{3,2,1,0:T(8,128)(2,1)S(1)}, u32[]{:S(2)}, u32[]{:S(2)}) collective-permute-start(bf16[2,8,64,256]{3,2,1,0:T(8,128)(2,1)S(1)} %get-tuple-element.13), channel_id=1, source_target_pairs={{0,8},{1,9},{2,10},{3,11},{4,12},{5,13},{6,14},{7,15},{8,16},{9,17... | collective-permute-start | bytes 1572872 | tf_op jit(solution)/shard_map/ppermute | solution.py:40
  135.4 114.4 %collective-permute-start.7 = (bf16[2,8,8,256]{3,2,1,0:T(8,128)(2,1)S(1)}, bf16[2,8,8,256]{3,2,1,0:T(8,128)(2,1)S(1)}, u32[]{:S(2)}, u32[]{:S(2)}) collective-permute-start(bf16[2,8,8,256]{3,2,1,0:T(8,128)(2,1)S(1)} %get-tuple-element.12), channel_id=1, source_target_pairs={{9,0},{10,1},{11,2},{12,3},{13,4},{14,5},{15,6},{17,8},{18,9},{19,... | collective-permute-start | bytes 196616 | tf_op jit(solution)/shard_map/ppermute | solution.py:40
  136.8 130.1 %collective-permute-start.4 = (bf16[2,32,8,256]{3,2,1,0:T(8,128)(2,1)S(1)}, bf16[2,32,8,256]{3,2,1,0:T(8,128)(2,1)S(1)}, u32[]{:S(2)}, u32[]{:S(2)}) collective-permute-start(bf16[2,32,8,256]{3,2,1,0:T(8,128)(2,1)S(1)} %get-tuple-element.16), channel_id=1, source_target_pairs={{1,0},{2,1},{3,2},{4,3},{5,4},{6,5},{7,6},{9,8},{10,9},{11,10},{12... | collective-permute-start | bytes 786440 | tf_op jit(solution)/shard_map/ppermute | solution.py:40
  140.4 126.5 %collective-permute-start.3 = (bf16[2,32,8,256]{3,2,1,0:T(8,128)(2,1)S(1)}, bf16[2,32,8,256]{3,2,1,0:T(8,128)(2,1)S(1)}, u32[]{:S(2)}, u32[]{:S(2)}) collective-permute-start(bf16[2,32,8,256]{3,2,1,0:T(8,128)(2,1)S(1)} %get-tuple-element.15), channel_id=1, source_target_pairs={{0,1},{1,2},{2,3},{3,4},{4,5},{5,6},{6,7},{8,9},{9,10},{10,11},{11... | collective-permute-start | bytes 786440 | tf_op jit(solution)/shard_map/ppermute | solution.py:40
  249.8 5.7 %collective-permute-start.5 = (bf16[2,8,8,256]{3,2,1,0:T(8,128)(2,1)S(1)}, bf16[2,8,8,256]{3,2,1,0:T(8,128)(2,1)S(1)}, u32[]{:S(2)}, u32[]{:S(2)}) collective-permute-start(bf16[2,8,8,256]{3,2,1,0:T(8,128)(2,1)S(1)} %get-tuple-element.10), channel_id=1, source_target_pairs={{8,1},{9,2},{10,3},{11,4},{12,5},{13,6},{14,7},{16,9},{17,10},{18,... | collective-permute-start | bytes 196616 | tf_op jit(solution)/shard_map/ppermute | solution.py:40
  255.5 3.1 collective-permute-start.2
  258.5 8.3 %collective-permute-start = (bf16[2,8,8,256]{3,2,1,0:T(8,128)(2,1)S(1)}, bf16[2,8,8,256]{3,2,1,0:T(8,128)(2,1)S(1)}, u32[]{:S(2)}, u32[]{:S(2)}) collective-permute-start(bf16[2,8,8,256]{3,2,1,0:T(8,128)(2,1)S(1)} %get-tuple-element.9), channel_id=1, source_target_pairs={{0,9},{1,10},{2,11},{3,12},{4,13},{5,14},{6,15},{8,17},{9,18},{10,... | collective-permute-start | bytes 196616 | tf_op jit(solution)/shard_map/ppermute | solution.py:40
  267.7 8.1 %copy-start = (bf16[2,48,80,256]{3,2,1,0:T(8,128)(2,1)}, bf16[2,48,80,256]{3,2,1,0:T(8,128)(2,1)S(1)}, u32[]{:S(2)}) copy-start(bf16[2,48,80,256]{3,2,1,0:T(8,128)(2,1)S(1)} %maximum_maximum_fusion) | copy-start | bytes 11796484
  295.5 53.7 %all-to-all-start.2 = ((s16[128,88,128]{2,1,0:T(8,128)(2,1)}), s16[128,88,128]{2,1,0:T(8,128)(2,1)S(1)}, u32[]{:S(2)}, u32[]{:S(2)}) async-start(s16[128,88,128]{2,1,0:T(8,128)(2,1)} %shard_map.46), calls=%async_computation.2 | async-start | bytes 5767168 | tf_op jit(solution)/shard_map/all_to_all | solution.py:296
  349.2 48.3 %copy-start.1 = (s16[128,88,128]{2,1,0:T(8,128)(2,1)}, s16[128,88,128]{2,1,0:T(8,128)(2,1)S(1)}, u32[]{:S(2)}) copy-start(s16[128,88,128]{2,1,0:T(8,128)(2,1)S(1)} %all-to-all-done.2.reply0) | copy-start | bytes 8650756

commit v4 on v2

--- a/solution.py
+++ b/solution.py
@@ -15,9 +15,11 @@
 QUERIES = SIDE * SIDE
 SLOTS = 2
 LANES = SLOTS * QUERIES
-REPLY_ROWS = -(-(WINDOW + 1) // 8) * 8
+PART_ROWS = 88
+EARLY_ROWS = 80
+REPLY_ROWS = EARLY_ROWS + PART_ROWS
 PEERS_A_STEP = 16
-BENCHES = 4
+BENCHES = 8
 FULL = 32767.0
 AXES = ("rows", "cols")
 
@@ -142,28 +144,33 @@
     return kernel
 
 
-def serve_body(level, rows, across, tiles, frames, peers):
-    def kernel(notes, queries, strips, reply, flat, lines, labels, sem):
-        step = pl.program_id(0)
+def window_table(query, cells, first, i_part, j_part):
+    tables = [
+        lax.dot_general(
+            window.reshape(SPAN * SPAN, -1),
+            query,
+            (((1,), (1,)), ((), ())),
+            preferred_element_type=jnp.float32,
+        )
+        for window in cells
+    ]
+    table = jnp.where(first, tables[0], tables[1]).reshape(SPAN, SPAN, LANES)
+    for bit in (4, 2, 1):
+        left = table.shape[0] - bit
+        table = jnp.where(i_part & bit != 0, table[bit:], table[:left])
+    table = table.reshape(WIN * SPAN, LANES)
+    for bit in (4, 2, 1):
+        table = jnp.where(j_part & bit != 0, pltpu.roll(table, WIN * SPAN - bit, 0), table)
+    return table
+
+
+def serve_body(rows, across, tiles, frames, label_of):
+    def run(step, queries, strips, flat, store):
         lane = lax.broadcasted_iota(jnp.int32, (1, LANES), 1)
         first = lane < QUERIES
         i_part = lane % QUERIES // SIDE
         j_part = lane % SIDE
-        row_id = lax.broadcasted_iota(jnp.int32, (REPLY_ROWS, LANES), 0)
-
-        @pl.when(step == 0)
-        def _():
-            flat[...] = jnp.zeros_like(flat)
-
-            def line(peer, carry):
-                values = notes[peer].astype(jnp.float32).astype(jnp.int32)
-                lines[pl.ds(peer, 1), :] = values[:1, : lines.shape[1]]
-                return carry
-
-            lax.fori_loop(0, peers, line, 0, unroll=8)
-            taken = pltpu.make_async_copy(lines, labels, sem)
-            taken.start()
-            taken.wait()
+        row_id = lax.broadcasted_iota(jnp.int32, (PART_ROWS, LANES), 0)
 
         def start_of(label):
             tile = label % tiles
@@ -171,29 +178,11 @@
             return (column * frames + label // tiles) * rows + tile // across * SIDE
 
         def one(peer, bench):
-            query = queries[peer]
-            tables = []
-            for slot in range(SLOTS):
-                label = labels[step * PEERS_A_STEP + peer, level * SLOTS + slot]
-                cells = strips[pl.ds(start_of(label), SPAN)]
-                tables.append(
-                    lax.dot_general(
-                        cells.reshape(SPAN * SPAN, -1),
-                        query,
-                        (((1,), (1,)), ((), ())),
-                        preferred_element_type=jnp.float32,
-                    )
-                )
-            table = jnp.where(first, tables[0], tables[1])
-            table = table.reshape(SPAN, SPAN, LANES)
-            for bit in (4, 2, 1):
-                left = table.shape[0] - bit
-                table = jnp.where(i_part & bit != 0, table[bit:], table[:left])
-            table = table.reshape(WIN * SPAN, LANES)
-            for bit in (4, 2, 1):
-                table = jnp.where(
-                    j_part & bit != 0, pltpu.roll(table, WIN * SPAN - bit, 0), table
-                )
+            cells = [
+                strips[pl.ds(start_of(label_of(step * PEERS_A_STEP + peer, slot)), SPAN)]
+                for slot in range(SLOTS)
+            ]
+            table = window_table(queries[peer], cells, first, i_part, j_part)
             for a in range(WIN):
                 flat[bench, a * WIN : (a + 1) * WIN, :] = table[a * SPAN : a * SPAN + WIN]
             values = flat[bench]
@@ -201,8 +190,7 @@
             power = jnp.ceil(jnp.log2(jnp.maximum(top, 1e-30)))
             coded = jnp.round(values * (jnp.exp2(-power) * FULL))
             coded = jnp.clip(coded, -FULL, FULL)
-            coded = jnp.where(row_id == WINDOW, power, coded)
-            reply[peer] = coded.astype(jnp.int32).astype(jnp.int16)
+            store(peer, row_id, jnp.where(row_id == WINDOW, power, coded).astype(jnp.int32))
 
         def turn(i, carry):
             for bench in range(BENCHES):
@@ -211,25 +199,93 @@
 
         lax.fori_loop(0, PEERS_A_STEP // BENCHES, turn, 0)
 
+    return run
+
+
+def serve1_body(rows, across, tiles, frames, peers):
+    def kernel(notes, queries, strips, part, others, flat, lines, labels, sem):
+        step = pl.program_id(0)
+
+        @pl.when(step == 0)
+        def _():
+            flat[...] = jnp.zeros_like(flat)
+
+            def line(peer, carry):
+                values = notes[peer].astype(jnp.float32).astype(jnp.int32)
+                lines[pl.ds(peer, 1), :] = values[:1, : lines.shape[1]]
+                return carry
+
+            lax.fori_loop(0, peers, line, 0, unroll=8)
+            taken = pltpu.make_async_copy(lines, labels, sem)
+            taken.start()
+            taken.wait()
+
+            def other(peer, carry):
+                for slot in range(SLOTS):
+                    others[peer * SLOTS + slot] = labels[peer, slot]
+                return carry
+
+            lax.fori_loop(0, peers, other, 0, unroll=4)
+
+        def store(peer, row_id, coded):
+            part[peer] = coded.astype(jnp.int16)
+
+        run = serve_body(rows, across, tiles, frames, lambda p, slot: labels[p, SLOTS + slot])
+        run(step, queries, strips, flat, store)
+
     return kernel
 
 
+def serve0_body(rows, across, tiles, frames):
+    def kernel(labels, queries, strips, part, reply, flat):
+        step = pl.program_id(0)
+
+        @pl.when(step == 0)
+        def _():
+            flat[...] = jnp.zeros_like(flat)
+
+        def store(peer, row_id, coded):
+            rest = part[peer, EARLY_ROWS:PART_ROWS].astype(jnp.int32)
+            coded = jnp.where(row_id == WINDOW + 1, rest[0:1], coded)
+            coded = jnp.where(row_id == WINDOW + 2, rest[1:2], coded)
+            reply[peer, :EARLY_ROWS] = part[peer, :EARLY_ROWS]
+            reply[peer, EARLY_ROWS:] = coded.astype(jnp.int16)
+
+        run = serve_body(rows, across, tiles, frames, lambda p, slot: labels[p * SLOTS + slot])
+        run(step, queries, strips, flat, store)
+
+    return kernel
+
+
 def finish_body(blocks, groups, scale):
-    def kernel(slots, reply0, reply1, out):
+    def kernel(slots, reply, out):
         step = pl.program_id(0)
         low = lax.broadcasted_iota(jnp.int32, (1, LANES), 1) < QUERIES
-        for level, reply in enumerate((reply0, reply1)):
-            for group in range(groups):
-                k = level * blocks + (step * groups + group) * 2
-                halves = []
-                for side in range(2):
-                    slot = slots[k + side]
-                    block = reply[slot // SLOTS].astype(jnp.int32)
-                    turned = pltpu.roll(block, QUERIES, 1)
-                    halves.append(jnp.where(slot % SLOTS == side, block, turned))
-                both = jnp.where(low, halves[0], halves[1]).astype(jnp.float32)
-                factor = jnp.exp2(both[WINDOW : WINDOW + 1]) * (scale / FULL)
-                out[:, level, group * LANES : (group + 1) * LANES] = both[:WINDOW] * factor
+
+        def joined(slot, begin, end):
+            block = [reply[at // SLOTS, begin:end].astype(jnp.int32) for at in slot]
+            straight = jnp.where(low, block[0], block[1])
+            turned = pltpu.roll(jnp.where(low, block[1], block[0]), QUERIES, 1)
+            kept = [slot[side] % SLOTS == side for side in range(2)]
+            left = jnp.where(kept[0], straight, turned)
+            right = jnp.where(kept[1], straight, turned)
+            return jnp.where(low, left, right).astype(jnp.float32)
+
+        def unit(power):
+            return jnp.exp2(power) * (scale / FULL)
+
+        for group in range(groups):
+            k = (step * groups + group) * 2
+            lanes = slice(group * LANES, (group + 1) * LANES)
+            late = joined([slots[k], slots[k + 1]], EARLY_ROWS, REPLY_ROWS)
+            out[:, 0, lanes] = late[:WINDOW] * unit(late[WINDOW : WINDOW + 1])
+            slot = [slots[blocks + k], slots[blocks + k + 1]]
+            early = joined(slot, 0, EARLY_ROWS)
+            last = joined(slot, REPLY_ROWS - 8, REPLY_ROWS)
+            at = WINDOW - EARLY_ROWS
+            factor = unit(last[at + 2 : at + 3])
+            out[:EARLY_ROWS, 1, lanes] = early * factor
+            out[EARLY_ROWS:, 1, lanes] = last[at + 1 : at + 2] * factor
 
     return kernel
 
@@ -292,27 +348,57 @@
     wide = jnp.concatenate([west, tall, east], axis=2)
     maps = [wide[:, RADIUS:-RADIUS, RADIUS:-RADIUS], pool_level(wide)]
 
-    replies = []
+    strips = []
     for level in range(LEVELS):
-        strips = window_strips(maps[level])
-        served = pl.pallas_call(
-            serve_body(level, maps[level].shape[1], across_of[level], tiles_of[level], frames, peers),
-            grid=(peers // PEERS_A_STEP,),
-            in_specs=[
-                pl.BlockSpec((peers, SIDE, channels), lambda s: (0, LANES // SIDE, 0)),
-                pl.BlockSpec((PEERS_A_STEP, LANES, channels), lambda s: (s, 0, 0)),
-                pl.BlockSpec(strips.shape, lambda s: (0, 0, 0)),
-            ],
-            out_specs=pl.BlockSpec((PEERS_A_STEP, REPLY_ROWS, LANES), lambda s: (s, 0, 0)),
-            scratch_shapes=[
-                pltpu.VMEM((BENCHES, REPLY_ROWS, LANES), jnp.float32),
-                pltpu.VMEM((peers, 128), jnp.int32),
-                pltpu.SMEM((peers, 128), jnp.int32),
-                pltpu.SemaphoreType.DMA,
-            ],
-            out_shape=jax.ShapeDtypeStruct((peers, REPLY_ROWS, LANES), jnp.int16),
-        )(arrived[1], arrived[level], strips)
-        replies.append(exchange(served))
+        strips.append(window_strips(maps[level]))
+
+    def facts(level):
+        return maps[level].shape[1], across_of[level], tiles_of[level], frames
+
+    grid = (peers // PEERS_A_STEP,)
+    query_block = pl.BlockSpec((PEERS_A_STEP, LANES, channels), lambda s, *_: (s, 0, 0))
+    part_block = pl.BlockSpec((PEERS_A_STEP, PART_ROWS, LANES), lambda s, *_: (s, 0, 0))
+    flat = pltpu.VMEM((BENCHES, PART_ROWS, LANES), jnp.float32)
+
+    def strip_block(level):
+        return pl.BlockSpec(strips[level].shape, lambda s, *_: (0, 0, 0))
+
+    part, labels0 = pl.pallas_call(
+        serve1_body(*facts(1), peers),
+        grid=grid,
+        in_specs=[
+            pl.BlockSpec((peers, SIDE, channels), lambda s: (0, LANES // SIDE, 0)),
+            query_block,
+            strip_block(1),
+        ],
+        out_specs=[part_block, smem],
+        out_shape=[
+            jax.ShapeDtypeStruct((peers, PART_ROWS, LANES), jnp.int16),
+            jax.ShapeDtypeStruct((peers * SLOTS,), jnp.int32),
+        ],
+        scratch_shapes=[
+            flat,
+            pltpu.VMEM((peers, 128), jnp.int32),
+            pltpu.SMEM((peers, 128), jnp.int32),
+            pltpu.SemaphoreType.DMA,
+        ],
+        name="serve1",
+    )(arrived[1], arrived[1], strips[1])
+    served = pl.pallas_call(
+        serve0_body(*facts(0)),
+        grid_spec=pltpu.PrefetchScalarGridSpec(
+            num_scalar_prefetch=1,
+            grid=grid,
+            in_specs=[query_block, strip_block(0), part_block],
+            out_specs=pl.BlockSpec(
+                (PEERS_A_STEP, REPLY_ROWS, LANES), lambda s, *_: (s, 0, 0)
+            ),
+            scratch_shapes=[flat],
+        ),
+        out_shape=jax.ShapeDtypeStruct((peers, REPLY_ROWS, LANES), jnp.int16),
+        name="serve0",
+    )(labels0, arrived[0], strips[0], part)
+    reply = exchange(served)
 
     groups = 4
     width = groups * LANES
@@ -322,12 +408,12 @@
         grid_spec=pltpu.PrefetchScalarGridSpec(
             num_scalar_prefetch=1,
             grid=(blocks * QUERIES // width,),
-            in_specs=[whole, whole],
+            in_specs=[whole],
             out_specs=pl.BlockSpec((WINDOW, LEVELS, width), lambda s, _: (0, 0, s)),
         ),
         out_shape=jax.ShapeDtypeStruct((WINDOW, LEVELS, blocks * QUERIES), jnp.float32),
         name="finish",
-    )(slots, *replies)
+    )(slots, reply)
     return out.transpose(1, 0, 2)
 
 

time: 402 us -> 418 us (1.040)
  waiting for transfers between devices: 108 us -> 207 us
  blocking collectives: 158 us -> 75.4 us
  Pallas kernels: 62.7 us -> 55.5 us
  starting transfers between devices: 35.7 us -> 42.4 us
    all_to_all x2, waiting for transfers between devices: 0.01 us -> 103 us  [exchange(): return lax.all_to_all(value, AXES, split_axis=0, concat_axis=0, tiled=True)]
    ppermute x2, waiting for transfers between devices: 106 us -> 5.94 us  [swapped(): lax.ppermute(downward, axis, backward)]
    ppermute x2, waiting for transfers between devices: 2.47 us -> 98.1 us  [swapped(): lax.ppermute(upward, axis, forward)]
    all_to_all x2 -> x1, blocking collectives: 158 us -> 75.4 us  [exchange(): return lax.all_to_all(value, AXES, split_axis=0, concat_axis=0, tiled=True)]
    pallas_call x2, Pallas kernels: 42.7 us -> 35.6 us  [the longest x1 18 us: steps(): pl.pallas_call(serve1_body(*facts(1), peers), grid=grid, in_specs=[pl.Blo...]
    all_to_all x2, starting transfers between devices: 18.5 us -> 23.9 us  [exchange(): return lax.all_to_all(value, AXES, split_axis=0, concat_axis=0, tiled=True)]
  transfers between devices with their start and end apart: 6 -> 6, of which waited for: 2 -> 5; matrix products, arithmetic and copies ran while one was open for 9% -> 9% of each run, Pallas kernels for 5% -> 5%
where the time goes in v4:
time: 418 us
  waiting for transfers between devices  207 us (50%)
  blocking collectives  75.4 us (18%)
  Pallas kernels  55.5 us (13%)
  starting transfers between devices  42.4 us (10%)
  other arithmetic  19.1 us (5%)
  local copies, waits for them, and re-layouts  18.2 us (4%)
    all_to_all x2, waiting for transfers between devices, exchange(): return lax.all_to_all(value, AXES, split_axis=0, concat_axis=0, tiled=True)  103 us
    ppermute x2, waiting for transfers between devices, swapped(): lax.ppermute(upward, axis, forward)  98.1 us
    all_to_all x1, blocking collectives, exchange(): return lax.all_to_all(value, AXES, split_axis=0, concat_axis=0, tiled=True)  75.4 us
    all_to_all x2, starting transfers between devices, exchange(): return lax.all_to_all(value, AXES, split_axis=0, concat_axis=0, tiled=True)  23.9 us
    pallas_call x1, Pallas kernels, steps(): pl.pallas_call(serve1_body(*facts(1), peers), grid=grid, in_specs=[pl.Blo...  18 us
    pallas_call x1, Pallas kernels, steps(): pl.pallas_call(serve0_body(*facts(0)), grid_spec=pltpu.PrefetchScalarGrid...  17.6 us
    ppermute x2, starting transfers between devices, swapped(): lax.ppermute(upward, axis, forward)  14.3 us
    reduce_sum x1, other arithmetic, pool_level(): return jnp.mean(pooled, axis=(2, 4)).astype(jnp.bfloat16)  10.6 us
  transfers between devices with their start and end apart: 6, of which 5 were waited for; matrix products, arithmetic and copies ran while one was open for 9% of the time, Pallas kernels for 5%

profile of v4, /device:TPU:1, one launch (start us, length us, event | category | flops | bytes accessed | tf_op | source)
XLA Modules:
  0.0 417.6 jit_solution(14544308213261310473)
XLA Ops:
  0.0 7.5 %build1.1 = (bf16[128,17,8,256]{3,2,1,0:T(8,128)(2,1)}, s32[128]{0:T(128)}) custom-call(s32[2,1,64]{2,1,0:T(1,128)} %bitcast.56, s32[2,64]{1,0:T(2,128)} %tile.1, bf16[64,8,8,256]{3,2,1,0:T(8,128)(2,1)} %bitcast.53), custom_call_target="tpu_custom_call" | custom-call | tf_op jit(solution)/shard_map/build1/pallas_call | solution.py:310
  7.5 11.9 %all-to-all-start = ((bf16[128,136,256]{2,1,0:T(8,128)(2,1)}), bf16[128,136,256]{2,1,0:T(8,128)(2,1)}, u32[]{:S(2)}, u32[]{:S(2)}) async-start(bf16[128,136,256]{2,1,0:T(8,128)(2,1)} %bitcast.52), calls=%async_computation | async-start | bytes 17825792 | tf_op jit(solution)/shard_map/all_to_all | solution.py:337
  19.4 4.5 %build0.1 = bf16[128,16,8,256]{3,2,1,0:T(8,128)(2,1)} custom-call(s32[128]{0:T(128)} %get-tuple-element.9.slots, bf16[64,8,8,256]{3,2,1,0:T(8,128)(2,1)} %bitcast.54), custom_call_target="tpu_custom_call" | custom-call | tf_op jit(solution)/shard_map/build0/pallas_call | solution.py:327
  23.9 102.7 %all-to-all-done.notes.queries = bf16[128,136,256]{2,1,0:T(8,128)(2,1)} async-done(((bf16[128,136,256]{2,1,0:T(8,128)(2,1)}), bf16[128,136,256]{2,1,0:T(8,128)(2,1)}, u32[]{:S(2)}, u32[]{:S(2)}) %all-to-all-start) | async-done | bytes 8912928 | tf_op jit(solution)/shard_map/all_to_all | solution.py:337
  126.6 0.0 copy-start.1
  126.6 12.0 %all-to-all-start.1 = ((bf16[128,128,256]{2,1,0:T(8,128)(2,1)}), bf16[128,128,256]{2,1,0:T(8,128)(2,1)}, u32[]{:S(2)}, u32[]{:S(2)}) async-start(bf16[128,128,256]{2,1,0:T(8,128)(2,1)} %bitcast.51), calls=%async_computation.1 | async-start | bytes 16777216 | tf_op jit(solution)/shard_map/all_to_all | solution.py:337
  138.6 0.0 copy-done.1
  138.6 0.0 copy-start.2
  138.6 0.1 fusion.11
  138.7 3.4 collective-permute-start
  142.1 1.3 collective-permute-start.1
  143.5 96.9 %collective-permute-done = bf16[2,8,64,256]{3,2,1,0:T(8,128)(2,1)S(1)} collective-permute-done((bf16[2,8,64,256]{3,2,1,0:T(8,128)(2,1)S(1)}, bf16[2,8,64,256]{3,2,1,0:T(8,128)(2,1)S(1)}, u32[]{:S(2)}, u32[]{:S(2)}) %collective-permute-start) | collective-permute-done | bytes 524320 | tf_op jit(solution)/shard_map/ppermute | solution.py:31
  240.4 2.9 collective-permute-done.1
  243.3 0.1 pad_maximum_fusion.4
  243.4 2.9 collective-permute-start.3
  246.3 0.1 pad_maximum_fusion.3
  246.3 10.9 %collective-permute-start.2 = (bf16[2,48,8,256]{3,2,1,0:T(8,128)(2,1)S(1)}, bf16[2,48,8,256]{3,2,1,0:T(8,128)(2,1)S(1)}, u32[]{:S(2)}, u32[]{:S(2)}) collective-permute-start(bf16[2,48,8,256]{3,2,1,0:T(8,128)(2,1)S(1)} %pad_maximum_fusion.3), channel_id=1, source_target_pairs={{0,1},{1,2},{2,3},{3,4},{4,5},{5,6},{6,7},{8,9},{9,10},{10,11},{11... | collective-permute-start | bytes 1179656 | tf_op jit(solution)/shard_map/ppermute | solution.py:31
  257.3 0.0 copy-done.2
  257.3 0.1 constant_dynamic-update-slice_fusion.1
  257.5 3.0 collective-permute-done.3
  260.5 1.2 collective-permute-done.2
  261.7 0.0 copy-start.3
  261.7 0.7 copy-done.3
  262.5 3.6 maximum_convert_fusion
  266.0 9.9 %reshape.24 = f32[2,24,2,40,2,256]{5,4,3,2,1,0:T(2,128)} reshape(f32[2,48,80,256]{3,2,1,0:T(8,128)} %maximum_convert_fusion) | data formatting | bytes 15728640 | tf_op jit(solution)/shard_map/convert_element_type | solution.py:41
  276.0 10.6 %reduce_sum.9 = f32[2,24,40,256]{3,2,1,0:T(8,128)} reduce(f32[2,24,2,40,2,256]{5,4,3,2,1,0:T(2,128)} %reshape.24, f32[]{:T(128)} %constant.1.clone.1), dimensions={2,4}, to_apply=%region_0.0 | reduce | flops 1474560 | bytes 9830404 | tf_op jit(solution)/shard_map/reduce_sum | solution.py:44
  286.6 2.1 fusion.9
  288.7 1.2 fusion.7
  289.9 1.2 fusion.6
  291.0 1.2 fusion.5
  292.2 1.2 fusion.4
  293.4 0.0 copy-start
  293.4 1.2 fusion.3
  294.6 1.1 fusion.2
  295.7 1.2 fusion.1
  297.0 0.0 copy-done
  297.0 0.2 multiply_convert_fusion
  297.1 0.2 slice_bitcast_fusion.9
  297.3 1.3 pad_maximum_fusion
  298.6 18.0 %serve1.1 = (s16[128,88,128]{2,1,0:T(8,128)(2,1)}, s32[256]{0:T(256)}) custom-call(bf16[128,136,256]{2,1,0:T(8,128)(2,1)} %all-to-all-done.notes.queries, bf16[128,136,256]{2,1,0:T(8,128)(2,1)} %all-to-all-done.notes.queries, bf16[192,16,256]{2,1,0:T(8,128)(2,1)} %bitcast.55), custom_call_target="tpu_custom_call" | custom-call | tf_op jit(solution)/shard_map/serve1/pallas_call | solution.py:366
  316.6 0.0 all-to-all-done.1.queries
  316.7 17.6 %serve0.1 = s16[128,168,128]{2,1,0:T(8,128)(2,1)} custom-call(s32[256]{0:T(256)} %get-tuple-element.11.labels, bf16[128,128,256]{2,1,0:T(8,128)(2,1)} %all-to-all-done.1.queries, bf16[640,16,256]{2,1,0:T(8,128)(2,1)} %bitcast.18.strips, s16[128,88,128]{2,1,0:T(8,128)(2,1)} %get-tuple-element.12.part), custom_call_target="tpu_custom_call" | custom-call | tf_op jit(solution)/shard_map/serve0/pallas_call | solution.py:387
  334.3 75.4 %all_to_all.15.reply = s16[128,168,128]{2,1,0:T(8,128)(2,1)} all-to-all(s16[128,168,128]{2,1,0:T(8,128)(2,1)} %serve0.1), channel_id=1, replica_groups=mesh['rows'=16,'cols'=8] {'rows','cols'}, dimensions={0} | all-to-all | bytes 11010048 | tf_op jit(solution)/shard_map/all_to_all | solution.py:337
  409.7 8.0 %finish.1 = f32[81,2,4096]{2,1,0:T(2,128)} custom-call(s32[128]{0:T(128)} %get-tuple-element.9.slots, s16[128,168,128]{2,1,0:T(8,128)(2,1)} %all_to_all.15.reply), custom_call_target="tpu_custom_call" | custom-call | tf_op jit(solution)/shard_map/finish/pallas_call | solution.py:406
  (5 shorter events, 0.1 us)
Async XLA Ops:
  7.5 119.1 %all-to-all-start = ((bf16[128,136,256]{2,1,0:T(8,128)(2,1)}), bf16[128,136,256]{2,1,0:T(8,128)(2,1)}, u32[]{:S(2)}, u32[]{:S(2)}) async-start(bf16[128,136,256]{2,1,0:T(8,128)(2,1)} %bitcast.52), calls=%async_computation | async-start | bytes 17825792 | tf_op jit(solution)/shard_map/all_to_all | solution.py:337
  126.6 12.0 %copy-start.1 = (bf16[2,32,64,256]{3,2,1,0:T(8,128)(2,1)S(1)}, bf16[2,32,64,256]{3,2,1,0:T(8,128)(2,1)}, u32[]{:S(2)}) copy-start(bf16[2,32,64,256]{3,2,1,0:T(8,128)(2,1)} %param.5) | copy-start | bytes 6291460
  126.6 190.1 %all-to-all-start.1 = ((bf16[128,128,256]{2,1,0:T(8,128)(2,1)}), bf16[128,128,256]{2,1,0:T(8,128)(2,1)}, u32[]{:S(2)}, u32[]{:S(2)}) async-start(bf16[128,128,256]{2,1,0:T(8,128)(2,1)} %bitcast.51), calls=%async_computation.1 | async-start | bytes 16777216 | tf_op jit(solution)/shard_map/all_to_all | solution.py:337
  138.6 118.7 %copy-start.2 = (bf16[2,32,64,256]{3,2,1,0:T(8,128)(2,1)S(1)}, bf16[2,32,64,256]{3,2,1,0:T(8,128)(2,1)}, u32[]{:S(2)}) copy-start(bf16[2,32,64,256]{3,2,1,0:T(8,128)(2,1)} %param.5) | copy-start | bytes 6291460
  138.7 101.7 %collective-permute-start = (bf16[2,8,64,256]{3,2,1,0:T(8,128)(2,1)S(1)}, bf16[2,8,64,256]{3,2,1,0:T(8,128)(2,1)S(1)}, u32[]{:S(2)}, u32[]{:S(2)}) collective-permute-start(bf16[2,8,64,256]{3,2,1,0:T(8,128)(2,1)S(1)} %get-tuple-element.15), channel_id=1, source_target_pairs={{0,8},{8,16},{16,24},{24,32},{32,40},{40,48},{48,56},{56,64},{64,7... | collective-permute-start | bytes 1572872 | tf_op jit(solution)/shard_map/ppermute | solution.py:31
  142.1 101.2 %collective-permute-start.1 = (bf16[2,8,64,256]{3,2,1,0:T(8,128)(2,1)S(1)}, bf16[2,8,64,256]{3,2,1,0:T(8,128)(2,1)S(1)}, u32[]{:S(2)}, u32[]{:S(2)}) collective-permute-start(bf16[2,8,64,256]{3,2,1,0:T(8,128)(2,1)S(1)} %get-tuple-element.16), channel_id=1, source_target_pairs={{8,0},{16,8},{24,16},{32,24},{40,32},{48,40},{56,48},{64,56},{72,6... | collective-permute-start | bytes 1572872 | tf_op jit(solution)/shard_map/ppermute | solution.py:31
  243.4 17.1 %collective-permute-start.3 = (bf16[2,48,8,256]{3,2,1,0:T(8,128)(2,1)S(1)}, bf16[2,48,8,256]{3,2,1,0:T(8,128)(2,1)S(1)}, u32[]{:S(2)}, u32[]{:S(2)}) collective-permute-start(bf16[2,48,8,256]{3,2,1,0:T(8,128)(2,1)S(1)} %pad_maximum_fusion.4), channel_id=1, source_target_pairs={{1,0},{2,1},{3,2},{4,3},{5,4},{6,5},{7,6},{9,8},{10,9},{11,10},{12... | collective-permute-start | bytes 1179656 | tf_op jit(solution)/shard_map/ppermute | solution.py:31
  246.3 15.4 %collective-permute-start.2 = (bf16[2,48,8,256]{3,2,1,0:T(8,128)(2,1)S(1)}, bf16[2,48,8,256]{3,2,1,0:T(8,128)(2,1)S(1)}, u32[]{:S(2)}, u32[]{:S(2)}) collective-permute-start(bf16[2,48,8,256]{3,2,1,0:T(8,128)(2,1)S(1)} %pad_maximum_fusion.3), channel_id=1, source_target_pairs={{0,1},{1,2},{2,3},{3,4},{4,5},{5,6},{6,7},{8,9},{9,10},{10,11},{11... | collective-permute-start | bytes 1179656 | tf_op jit(solution)/shard_map/ppermute | solution.py:31
  261.7 0.7 copy-start.3
  293.4 3.6 copy-start

commit v5 on v4

--- a/solution.py
+++ b/solution.py
@@ -8,6 +8,8 @@
 
 RADIUS = 4
 LEVELS = 2
+EARLY = 0
+LATE = 1
 SIDE = 2 * RADIUS
 SPAN = 4 * RADIUS
 WIN = 2 * RADIUS + 1
@@ -18,7 +20,7 @@
 PART_ROWS = 88
 EARLY_ROWS = 80
 REPLY_ROWS = EARLY_ROWS + PART_ROWS
-PEERS_A_STEP = 16
+PEERS_A_STEP = 32
 BENCHES = 8
 FULL = 32767.0
 AXES = ("rows", "cols")
@@ -68,8 +70,6 @@
 
 
 def first_body(peers, blocks, tiles_of, per_frame, across, band_rows):
-    last = LEVELS - 1
-
     def kernel(owner, tile, fmap, send, slots, count, labels, notes, sems, note_sem):
         copy = tile_copy(fmap, send, sems, per_frame, across, band_rows)
 
@@ -77,16 +77,16 @@
             count[i] = 0
             return carry
 
-        lax.fori_loop(0, LEVELS * peers, clear, 0, unroll=8)
+        lax.fori_loop(0, LEVELS * peers, clear, 0, unroll=32)
 
         def blank(i, carry):
             labels[i] = 0
             return carry
 
-        lax.fori_loop(0, LEVELS * SLOTS * peers, blank, 0, unroll=8)
+        lax.fori_loop(0, LEVELS * SLOTS * peers, blank, 0, unroll=32)
 
         def place(k, carry):
-            for level in reversed(range(LEVELS)):
+            for level in (EARLY, LATE):
                 own = owner[level, 0, k]
                 seen = count[level * peers + own]
                 count[level * peers + own] = seen + 1
@@ -95,11 +95,11 @@
                 labels[level * SLOTS * peers + slot] = k // per_frame * tiles_of[level] + lax.rem(
                     tile[level, k], tiles_of[level]
                 )
-                if level == last:
+                if level == EARLY:
                     copy(k, slot).start()
             return carry
 
-        lax.fori_loop(0, blocks, place, 0)
+        lax.fori_loop(0, blocks, place, 0, unroll=4)
 
         lane = lax.broadcasted_iota(jnp.int32, notes.shape[1:], 1)
 
@@ -112,15 +112,15 @@
             notes[peer] = values.astype(jnp.float32).astype(jnp.bfloat16)
             return carry
 
-        lax.fori_loop(0, peers, note, 0, unroll=4)
+        lax.fori_loop(0, peers, note, 0, unroll=8)
         noted = pltpu.make_async_copy(notes, send.at[:, SLOTS * SIDE], note_sem)
         noted.start()
 
         def finish(k, carry):
-            copy(k, slots[last * blocks + k]).wait()
-            return carry
-
-        lax.fori_loop(0, blocks, finish, 0)
+            copy(k, slots[EARLY * blocks + k]).wait()
+            return carry
+
+        lax.fori_loop(0, blocks, finish, 0, unroll=8)
         noted.wait()
 
     return kernel
@@ -131,15 +131,15 @@
         copy = tile_copy(fmap, send, sems, per_frame, across, band_rows)
 
         def place(k, carry):
-            copy(k, slots[k]).start()
+            copy(k, slots[LATE * blocks + k]).start()
             return carry
 
         def finish(k, carry):
-            copy(k, slots[k]).wait()
-            return carry
-
-        lax.fori_loop(0, blocks, place, 0)
-        lax.fori_loop(0, blocks, finish, 0)
+            copy(k, slots[LATE * blocks + k]).wait()
+            return carry
+
+        lax.fori_loop(0, blocks, place, 0, unroll=4)
+        lax.fori_loop(0, blocks, finish, 0, unroll=8)
 
     return kernel
 
@@ -202,7 +202,7 @@
     return run
 
 
-def serve1_body(rows, across, tiles, frames, peers):
+def early_body(rows, across, tiles, frames, peers):
     def kernel(notes, queries, strips, part, others, flat, lines, labels, sem):
         step = pl.program_id(0)
 
@@ -222,7 +222,7 @@
 
             def other(peer, carry):
                 for slot in range(SLOTS):
-                    others[peer * SLOTS + slot] = labels[peer, slot]
+                    others[peer * SLOTS + slot] = labels[peer, LATE * SLOTS + slot]
                 return carry
 
             lax.fori_loop(0, peers, other, 0, unroll=4)
@@ -230,13 +230,13 @@
         def store(peer, row_id, coded):
             part[peer] = coded.astype(jnp.int16)
 
-        run = serve_body(rows, across, tiles, frames, lambda p, slot: labels[p, SLOTS + slot])
+        run = serve_body(rows, across, tiles, frames, lambda p, slot: labels[p, EARLY * SLOTS + slot])
         run(step, queries, strips, flat, store)
 
     return kernel
 
 
-def serve0_body(rows, across, tiles, frames):
+def late_body(rows, across, tiles, frames):
     def kernel(labels, queries, strips, part, reply, flat):
         step = pl.program_id(0)
 
@@ -277,15 +277,16 @@
         for group in range(groups):
             k = (step * groups + group) * 2
             lanes = slice(group * LANES, (group + 1) * LANES)
-            late = joined([slots[k], slots[k + 1]], EARLY_ROWS, REPLY_ROWS)
-            out[:, 0, lanes] = late[:WINDOW] * unit(late[WINDOW : WINDOW + 1])
-            slot = [slots[blocks + k], slots[blocks + k + 1]]
+            slot = [slots[LATE * blocks + k + side] for side in range(2)]
+            late = joined(slot, EARLY_ROWS, REPLY_ROWS)
+            out[:, LATE, lanes] = late[:WINDOW] * unit(late[WINDOW : WINDOW + 1])
+            slot = [slots[EARLY * blocks + k + side] for side in range(2)]
             early = joined(slot, 0, EARLY_ROWS)
             last = joined(slot, REPLY_ROWS - 8, REPLY_ROWS)
             at = WINDOW - EARLY_ROWS
             factor = unit(last[at + 2 : at + 3])
-            out[:EARLY_ROWS, 1, lanes] = early * factor
-            out[EARLY_ROWS:, 1, lanes] = last[at + 1 : at + 2] * factor
+            out[:EARLY_ROWS, EARLY, lanes] = early * factor
+            out[EARLY_ROWS:, EARLY, lanes] = last[at + 1 : at + 2] * factor
 
     return kernel
 
@@ -307,7 +308,7 @@
     def send_shape(parts):
         return jax.ShapeDtypeStruct((peers, parts, SIDE, channels), jnp.bfloat16)
 
-    send1, slots = pl.pallas_call(
+    send_a, slots = pl.pallas_call(
         first_body(peers, blocks, tiles_of, per_frame, across, band_rows),
         in_specs=[smem, smem, vmem],
         out_specs=[hbm, smem],
@@ -322,21 +323,21 @@
             pltpu.SemaphoreType.DMA((blocks,)),
             pltpu.SemaphoreType.DMA,
         ],
-        name="build1",
+        name="build_a",
     )(target_owner.transpose(0, 2, 1), target_tile, tiles)
-    send0 = pl.pallas_call(
+    send_b = pl.pallas_call(
         second_body(blocks, per_frame, across, band_rows),
         in_specs=[smem, vmem],
         out_specs=hbm,
         out_shape=send_shape(SLOTS * SIDE),
         scratch_shapes=[pltpu.SemaphoreType.DMA((blocks,))],
-        name="build0",
+        name="build_b",
     )(slots, tiles)
 
     def exchange(value):
         return lax.all_to_all(value, AXES, split_axis=0, concat_axis=0, tiled=True)
 
-    arrived = [exchange(send.reshape(peers, -1, channels)) for send in (send0, send1)]
+    arrived = [exchange(send.reshape(peers, -1, channels)) for send in (send_a, send_b)]
 
     low, high = neighbours(fmap2, "rows", 1, SIDE)
     edges = [
@@ -363,13 +364,13 @@
     def strip_block(level):
         return pl.BlockSpec(strips[level].shape, lambda s, *_: (0, 0, 0))
 
-    part, labels0 = pl.pallas_call(
-        serve1_body(*facts(1), peers),
+    part, labels = pl.pallas_call(
+        early_body(*facts(EARLY), peers),
         grid=grid,
         in_specs=[
             pl.BlockSpec((peers, SIDE, channels), lambda s: (0, LANES // SIDE, 0)),
             query_block,
-            strip_block(1),
+            strip_block(EARLY),
         ],
         out_specs=[part_block, smem],
         out_shape=[
@@ -382,25 +383,25 @@
             pltpu.SMEM((peers, 128), jnp.int32),
             pltpu.SemaphoreType.DMA,
         ],
-        name="serve1",
-    )(arrived[1], arrived[1], strips[1])
+        name="serve_a",
+    )(arrived[0], arrived[0], strips[EARLY])
     served = pl.pallas_call(
-        serve0_body(*facts(0)),
+        late_body(*facts(LATE)),
         grid_spec=pltpu.PrefetchScalarGridSpec(
             num_scalar_prefetch=1,
             grid=grid,
-            in_specs=[query_block, strip_block(0), part_block],
+            in_specs=[query_block, strip_block(LATE), part_block],
             out_specs=pl.BlockSpec(
                 (PEERS_A_STEP, REPLY_ROWS, LANES), lambda s, *_: (s, 0, 0)
             ),
             scratch_shapes=[flat],
         ),
         out_shape=jax.ShapeDtypeStruct((peers, REPLY_ROWS, LANES), jnp.int16),
-        name="serve0",
-    )(labels0, arrived[0], strips[0], part)
+        name="serve_b",
+    )(labels, arrived[1], strips[LATE], part)
     reply = exchange(served)
 
-    groups = 4
+    groups = 8
     width = groups * LANES
     whole = pl.BlockSpec((peers, REPLY_ROWS, LANES), lambda s, _: (0, 0, 0))
     out = pl.pallas_call(

time: 418 us -> 410 us (0.981)
  local copies, waits for them, and re-layouts: 18.2 us -> 13.4 us
    ppermute x2, waiting for transfers between devices: 5.94 us -> 104 us  [swapped(): lax.ppermute(downward, axis, backward)]
    ppermute x2, waiting for transfers between devices: 98.1 us -> 2.29 us  [swapped(): lax.ppermute(upward, axis, forward)]
    unnamed x16 -> x18, local copies, waits for them, and re-layouts: 7.95 us -> 3.17 us
  transfers between devices with their start and end apart: 6 -> 6, of which waited for: 5 -> 4; matrix products, arithmetic and copies ran while one was open for 9% -> 7% of each run, Pallas kernels for 5% -> 6%
where the time goes in v5:
time: 410 us
  waiting for transfers between devices  209 us (51%)
  blocking collectives  72 us (18%)
  Pallas kernels  54.3 us (13%)
  starting transfers between devices  43.1 us (11%)
  other arithmetic  17.8 us (4%)
  local copies, waits for them, and re-layouts  13.4 us (3%)
    ppermute x2, waiting for transfers between devices, swapped(): lax.ppermute(downward, axis, backward)  104 us
    all_to_all x2, waiting for transfers between devices, exchange(): return lax.all_to_all(value, AXES, split_axis=0, concat_axis=0, tiled=True)  103 us
    all_to_all x1, blocking collectives, exchange(): return lax.all_to_all(value, AXES, split_axis=0, concat_axis=0, tiled=True)  72 us
    all_to_all x2, starting transfers between devices, exchange(): return lax.all_to_all(value, AXES, split_axis=0, concat_axis=0, tiled=True)  23.9 us
    pallas_call x1, Pallas kernels, steps(): pl.pallas_call(early_body(*facts(EARLY), peers), grid=grid, in_specs=[pl....  19.3 us
    pallas_call x1, Pallas kernels, steps(): pl.pallas_call(late_body(*facts(LATE)), grid_spec=pltpu.PrefetchScalarGri...  17.1 us
    ppermute x2, starting transfers between devices, swapped(): lax.ppermute(upward, axis, forward)  15.7 us
    reduce_sum x1, other arithmetic, pool_level(): return jnp.mean(pooled, axis=(2, 4)).astype(jnp.bfloat16)  10.6 us
  transfers between devices with their start and end apart: 6, of which 4 were waited for; matrix products, arithmetic and copies ran while one was open for 7% of the time, Pallas kernels for 6%

profile of v5, /device:TPU:1, one launch (start us, length us, event | category | flops | bytes accessed | tf_op | source)
XLA Modules:
  0.0 409.6 jit_solution(15210892868837071047)
XLA Ops:
  0.0 6.6 %build_a.1 = (bf16[128,17,8,256]{3,2,1,0:T(8,128)(2,1)}, s32[128]{0:T(128)}) custom-call(s32[2,1,64]{2,1,0:T(1,128)} %bitcast.57, s32[2,64]{1,0:T(2,128)} %tile.1, bf16[64,8,8,256]{3,2,1,0:T(8,128)(2,1)} %bitcast.53), custom_call_target="tpu_custom_call" | custom-call | tf_op jit(solution)/shard_map/build_a/pallas_call | solution.py:311
  6.6 11.9 %all-to-all-start = ((bf16[128,136,256]{2,1,0:T(8,128)(2,1)}), bf16[128,136,256]{2,1,0:T(8,128)(2,1)}, u32[]{:S(2)}, u32[]{:S(2)}) async-start(bf16[128,136,256]{2,1,0:T(8,128)(2,1)} %bitcast.52), calls=%async_computation | async-start | bytes 17825792 | tf_op jit(solution)/shard_map/all_to_all | solution.py:338
  18.5 4.2 %build_b.1 = bf16[128,16,8,256]{3,2,1,0:T(8,128)(2,1)} custom-call(s32[128]{0:T(128)} %get-tuple-element.9.slots, bf16[64,8,8,256]{3,2,1,0:T(8,128)(2,1)} %bitcast.54), custom_call_target="tpu_custom_call" | custom-call | tf_op jit(solution)/shard_map/build_b/pallas_call | solution.py:328
  22.7 103.0 %all-to-all-done.notes.queries = bf16[128,136,256]{2,1,0:T(8,128)(2,1)} async-done(((bf16[128,136,256]{2,1,0:T(8,128)(2,1)}), bf16[128,136,256]{2,1,0:T(8,128)(2,1)}, u32[]{:S(2)}, u32[]{:S(2)}) %all-to-all-start) | async-done | bytes 8912928 | tf_op jit(solution)/shard_map/all_to_all | solution.py:338
  125.7 0.0 copy-start.2
  125.7 12.0 %all-to-all-start.1 = ((bf16[128,128,256]{2,1,0:T(8,128)(2,1)}), bf16[128,128,256]{2,1,0:T(8,128)(2,1)}, u32[]{:S(2)}, u32[]{:S(2)}) async-start(bf16[128,128,256]{2,1,0:T(8,128)(2,1)} %bitcast.51), calls=%async_computation.1 | async-start | bytes 16777216 | tf_op jit(solution)/shard_map/all_to_all | solution.py:338
  137.7 0.0 copy-done.2
  137.7 0.0 copy-start.3
  137.7 0.1 fusion.11
  137.8 1.4 collective-permute-start.1
  139.3 4.0 collective-permute-start
  143.3 99.1 %collective-permute-done.1 = bf16[2,8,64,256]{3,2,1,0:T(8,128)(2,1)S(1)} collective-permute-done((bf16[2,8,64,256]{3,2,1,0:T(8,128)(2,1)S(1)}, bf16[2,8,64,256]{3,2,1,0:T(8,128)(2,1)S(1)}, u32[]{:S(2)}, u32[]{:S(2)}) %collective-permute-start.1) | collective-permute-done | bytes 524320 | tf_op jit(solution)/shard_map/ppermute | solution.py:33
  242.4 0.0 collective-permute-done
  242.5 0.1 pad_maximum_fusion.3
  242.5 11.7 %collective-permute-start.2 = (bf16[2,48,8,256]{3,2,1,0:T(8,128)(2,1)S(1)}, bf16[2,48,8,256]{3,2,1,0:T(8,128)(2,1)S(1)}, u32[]{:S(2)}, u32[]{:S(2)}) collective-permute-start(bf16[2,48,8,256]{3,2,1,0:T(8,128)(2,1)S(1)} %pad_maximum_fusion.3), channel_id=1, source_target_pairs={{0,1},{1,2},{2,3},{3,4},{4,5},{5,6},{6,7},{8,9},{9,10},{10,11},{11... | collective-permute-start | bytes 1179656 | tf_op jit(solution)/shard_map/ppermute | solution.py:33
  254.2 0.1 pad_maximum_fusion.4
  254.3 2.1 collective-permute-start.3
  256.4 0.0 copy-done.3
  256.4 0.1 constant_dynamic-update-slice_fusion.1
  256.6 2.3 collective-permute-done.2
  258.9 0.0 copy-start.4
  258.9 4.5 %collective-permute-done.3 = bf16[2,48,8,256]{3,2,1,0:T(8,128)(2,1)S(1)} collective-permute-done((bf16[2,48,8,256]{3,2,1,0:T(8,128)(2,1)S(1)}, bf16[2,48,8,256]{3,2,1,0:T(8,128)(2,1)S(1)}, u32[]{:S(2)}, u32[]{:S(2)}) %collective-permute-start.3) | collective-permute-done | bytes 393248 | tf_op jit(solution)/shard_map/ppermute | solution.py:33
  263.4 0.0 copy-done.4
  263.4 3.5 maximum_convert_fusion
  266.9 9.9 %reshape.24 = f32[2,24,2,40,2,256]{5,4,3,2,1,0:T(2,128)} reshape(f32[2,48,80,256]{3,2,1,0:T(8,128)} %maximum_convert_fusion) | data formatting | bytes 15728640 | tf_op jit(solution)/shard_map/convert_element_type | solution.py:43
  276.8 10.6 %reduce_sum.9 = f32[2,24,40,256]{3,2,1,0:T(8,128)} reduce(f32[2,24,2,40,2,256]{5,4,3,2,1,0:T(2,128)} %reshape.24, f32[]{:T(128)} %constant.1.clone.1), dimensions={2,4}, to_apply=%region_0.0 | reduce | flops 1474560 | bytes 9830404 | tf_op jit(solution)/shard_map/reduce_sum | solution.py:46
  287.5 1.2 fusion.9
  288.7 0.3 fusion.7
  289.0 0.3 fusion.6
  289.3 0.3 fusion.5
  289.5 0.3 fusion.4
  289.8 0.0 copy-start
  289.8 0.3 fusion.3
  290.1 0.3 fusion.2
  290.4 0.4 fusion.1
  290.8 0.6 copy-done
  291.4 0.0 copy-start.1
  291.4 0.2 multiply_convert_fusion
  291.6 0.2 slice_bitcast_fusion.9
  291.7 1.7 pad_maximum_fusion
  293.4 0.7 copy-done.1
  294.2 19.3 %serve_a.1 = (s16[128,88,128]{2,1,0:T(8,128)(2,1)}, s32[256]{0:T(256)}) custom-call(bf16[128,136,256]{2,1,0:T(8,128)(2,1)} %all-to-all-done.notes.queries, bf16[128,136,256]{2,1,0:T(8,128)(2,1)} %all-to-all-done.notes.queries, bf16[640,16,256]{2,1,0:T(8,128)(2,1)} %bitcast.55), custom_call_target="tpu_custom_call" | custom-call | tf_op jit(solution)/shard_map/serve_a/pallas_call | solution.py:367
  313.5 0.0 all-to-all-done.1.queries
  313.5 17.1 %serve_b.1 = s16[128,168,128]{2,1,0:T(8,128)(2,1)} custom-call(s32[256]{0:T(256)} %get-tuple-element.11.labels, bf16[128,128,256]{2,1,0:T(8,128)(2,1)} %all-to-all-done.1.queries, bf16[192,16,256]{2,1,0:T(8,128)(2,1)} %bitcast.56, s16[128,88,128]{2,1,0:T(8,128)(2,1)} %get-tuple-element.12.part), custom_call_target="tpu_custom_call" | custom-call | tf_op jit(solution)/shard_map/serve_b/pallas_call | solution.py:388
  330.6 72.0 %all_to_all.15.reply = s16[128,168,128]{2,1,0:T(8,128)(2,1)} all-to-all(s16[128,168,128]{2,1,0:T(8,128)(2,1)} %serve_b.1), channel_id=1, replica_groups=mesh['rows'=16,'cols'=8] {'rows','cols'}, dimensions={0} | all-to-all | bytes 11010048 | tf_op jit(solution)/shard_map/all_to_all | solution.py:338
  402.5 7.1 %finish.1 = f32[81,2,4096]{2,1,0:T(2,128)} custom-call(s32[128]{0:T(128)} %get-tuple-element.9.slots, s16[128,168,128]{2,1,0:T(8,128)(2,1)} %all_to_all.15.reply), custom_call_target="tpu_custom_call" | custom-call | tf_op jit(solution)/shard_map/finish/pallas_call | solution.py:407
  (5 shorter events, 0.1 us)
Async XLA Ops:
  6.6 119.1 %all-to-all-start = ((bf16[128,136,256]{2,1,0:T(8,128)(2,1)}), bf16[128,136,256]{2,1,0:T(8,128)(2,1)}, u32[]{:S(2)}, u32[]{:S(2)}) async-start(bf16[128,136,256]{2,1,0:T(8,128)(2,1)} %bitcast.52), calls=%async_computation | async-start | bytes 17825792 | tf_op jit(solution)/shard_map/all_to_all | solution.py:338
  125.7 12.0 %copy-start.2 = (bf16[2,32,64,256]{3,2,1,0:T(8,128)(2,1)S(1)}, bf16[2,32,64,256]{3,2,1,0:T(8,128)(2,1)}, u32[]{:S(2)}) copy-start(bf16[2,32,64,256]{3,2,1,0:T(8,128)(2,1)} %param.5) | copy-start | bytes 6291460
  125.7 187.8 %all-to-all-start.1 = ((bf16[128,128,256]{2,1,0:T(8,128)(2,1)}), bf16[128,128,256]{2,1,0:T(8,128)(2,1)}, u32[]{:S(2)}, u32[]{:S(2)}) async-start(bf16[128,128,256]{2,1,0:T(8,128)(2,1)} %bitcast.51), calls=%async_computation.1 | async-start | bytes 16777216 | tf_op jit(solution)/shard_map/all_to_all | solution.py:338
  137.7 118.7 %copy-start.3 = (bf16[2,32,64,256]{3,2,1,0:T(8,128)(2,1)S(1)}, bf16[2,32,64,256]{3,2,1,0:T(8,128)(2,1)}, u32[]{:S(2)}) copy-start(bf16[2,32,64,256]{3,2,1,0:T(8,128)(2,1)} %param.5) | copy-start | bytes 6291460
  137.8 104.6 %collective-permute-start.1 = (bf16[2,8,64,256]{3,2,1,0:T(8,128)(2,1)S(1)}, bf16[2,8,64,256]{3,2,1,0:T(8,128)(2,1)S(1)}, u32[]{:S(2)}, u32[]{:S(2)}) collective-permute-start(bf16[2,8,64,256]{3,2,1,0:T(8,128)(2,1)S(1)} %get-tuple-element.15), channel_id=1, source_target_pairs={{8,0},{16,8},{24,16},{32,24},{40,32},{48,40},{56,48},{64,56},{72,6... | collective-permute-start | bytes 1572872 | tf_op jit(solution)/shard_map/ppermute | solution.py:33
  139.3 103.2 %collective-permute-start = (bf16[2,8,64,256]{3,2,1,0:T(8,128)(2,1)S(1)}, bf16[2,8,64,256]{3,2,1,0:T(8,128)(2,1)S(1)}, u32[]{:S(2)}, u32[]{:S(2)}) collective-permute-start(bf16[2,8,64,256]{3,2,1,0:T(8,128)(2,1)S(1)} %get-tuple-element.16), channel_id=1, source_target_pairs={{0,8},{8,16},{16,24},{24,32},{32,40},{40,48},{48,56},{56,64},{64,7... | collective-permute-start | bytes 1572872 | tf_op jit(solution)/shard_map/ppermute | solution.py:33
  242.5 16.4 %collective-permute-start.2 = (bf16[2,48,8,256]{3,2,1,0:T(8,128)(2,1)S(1)}, bf16[2,48,8,256]{3,2,1,0:T(8,128)(2,1)S(1)}, u32[]{:S(2)}, u32[]{:S(2)}) collective-permute-start(bf16[2,48,8,256]{3,2,1,0:T(8,128)(2,1)S(1)} %pad_maximum_fusion.3), channel_id=1, source_target_pairs={{0,1},{1,2},{2,3},{3,4},{4,5},{5,6},{6,7},{8,9},{9,10},{10,11},{11... | collective-permute-start | bytes 1179656 | tf_op jit(solution)/shard_map/ppermute | solution.py:33
  254.3 9.1 %collective-permute-start.3 = (bf16[2,48,8,256]{3,2,1,0:T(8,128)(2,1)S(1)}, bf16[2,48,8,256]{3,2,1,0:T(8,128)(2,1)S(1)}, u32[]{:S(2)}, u32[]{:S(2)}) collective-permute-start(bf16[2,48,8,256]{3,2,1,0:T(8,128)(2,1)S(1)} %pad_maximum_fusion.4), channel_id=1, source_target_pairs={{1,0},{2,1},{3,2},{4,3},{5,4},{6,5},{7,6},{9,8},{10,9},{11,10},{12... | collective-permute-start | bytes 1179656 | tf_op jit(solution)/shard_map/ppermute | solution.py:33
  258.9 4.5 %copy-start.4 = (bf16[2,48,8,256]{3,2,1,0:T(8,128)(2,1)}, bf16[2,48,8,256]{3,2,1,0:T(8,128)(2,1)S(1)}, u32[]{:S(2)}) copy-start(bf16[2,48,8,256]{3,2,1,0:T(8,128)(2,1)S(1)} %collective-permute-done.2) | copy-start | bytes 1179652
  289.8 1.5 copy-start
  291.4 2.8 copy-start.1

commit v6 on v5

--- a/solution.py
+++ b/solution.py
@@ -23,6 +23,9 @@
 PEERS_A_STEP = 32
 BENCHES = 8
 FULL = 32767.0
+MIB = 1 << 20
+SERVE_B_VMEM = 14 * MIB
+FINISH_VMEM = 12 * MIB
 AXES = ("rows", "cols")
 
 
@@ -397,6 +400,7 @@
             scratch_shapes=[flat],
         ),
         out_shape=jax.ShapeDtypeStruct((peers, REPLY_ROWS, LANES), jnp.int16),
+        compiler_params=pltpu.CompilerParams(vmem_limit_bytes=SERVE_B_VMEM),
         name="serve_b",
     )(labels, arrived[1], strips[LATE], part)
     reply = exchange(served)
@@ -413,6 +417,7 @@
             out_specs=pl.BlockSpec((WINDOW, LEVELS, width), lambda s, _: (0, 0, s)),
         ),
         out_shape=jax.ShapeDtypeStruct((WINDOW, LEVELS, blocks * QUERIES), jnp.float32),
+        compiler_params=pltpu.CompilerParams(vmem_limit_bytes=FINISH_VMEM),
         name="finish",
     )(slots, reply)
     return out.transpose(1, 0, 2)

time: 410 us -> 407 us (level)
  Pallas kernels: 54.3 us -> 49.6 us
where the time goes in v6:
time: 407 us
  waiting for transfers between devices  209 us (51%)
  blocking collectives  71.7 us (18%)
  Pallas kernels  49.6 us (12%)
  starting transfers between devices  43.1 us (11%)
  local copies, waits for them, and re-layouts  16.9 us (4%)
  other arithmetic  16.3 us (4%)
    ppermute x2, waiting for transfers between devices, swapped(): lax.ppermute(downward, axis, backward)  104 us
    all_to_all x2, waiting for transfers between devices, exchange(): return lax.all_to_all(value, AXES, split_axis=0, concat_axis=0, tiled=True)  103 us
    all_to_all x1, blocking collectives, exchange(): return lax.all_to_all(value, AXES, split_axis=0, concat_axis=0, tiled=True)  71.7 us
    all_to_all x2, starting transfers between devices, exchange(): return lax.all_to_all(value, AXES, split_axis=0, concat_axis=0, tiled=True)  23.9 us
    pallas_call x1, Pallas kernels, steps(): pl.pallas_call(early_body(*facts(EARLY), peers), grid=grid, in_specs=[pl....  19.3 us
    ppermute x2, starting transfers between devices, swapped(): lax.ppermute(upward, axis, forward)  15.7 us
    pallas_call x1, Pallas kernels, steps(): pl.pallas_call(late_body(*facts(LATE)), grid_spec=pltpu.PrefetchScalarGri...  15.1 us
    reduce_sum x1, other arithmetic, pool_level(): return jnp.mean(pooled, axis=(2, 4)).astype(jnp.bfloat16)  10.6 us
  transfers between devices with their start and end apart: 6, of which 4 were waited for; matrix products, arithmetic and copies ran while one was open for 7% of the time, Pallas kernels for 6%

profile of v6, /device:TPU:1, one launch (start us, length us, event | category | flops | bytes accessed | tf_op | source)
XLA Modules:
  0.0 406.7 jit_solution(16678669410820676010)
XLA Ops:
  0.0 6.6 %build_a.1 = (bf16[128,17,8,256]{3,2,1,0:T(8,128)(2,1)}, s32[128]{0:T(128)}) custom-call(s32[2,1,64]{2,1,0:T(1,128)} %bitcast.57, s32[2,64]{1,0:T(2,128)} %tile.1, bf16[64,8,8,256]{3,2,1,0:T(8,128)(2,1)} %bitcast.54), custom_call_target="tpu_custom_call" | custom-call | tf_op jit(solution)/shard_map/build_a/pallas_call | solution.py:314
  6.6 11.9 %all-to-all-start = ((bf16[128,136,256]{2,1,0:T(8,128)(2,1)}), bf16[128,136,256]{2,1,0:T(8,128)(2,1)}, u32[]{:S(2)}, u32[]{:S(2)}) async-start(bf16[128,136,256]{2,1,0:T(8,128)(2,1)} %bitcast.53), calls=%async_computation | async-start | bytes 17825792 | tf_op jit(solution)/shard_map/all_to_all | solution.py:341
  18.5 4.1 %build_b.1 = bf16[128,16,8,256]{3,2,1,0:T(8,128)(2,1)} custom-call(s32[128]{0:T(128)} %get-tuple-element.9.slots, bf16[64,8,8,256]{3,2,1,0:T(8,128)(2,1)} %bitcast.55), custom_call_target="tpu_custom_call" | custom-call | tf_op jit(solution)/shard_map/build_b/pallas_call | solution.py:331
  22.7 103.0 %all-to-all-done.notes.queries = bf16[128,136,256]{2,1,0:T(8,128)(2,1)} async-done(((bf16[128,136,256]{2,1,0:T(8,128)(2,1)}), bf16[128,136,256]{2,1,0:T(8,128)(2,1)}, u32[]{:S(2)}, u32[]{:S(2)}) %all-to-all-start) | async-done | bytes 8912928 | tf_op jit(solution)/shard_map/all_to_all | solution.py:341
  125.7 12.0 %all-to-all-start.1 = ((bf16[128,128,256]{2,1,0:T(8,128)(2,1)}), bf16[128,128,256]{2,1,0:T(8,128)(2,1)}, u32[]{:S(2)}, u32[]{:S(2)}) async-start(bf16[128,128,256]{2,1,0:T(8,128)(2,1)} %bitcast.52), calls=%async_computation.1 | async-start | bytes 16777216 | tf_op jit(solution)/shard_map/all_to_all | solution.py:341
  137.7 0.0 copy-done.5
  137.7 0.0 copy-start.6
  137.7 0.1 fusion.11
  137.8 1.4 collective-permute-start.1
  139.3 4.0 collective-permute-start
  143.3 99.1 %collective-permute-done.1 = bf16[2,8,64,256]{3,2,1,0:T(8,128)(2,1)S(1)} collective-permute-done((bf16[2,8,64,256]{3,2,1,0:T(8,128)(2,1)S(1)}, bf16[2,8,64,256]{3,2,1,0:T(8,128)(2,1)S(1)}, u32[]{:S(2)}, u32[]{:S(2)}) %collective-permute-start.1) | collective-permute-done | bytes 524320 | tf_op jit(solution)/shard_map/ppermute | solution.py:36
  242.4 0.0 collective-permute-done
  242.5 0.1 pad_maximum_fusion.3
  242.5 11.7 %collective-permute-start.2 = (bf16[2,48,8,256]{3,2,1,0:T(8,128)(2,1)S(1)}, bf16[2,48,8,256]{3,2,1,0:T(8,128)(2,1)S(1)}, u32[]{:S(2)}, u32[]{:S(2)}) collective-permute-start(bf16[2,48,8,256]{3,2,1,0:T(8,128)(2,1)S(1)} %pad_maximum_fusion.3), channel_id=1, source_target_pairs={{0,1},{1,2},{2,3},{3,4},{4,5},{5,6},{6,7},{8,9},{9,10},{10,11},{11... | collective-permute-start | bytes 1179656 | tf_op jit(solution)/shard_map/ppermute | solution.py:36
  254.2 0.1 pad_maximum_fusion.4
  254.3 2.1 collective-permute-start.3
  256.4 0.0 copy-done.6
  256.4 0.1 constant_dynamic-update-slice_fusion.1
  256.6 2.3 collective-permute-done.2
  258.9 4.5 %collective-permute-done.3 = bf16[2,48,8,256]{3,2,1,0:T(8,128)(2,1)S(1)} collective-permute-done((bf16[2,48,8,256]{3,2,1,0:T(8,128)(2,1)S(1)}, bf16[2,48,8,256]{3,2,1,0:T(8,128)(2,1)S(1)}, u32[]{:S(2)}, u32[]{:S(2)}) %collective-permute-start.3) | collective-permute-done | bytes 393248 | tf_op jit(solution)/shard_map/ppermute | solution.py:36
  263.4 0.0 copy-done.7
  263.4 3.5 maximum_convert_fusion
  266.9 9.9 %reshape.24 = f32[2,24,2,40,2,256]{5,4,3,2,1,0:T(2,128)} reshape(f32[2,48,80,256]{3,2,1,0:T(8,128)} %maximum_convert_fusion) | data formatting | bytes 15728640 | tf_op jit(solution)/shard_map/convert_element_type | solution.py:46
  276.8 10.6 %reduce_sum.9 = f32[2,24,40,256]{3,2,1,0:T(8,128)} reduce(f32[2,24,2,40,2,256]{5,4,3,2,1,0:T(2,128)} %reshape.24, f32[]{:T(128)} %constant.1.clone.1), dimensions={2,4}, to_apply=%region_0.0 | reduce | flops 1474560 | bytes 9830404 | tf_op jit(solution)/shard_map/reduce_sum | solution.py:49
  287.5 1.2 fusion.9
  288.7 0.3 fusion.7
  289.0 0.3 fusion.6
  289.3 0.3 fusion.5
  289.5 0.3 fusion.4
  289.8 0.0 copy-start.3
  289.8 0.3 fusion.3
  290.1 0.3 fusion.2
  290.4 0.4 fusion.1
  290.8 0.6 copy-done.3
  291.4 0.2 multiply_convert_fusion
  291.6 0.2 slice_bitcast_fusion.9
  291.7 0.2 pad_maximum_fusion
  291.9 1.7 copy-done.4
  293.7 19.3 %serve_a.1 = (s16[128,88,128]{2,1,0:T(8,128)(2,1)}, s32[256]{0:T(256)}) custom-call(bf16[128,136,256]{2,1,0:T(8,128)(2,1)} %all-to-all-done.notes.queries, bf16[128,136,256]{2,1,0:T(8,128)(2,1)} %all-to-all-done.notes.queries, bf16[640,16,256]{2,1,0:T(8,128)(2,1)} %bitcast.56), custom_call_target="tpu_custom_call" | custom-call | tf_op jit(solution)/shard_map/serve_a/pallas_call | solution.py:370
  313.0 0.0 all-to-all-done.1.queries
  313.0 0.0 copy-start
  313.0 1.8 copy-done
  314.8 0.7 copy-done.2
  315.5 15.1 %serve_b.1 = s16[128,168,128]{2,1,0:T(8,128)(2,1)S(1)} custom-call(s32[256]{0:T(256)S(1)} %copy-done.2, bf16[128,128,256]{2,1,0:T(8,128)(2,1)} %all-to-all-done.1.queries, bf16[192,16,256]{2,1,0:T(8,128)(2,1)S(1)} %bitcast.51, s16[128,88,128]{2,1,0:T(8,128)(2,1)S(1)} %copy-done), custom_call_target="tpu_custom_call" | custom-call | tf_op jit(solution)/shard_map/serve_b/pallas_call | solution.py:391
  330.6 0.0 copy-start.1
  330.6 71.7 %all_to_all.15.reply = s16[128,168,128]{2,1,0:T(8,128)(2,1)S(1)} all-to-all(s16[128,168,128]{2,1,0:T(8,128)(2,1)S(1)} %serve_b.1), channel_id=1, replica_groups=mesh['rows'=16,'cols'=8] {'rows','cols'}, dimensions={0} | all-to-all | bytes 11010048 | tf_op jit(solution)/shard_map/all_to_all | solution.py:341
  402.3 0.0 copy-done.1
  402.3 4.4 %finish.1 = f32[81,2,4096]{2,1,0:T(2,128)} custom-call(s32[128]{0:T(128)S(1)} %copy-done.1, s16[128,168,128]{2,1,0:T(8,128)(2,1)S(1)} %all_to_all.15.reply), custom_call_target="tpu_custom_call" | custom-call | tf_op jit(solution)/shard_map/finish/pallas_call | solution.py:411
  (9 shorter events, 0.1 us)
Async XLA Ops:
  6.6 119.1 %all-to-all-start = ((bf16[128,136,256]{2,1,0:T(8,128)(2,1)}), bf16[128,136,256]{2,1,0:T(8,128)(2,1)}, u32[]{:S(2)}, u32[]{:S(2)}) async-start(bf16[128,136,256]{2,1,0:T(8,128)(2,1)} %bitcast.53), calls=%async_computation | async-start | bytes 17825792 | tf_op jit(solution)/shard_map/all_to_all | solution.py:341
  125.7 12.0 %copy-start.5 = (bf16[2,32,64,256]{3,2,1,0:T(8,128)(2,1)S(1)}, bf16[2,32,64,256]{3,2,1,0:T(8,128)(2,1)}, u32[]{:S(2)}) copy-start(bf16[2,32,64,256]{3,2,1,0:T(8,128)(2,1)} %param.5) | copy-start | bytes 6291460
  125.7 187.3 %all-to-all-start.1 = ((bf16[128,128,256]{2,1,0:T(8,128)(2,1)}), bf16[128,128,256]{2,1,0:T(8,128)(2,1)}, u32[]{:S(2)}, u32[]{:S(2)}) async-start(bf16[128,128,256]{2,1,0:T(8,128)(2,1)} %bitcast.52), calls=%async_computation.1 | async-start | bytes 16777216 | tf_op jit(solution)/shard_map/all_to_all | solution.py:341
  137.7 118.7 %copy-start.6 = (bf16[2,32,64,256]{3,2,1,0:T(8,128)(2,1)S(1)}, bf16[2,32,64,256]{3,2,1,0:T(8,128)(2,1)}, u32[]{:S(2)}) copy-start(bf16[2,32,64,256]{3,2,1,0:T(8,128)(2,1)} %param.5) | copy-start | bytes 6291460
  137.8 104.6 %collective-permute-start.1 = (bf16[2,8,64,256]{3,2,1,0:T(8,128)(2,1)S(1)}, bf16[2,8,64,256]{3,2,1,0:T(8,128)(2,1)S(1)}, u32[]{:S(2)}, u32[]{:S(2)}) collective-permute-start(bf16[2,8,64,256]{3,2,1,0:T(8,128)(2,1)S(1)} %get-tuple-element.15), channel_id=1, source_target_pairs={{8,0},{16,8},{24,16},{32,24},{40,32},{48,40},{56,48},{64,56},{72,6... | collective-permute-start | bytes 1572872 | tf_op jit(solution)/shard_map/ppermute | solution.py:36
  139.3 103.2 %collective-permute-start = (bf16[2,8,64,256]{3,2,1,0:T(8,128)(2,1)S(1)}, bf16[2,8,64,256]{3,2,1,0:T(8,128)(2,1)S(1)}, u32[]{:S(2)}, u32[]{:S(2)}) collective-permute-start(bf16[2,8,64,256]{3,2,1,0:T(8,128)(2,1)S(1)} %get-tuple-element.16), channel_id=1, source_target_pairs={{0,8},{8,16},{16,24},{24,32},{32,40},{40,48},{48,56},{56,64},{64,7... | collective-permute-start | bytes 1572872 | tf_op jit(solution)/shard_map/ppermute | solution.py:36
  242.5 16.4 %collective-permute-start.2 = (bf16[2,48,8,256]{3,2,1,0:T(8,128)(2,1)S(1)}, bf16[2,48,8,256]{3,2,1,0:T(8,128)(2,1)S(1)}, u32[]{:S(2)}, u32[]{:S(2)}) collective-permute-start(bf16[2,48,8,256]{3,2,1,0:T(8,128)(2,1)S(1)} %pad_maximum_fusion.3), channel_id=1, source_target_pairs={{0,1},{1,2},{2,3},{3,4},{4,5},{5,6},{6,7},{8,9},{9,10},{10,11},{11... | collective-permute-start | bytes 1179656 | tf_op jit(solution)/shard_map/ppermute | solution.py:36
  254.3 9.1 %collective-permute-start.3 = (bf16[2,48,8,256]{3,2,1,0:T(8,128)(2,1)S(1)}, bf16[2,48,8,256]{3,2,1,0:T(8,128)(2,1)S(1)}, u32[]{:S(2)}, u32[]{:S(2)}) collective-permute-start(bf16[2,48,8,256]{3,2,1,0:T(8,128)(2,1)S(1)} %pad_maximum_fusion.4), channel_id=1, source_target_pairs={{1,0},{2,1},{3,2},{4,3},{5,4},{6,5},{7,6},{9,8},{10,9},{11,10},{12... | collective-permute-start | bytes 1179656 | tf_op jit(solution)/shard_map/ppermute | solution.py:36
  258.9 4.5 %copy-start.7 = (bf16[2,48,8,256]{3,2,1,0:T(8,128)(2,1)}, bf16[2,48,8,256]{3,2,1,0:T(8,128)(2,1)S(1)}, u32[]{:S(2)}) copy-start(bf16[2,48,8,256]{3,2,1,0:T(8,128)(2,1)S(1)} %collective-permute-done.2) | copy-start | bytes 1179652
  289.8 1.5 copy-start.3
  291.4 2.3 copy-start.4
  313.0 1.8 copy-start
  314.8 0.7 copy-start.2
  330.6 71.7 %copy-start.1 = (s32[128]{0:T(128)S(1)}, s32[128]{0:T(128)}, u32[]{:S(2)}) copy-start(s32[128]{0:T(128)} %get-tuple-element.9.slots) | copy-start | bytes 1540

commit v7 on v2

--- a/solution.py
+++ b/solution.py
@@ -17,8 +17,9 @@
 LANES = SLOTS * QUERIES
 REPLY_ROWS = -(-(WINDOW + 1) // 8) * 8
 PEERS_A_STEP = 16
-BENCHES = 4
+BENCHES = 8
 FULL = 32767.0
+FINISH_VMEM = 16 << 20
 AXES = ("rows", "cols")
 
 
@@ -75,13 +76,13 @@
             count[i] = 0
             return carry
 
-        lax.fori_loop(0, LEVELS * peers, clear, 0, unroll=8)
+        lax.fori_loop(0, LEVELS * peers, clear, 0, unroll=32)
 
         def blank(i, carry):
             labels[i] = 0
             return carry
 
-        lax.fori_loop(0, LEVELS * SLOTS * peers, blank, 0, unroll=8)
+        lax.fori_loop(0, LEVELS * SLOTS * peers, blank, 0, unroll=32)
 
         def place(k, carry):
             for level in reversed(range(LEVELS)):
@@ -97,7 +98,7 @@
                     copy(k, slot).start()
             return carry
 
-        lax.fori_loop(0, blocks, place, 0)
+        lax.fori_loop(0, blocks, place, 0, unroll=4)
 
         lane = lax.broadcasted_iota(jnp.int32, notes.shape[1:], 1)
 
@@ -110,7 +111,7 @@
             notes[peer] = values.astype(jnp.float32).astype(jnp.bfloat16)
             return carry
 
-        lax.fori_loop(0, peers, note, 0, unroll=4)
+        lax.fori_loop(0, peers, note, 0, unroll=8)
         noted = pltpu.make_async_copy(notes, send.at[:, SLOTS * SIDE], note_sem)
         noted.start()
 
@@ -118,7 +119,7 @@
             copy(k, slots[last * blocks + k]).wait()
             return carry
 
-        lax.fori_loop(0, blocks, finish, 0)
+        lax.fori_loop(0, blocks, finish, 0, unroll=8)
         noted.wait()
 
     return kernel
@@ -136,8 +137,8 @@
             copy(k, slots[k]).wait()
             return carry
 
-        lax.fori_loop(0, blocks, place, 0)
-        lax.fori_loop(0, blocks, finish, 0)
+        lax.fori_loop(0, blocks, place, 0, unroll=4)
+        lax.fori_loop(0, blocks, finish, 0, unroll=8)
 
     return kernel
 
@@ -221,13 +222,14 @@
         for level, reply in enumerate((reply0, reply1)):
             for group in range(groups):
                 k = level * blocks + (step * groups + group) * 2
-                halves = []
-                for side in range(2):
-                    slot = slots[k + side]
-                    block = reply[slot // SLOTS].astype(jnp.int32)
-                    turned = pltpu.roll(block, QUERIES, 1)
-                    halves.append(jnp.where(slot % SLOTS == side, block, turned))
-                both = jnp.where(low, halves[0], halves[1]).astype(jnp.float32)
+                slot = [slots[k + side] for side in range(2)]
+                block = [reply[at // SLOTS].astype(jnp.int32) for at in slot]
+                straight = jnp.where(low, block[0], block[1])
+                turned = pltpu.roll(jnp.where(low, block[1], block[0]), QUERIES, 1)
+                kept = [slot[side] % SLOTS == side for side in range(2)]
+                left = jnp.where(kept[0], straight, turned)
+                right = jnp.where(kept[1], straight, turned)
+                both = jnp.where(low, left, right).astype(jnp.float32)
                 factor = jnp.exp2(both[WINDOW : WINDOW + 1]) * (scale / FULL)
                 out[:, level, group * LANES : (group + 1) * LANES] = both[:WINDOW] * factor
 
@@ -314,7 +316,7 @@
         )(arrived[1], arrived[level], strips)
         replies.append(exchange(served))
 
-    groups = 4
+    groups = 8
     width = groups * LANES
     whole = pl.BlockSpec((peers, REPLY_ROWS, LANES), lambda s, _: (0, 0, 0))
     out = pl.pallas_call(
@@ -326,6 +328,7 @@
             out_specs=pl.BlockSpec((WINDOW, LEVELS, width), lambda s, _: (0, 0, s)),
         ),
         out_shape=jax.ShapeDtypeStruct((WINDOW, LEVELS, blocks * QUERIES), jnp.float32),
+        compiler_params=pltpu.CompilerParams(vmem_limit_bytes=FINISH_VMEM),
         name="finish",
     )(slots, *replies)
     return out.transpose(1, 0, 2)

time: 402 us -> 393 us (0.978)
  Pallas kernels: 62.7 us -> 51.2 us
    pallas_call x2, Pallas kernels: 42.7 us -> 36 us  [steps(): pl.pallas_call(serve_body(level, maps[level].shape[1], across_of[level],...]
  transfers between devices with their start and end apart: 6 -> 6, of which waited for: 2 -> 2; matrix products, arithmetic and copies ran while one was open for 9% -> 10% of each run, Pallas kernels for 5% -> 4%
where the time goes in v7:
time: 393 us; the launch traced here: 392 us
  blocking collectives  158 us (40%)
  waiting for transfers between devices  108 us (27%)
  Pallas kernels  51.2 us (13%)
  starting transfers between devices  35.2 us (9%)
  other arithmetic  21.4 us (5%)
  local copies, waits for them, and re-layouts  17.5 us (4%)
    all_to_all x2, blocking collectives, exchange(): return lax.all_to_all(value, AXES, split_axis=0, concat_axis=0, tiled=True)  158 us
    ppermute x2, waiting for transfers between devices, swapped(): lax.ppermute(downward, axis, backward)  106 us
    pallas_call x2, Pallas kernels, steps(): pl.pallas_call(serve_body(level, maps[level].shape[1], across_of[level],...  36 us
    all_to_all x2, starting transfers between devices, exchange(): return lax.all_to_all(value, AXES, split_axis=0, concat_axis=0, tiled=True)  18.1 us
    ppermute x2, starting transfers between devices, swapped(): lax.ppermute(upward, axis, forward)  13.8 us
    reduce_sum x1, other arithmetic, pool_level(): return jnp.mean(pooled, axis=(2, 4)).astype(jnp.bfloat16)  10.7 us
    convert_element_type x1, local copies, waits for them, and re-layouts, pool_level(): level_map.astype(jnp.float32)  9.92 us
  transfers between devices with their start and end apart: 6, of which 2 were waited for; matrix products, arithmetic and copies ran while one was open for 10% of the time, Pallas kernels for 4%

profile of v7, /device:TPU:1, one launch (start us, length us, event | category | flops | bytes accessed | tf_op | source)
XLA Modules:
  0.0 392.2 jit_solution(14929409540259295450)
XLA Ops:
  0.0 6.6 %build1.1 = (bf16[128,17,8,256]{3,2,1,0:T(8,128)(2,1)}, s32[128]{0:T(128)}) custom-call(s32[2,1,64]{2,1,0:T(1,128)} %bitcast.56, s32[2,64]{1,0:T(2,128)} %tile.1, bf16[64,8,8,256]{3,2,1,0:T(8,128)(2,1)} %bitcast.53), custom_call_target="tpu_custom_call" | custom-call | tf_op jit(solution)/shard_map/build1/pallas_call | solution.py:256
  6.6 4.2 %build0.1 = bf16[128,16,8,256]{3,2,1,0:T(8,128)(2,1)} custom-call(s32[128]{0:T(128)} %get-tuple-element.7.slots, bf16[64,8,8,256]{3,2,1,0:T(8,128)(2,1)} %bitcast.54), custom_call_target="tpu_custom_call" | custom-call | tf_op jit(solution)/shard_map/build0/pallas_call | solution.py:273
  10.8 110.2 %all_to_all.20.queries = bf16[128,128,256]{2,1,0:T(8,128)(2,1)} all-to-all(bf16[128,128,256]{2,1,0:T(8,128)(2,1)} %bitcast.51), channel_id=1, replica_groups=mesh['rows'=16,'cols'=8] {'rows','cols'}, dimensions={0} | all-to-all | bytes 16777216 | tf_op jit(solution)/shard_map/all_to_all | solution.py:283
  121.0 0.0 copy-start.2
  121.0 7.8 %all-to-all-start = ((bf16[128,136,256]{2,1,0:T(8,128)(2,1)}), bf16[128,136,256]{2,1,0:T(8,128)(2,1)}, u32[]{:S(2)}, u32[]{:S(2)}) async-start(bf16[128,136,256]{2,1,0:T(8,128)(2,1)} %bitcast.52), calls=%async_computation | async-start | bytes 17825792 | tf_op jit(solution)/shard_map/all_to_all | solution.py:283
  128.8 0.0 copy-done.2
  128.8 0.1 fusion.11
  128.9 1.3 collective-permute-start.1
  130.2 4.0 %collective-permute-start = (bf16[2,8,64,256]{3,2,1,0:T(8,128)(2,1)S(1)}, bf16[2,8,64,256]{3,2,1,0:T(8,128)(2,1)S(1)}, u32[]{:S(2)}, u32[]{:S(2)}) collective-permute-start(bf16[2,8,64,256]{3,2,1,0:T(8,128)(2,1)S(1)} %get-tuple-element.12), channel_id=1, source_target_pairs={{0,8},{8,16},{16,24},{24,32},{32,40},{40,48},{48,56},{56,64},{64,7... | collective-permute-start | bytes 1572872 | tf_op jit(solution)/shard_map/ppermute | solution.py:30
  134.3 105.9 %collective-permute-done.1 = bf16[2,8,64,256]{3,2,1,0:T(8,128)(2,1)S(1)} collective-permute-done((bf16[2,8,64,256]{3,2,1,0:T(8,128)(2,1)S(1)}, bf16[2,8,64,256]{3,2,1,0:T(8,128)(2,1)S(1)}, u32[]{:S(2)}, u32[]{:S(2)}) %collective-permute-start.1) | collective-permute-done | bytes 524320 | tf_op jit(solution)/shard_map/ppermute | solution.py:30
  240.2 0.0 collective-permute-done
  240.3 0.1 pad_maximum_fusion.3
  240.3 9.8 %collective-permute-start.2 = (bf16[2,48,8,256]{3,2,1,0:T(8,128)(2,1)S(1)}, bf16[2,48,8,256]{3,2,1,0:T(8,128)(2,1)S(1)}, u32[]{:S(2)}, u32[]{:S(2)}) collective-permute-start(bf16[2,48,8,256]{3,2,1,0:T(8,128)(2,1)S(1)} %pad_maximum_fusion.3), channel_id=1, source_target_pairs={{0,1},{1,2},{2,3},{3,4},{4,5},{5,6},{6,7},{8,9},{9,10},{10,11},{11... | collective-permute-start | bytes 1179656 | tf_op jit(solution)/shard_map/ppermute | solution.py:30
  250.1 0.1 pad_maximum_fusion.4
  250.2 1.9 collective-permute-start.3
  252.2 0.1 constant_dynamic-update-slice_fusion.1
  252.4 0.0 copy-start.1
  252.4 2.5 collective-permute-done.2
  254.8 1.2 fusion.9
  256.0 1.1 fusion.7
  257.2 1.2 fusion.6
  258.3 1.2 fusion.5
  259.5 1.2 fusion.4
  260.7 1.2 fusion.3
  261.9 1.2 fusion.2
  263.0 0.0 collective-permute-done.3
  263.0 0.0 copy-done.1
  263.0 0.0 copy-start.3
  263.0 1.3 fusion.1
  264.3 0.0 all-to-all-done.notes.queries
  264.4 18.5 %shard_map.46 = s16[128,88,128]{2,1,0:T(8,128)(2,1)} custom-call(bf16[128,136,256]{2,1,0:T(8,128)(2,1)} %all-to-all-done.notes.queries, bf16[128,128,256]{2,1,0:T(8,128)(2,1)} %all_to_all.20.queries, bf16[640,16,256]{2,1,0:T(8,128)(2,1)} %bitcast.13.strips), custom_call_target="tpu_custom_call" | custom-call | tf_op jit(solution)/shard_map/pallas_call | solution.py:300
  282.9 0.0 copy-done.3
  282.9 10.3 %all-to-all-start.2 = ((s16[128,88,128]{2,1,0:T(8,128)(2,1)}), s16[128,88,128]{2,1,0:T(8,128)(2,1)S(1)}, u32[]{:S(2)}, u32[]{:S(2)}) async-start(s16[128,88,128]{2,1,0:T(8,128)(2,1)} %shard_map.46), calls=%async_computation.2 | async-start | bytes 5767168 | tf_op jit(solution)/shard_map/all_to_all | solution.py:283
  293.2 5.1 %maximum_convert_fusion = f32[2,48,80,256]{3,2,1,0:T(8,128)} fusion(bf16[2,48,8,256]{3,2,1,0:T(8,128)(2,1)} %copy-done.3, bf16[2,48,64,256]{3,2,1,0:T(8,128)(2,1)} %copy-done.1, bf16[2,48,8,256]{3,2,1,0:T(8,128)(2,1)S(1)} %collective-permute-done.2), kind=kLoop, calls=%fused_computation | loop fusion | flops 11796480 | bytes 11796480 | tf_op jit(solution)/shard_map/convert_element_type | solution.py:40
  298.3 9.9 %reshape.24 = f32[2,24,2,40,2,256]{5,4,3,2,1,0:T(2,128)} reshape(f32[2,48,80,256]{3,2,1,0:T(8,128)} %maximum_convert_fusion) | data formatting | bytes 15728640 | tf_op jit(solution)/shard_map/convert_element_type | solution.py:40
  308.2 10.7 %reduce_sum.9 = f32[2,24,40,256]{3,2,1,0:T(8,128)} reduce(f32[2,24,2,40,2,256]{5,4,3,2,1,0:T(2,128)} %reshape.24, f32[]{:T(128)} %constant.1.clone.1), dimensions={2,4}, to_apply=%region_0.0 | reduce | flops 1474560 | bytes 9830404 | tf_op jit(solution)/shard_map/reduce_sum | solution.py:43
  318.9 1.7 multiply_convert_fusion
  320.6 0.2 slice_bitcast_fusion.9
  320.8 1.3 pad_maximum_fusion
  322.1 17.5 %shard_map.47 = s16[128,88,128]{2,1,0:T(8,128)(2,1)} custom-call(bf16[128,136,256]{2,1,0:T(8,128)(2,1)} %all-to-all-done.notes.queries, bf16[128,136,256]{2,1,0:T(8,128)(2,1)} %all-to-all-done.notes.queries, bf16[192,16,256]{2,1,0:T(8,128)(2,1)} %bitcast.55), custom_call_target="tpu_custom_call" | custom-call | tf_op jit(solution)/shard_map/pallas_call | solution.py:300
  339.6 0.0 copy-start
  339.6 0.0 all-to-all-done.2.reply0
  339.6 48.2 %all_to_all.21.reply1 = s16[128,88,128]{2,1,0:T(8,128)(2,1)S(1)} all-to-all(s16[128,88,128]{2,1,0:T(8,128)(2,1)} %shard_map.47), channel_id=1, replica_groups=mesh['rows'=16,'cols'=8] {'rows','cols'}, dimensions={0} | all-to-all | bytes 5767168 | tf_op jit(solution)/shard_map/all_to_all | solution.py:283
  387.8 0.0 copy-done
  387.8 4.4 %finish.1 = f32[81,2,4096]{2,1,0:T(2,128)} custom-call(s32[128]{0:T(128)S(1)} %copy-done, s16[128,88,128]{2,1,0:T(8,128)(2,1)S(1)} %all-to-all-done.2.reply0, s16[128,88,128]{2,1,0:T(8,128)(2,1)S(1)} %all_to_all.21.reply1), custom_call_target="tpu_custom_call" | custom-call | tf_op jit(solution)/shard_map/finish/pallas_call | solution.py:322
  (5 shorter events, 0.1 us)
Async XLA Ops:
  121.0 7.8 %copy-start.2 = (bf16[2,32,64,256]{3,2,1,0:T(8,128)(2,1)S(1)}, bf16[2,32,64,256]{3,2,1,0:T(8,128)(2,1)}, u32[]{:S(2)}) copy-start(bf16[2,32,64,256]{3,2,1,0:T(8,128)(2,1)} %param.5) | copy-start | bytes 6291460
  121.0 143.4 %all-to-all-start = ((bf16[128,136,256]{2,1,0:T(8,128)(2,1)}), bf16[128,136,256]{2,1,0:T(8,128)(2,1)}, u32[]{:S(2)}, u32[]{:S(2)}) async-start(bf16[128,136,256]{2,1,0:T(8,128)(2,1)} %bitcast.52), calls=%async_computation | async-start | bytes 17825792 | tf_op jit(solution)/shard_map/all_to_all | solution.py:283
  128.9 111.3 %collective-permute-start.1 = (bf16[2,8,64,256]{3,2,1,0:T(8,128)(2,1)S(1)}, bf16[2,8,64,256]{3,2,1,0:T(8,128)(2,1)S(1)}, u32[]{:S(2)}, u32[]{:S(2)}) collective-permute-start(bf16[2,8,64,256]{3,2,1,0:T(8,128)(2,1)S(1)} %get-tuple-element.11), channel_id=1, source_target_pairs={{8,0},{16,8},{24,16},{32,24},{40,32},{48,40},{56,48},{64,56},{72,6... | collective-permute-start | bytes 1572872 | tf_op jit(solution)/shard_map/ppermute | solution.py:30
  130.2 110.0 %collective-permute-start = (bf16[2,8,64,256]{3,2,1,0:T(8,128)(2,1)S(1)}, bf16[2,8,64,256]{3,2,1,0:T(8,128)(2,1)S(1)}, u32[]{:S(2)}, u32[]{:S(2)}) collective-permute-start(bf16[2,8,64,256]{3,2,1,0:T(8,128)(2,1)S(1)} %get-tuple-element.12), channel_id=1, source_target_pairs={{0,8},{8,16},{16,24},{24,32},{32,40},{40,48},{48,56},{56,64},{64,7... | collective-permute-start | bytes 1572872 | tf_op jit(solution)/shard_map/ppermute | solution.py:30
  240.3 14.5 %collective-permute-start.2 = (bf16[2,48,8,256]{3,2,1,0:T(8,128)(2,1)S(1)}, bf16[2,48,8,256]{3,2,1,0:T(8,128)(2,1)S(1)}, u32[]{:S(2)}, u32[]{:S(2)}) collective-permute-start(bf16[2,48,8,256]{3,2,1,0:T(8,128)(2,1)S(1)} %pad_maximum_fusion.3), channel_id=1, source_target_pairs={{0,1},{1,2},{2,3},{3,4},{4,5},{5,6},{6,7},{8,9},{9,10},{10,11},{11... | collective-permute-start | bytes 1179656 | tf_op jit(solution)/shard_map/ppermute | solution.py:30
  250.2 12.8 %collective-permute-start.3 = (bf16[2,48,8,256]{3,2,1,0:T(8,128)(2,1)S(1)}, bf16[2,48,8,256]{3,2,1,0:T(8,128)(2,1)S(1)}, u32[]{:S(2)}, u32[]{:S(2)}) collective-permute-start(bf16[2,48,8,256]{3,2,1,0:T(8,128)(2,1)S(1)} %pad_maximum_fusion.4), channel_id=1, source_target_pairs={{1,0},{2,1},{3,2},{4,3},{5,4},{6,5},{7,6},{9,8},{10,9},{11,10},{12... | collective-permute-start | bytes 1179656 | tf_op jit(solution)/shard_map/ppermute | solution.py:30
  252.4 10.7 %copy-start.1 = (bf16[2,48,64,256]{3,2,1,0:T(8,128)(2,1)}, bf16[2,48,64,256]{3,2,1,0:T(8,128)(2,1)S(1)}, u32[]{:S(2)}) copy-start(bf16[2,48,64,256]{3,2,1,0:T(8,128)(2,1)S(1)} %constant_dynamic-update-slice_fusion) | copy-start | bytes 9437188
  263.0 19.8 %copy-start.3 = (bf16[2,48,8,256]{3,2,1,0:T(8,128)(2,1)}, bf16[2,48,8,256]{3,2,1,0:T(8,128)(2,1)S(1)}, u32[]{:S(2)}) copy-start(bf16[2,48,8,256]{3,2,1,0:T(8,128)(2,1)S(1)} %collective-permute-done.3) | copy-start | bytes 1179652
  282.9 56.7 %all-to-all-start.2 = ((s16[128,88,128]{2,1,0:T(8,128)(2,1)}), s16[128,88,128]{2,1,0:T(8,128)(2,1)S(1)}, u32[]{:S(2)}, u32[]{:S(2)}) async-start(s16[128,88,128]{2,1,0:T(8,128)(2,1)} %shard_map.46), calls=%async_computation.2 | async-start | bytes 5767168 | tf_op jit(solution)/shard_map/all_to_all | solution.py:283
  339.6 48.2 %copy-start = (s32[128]{0:T(128)S(1)}, s32[128]{0:T(128)}, u32[]{:S(2)}) copy-start(s32[128]{0:T(128)} %get-tuple-element.7.slots) | copy-start | bytes 1540

commit v8 on v7

--- a/solution.py
+++ b/solution.py
@@ -111,8 +111,8 @@
             notes[peer] = values.astype(jnp.float32).astype(jnp.bfloat16)
             return carry
 
-        lax.fori_loop(0, peers, note, 0, unroll=8)
-        noted = pltpu.make_async_copy(notes, send.at[:, SLOTS * SIDE], note_sem)
+        lax.fori_loop(0, peers, note, 0, unroll=16)
+        noted = pltpu.make_async_copy(notes, send.at[:, SLOTS * SIDE, :, pl.ds(0, 128)], note_sem)
         noted.start()
 
         def finish(k, carry):
@@ -264,7 +264,7 @@
         scratch_shapes=[
             pltpu.SMEM((LEVELS * peers,), jnp.int32),
             pltpu.SMEM((LEVELS * SLOTS * peers,), jnp.int32),
-            pltpu.VMEM((peers, SIDE, channels), jnp.bfloat16),
+            pltpu.VMEM((peers, SIDE, 128), jnp.bfloat16),
             pltpu.SemaphoreType.DMA((blocks,)),
             pltpu.SemaphoreType.DMA,
         ],

time: 393 us -> 393 us (level)
  no operation moved by 1% of the time
where the time goes in v8:
time: 393 us; the launch traced here: 392 us
  blocking collectives  158 us (40%)
  waiting for transfers between devices  108 us (27%)
  Pallas kernels  51 us (13%)
  starting transfers between devices  35.2 us (9%)
  other arithmetic  21.4 us (5%)
  local copies, waits for them, and re-layouts  17.5 us (4%)
    all_to_all x2, blocking collectives, exchange(): return lax.all_to_all(value, AXES, split_axis=0, concat_axis=0, tiled=True)  158 us
    ppermute x2, waiting for transfers between devices, swapped(): lax.ppermute(downward, axis, backward)  106 us
    pallas_call x2, Pallas kernels, steps(): pl.pallas_call(serve_body(level, maps[level].shape[1], across_of[level],...  36 us
    all_to_all x2, starting transfers between devices, exchange(): return lax.all_to_all(value, AXES, split_axis=0, concat_axis=0, tiled=True)  18.1 us
    ppermute x2, starting transfers between devices, swapped(): lax.ppermute(upward, axis, forward)  13.8 us
    reduce_sum x1, other arithmetic, pool_level(): return jnp.mean(pooled, axis=(2, 4)).astype(jnp.bfloat16)  10.7 us
    convert_element_type x1, local copies, waits for them, and re-layouts, pool_level(): level_map.astype(jnp.float32)  9.92 us
  transfers between devices with their start and end apart: 6, of which 2 were waited for; matrix products, arithmetic and copies ran while one was open for 10% of the time, Pallas kernels for 4%

profile of v8, /device:TPU:1, one launch (start us, length us, event | category | flops | bytes accessed | tf_op | source)
XLA Modules:
  0.0 392.0 jit_solution(10410244338583549077)
XLA Ops:
  0.0 6.4 %build1.1 = (bf16[128,17,8,256]{3,2,1,0:T(8,128)(2,1)}, s32[128]{0:T(128)}) custom-call(s32[2,1,64]{2,1,0:T(1,128)} %bitcast.56, s32[2,64]{1,0:T(2,128)} %tile.1, bf16[64,8,8,256]{3,2,1,0:T(8,128)(2,1)} %bitcast.53), custom_call_target="tpu_custom_call" | custom-call | tf_op jit(solution)/shard_map/build1/pallas_call | solution.py:256
  6.4 4.2 %build0.1 = bf16[128,16,8,256]{3,2,1,0:T(8,128)(2,1)} custom-call(s32[128]{0:T(128)} %get-tuple-element.7.slots, bf16[64,8,8,256]{3,2,1,0:T(8,128)(2,1)} %bitcast.54), custom_call_target="tpu_custom_call" | custom-call | tf_op jit(solution)/shard_map/build0/pallas_call | solution.py:273
  10.6 110.2 %all_to_all.20.queries = bf16[128,128,256]{2,1,0:T(8,128)(2,1)} all-to-all(bf16[128,128,256]{2,1,0:T(8,128)(2,1)} %bitcast.51), channel_id=1, replica_groups=mesh['rows'=16,'cols'=8] {'rows','cols'}, dimensions={0} | all-to-all | bytes 16777216 | tf_op jit(solution)/shard_map/all_to_all | solution.py:283
  120.8 0.0 copy-start.2
  120.8 7.8 %all-to-all-start = ((bf16[128,136,256]{2,1,0:T(8,128)(2,1)}), bf16[128,136,256]{2,1,0:T(8,128)(2,1)}, u32[]{:S(2)}, u32[]{:S(2)}) async-start(bf16[128,136,256]{2,1,0:T(8,128)(2,1)} %bitcast.52), calls=%async_computation | async-start | bytes 17825792 | tf_op jit(solution)/shard_map/all_to_all | solution.py:283
  128.6 0.0 copy-done.2
  128.6 0.1 fusion.11
  128.7 1.3 collective-permute-start.1
  130.0 4.0 %collective-permute-start = (bf16[2,8,64,256]{3,2,1,0:T(8,128)(2,1)S(1)}, bf16[2,8,64,256]{3,2,1,0:T(8,128)(2,1)S(1)}, u32[]{:S(2)}, u32[]{:S(2)}) collective-permute-start(bf16[2,8,64,256]{3,2,1,0:T(8,128)(2,1)S(1)} %get-tuple-element.12), channel_id=1, source_target_pairs={{0,8},{8,16},{16,24},{24,32},{32,40},{40,48},{48,56},{56,64},{64,7... | collective-permute-start | bytes 1572872 | tf_op jit(solution)/shard_map/ppermute | solution.py:30
  134.1 105.9 %collective-permute-done.1 = bf16[2,8,64,256]{3,2,1,0:T(8,128)(2,1)S(1)} collective-permute-done((bf16[2,8,64,256]{3,2,1,0:T(8,128)(2,1)S(1)}, bf16[2,8,64,256]{3,2,1,0:T(8,128)(2,1)S(1)}, u32[]{:S(2)}, u32[]{:S(2)}) %collective-permute-start.1) | collective-permute-done | bytes 524320 | tf_op jit(solution)/shard_map/ppermute | solution.py:30
  240.0 0.0 collective-permute-done
  240.0 0.1 pad_maximum_fusion.3
  240.1 9.8 %collective-permute-start.2 = (bf16[2,48,8,256]{3,2,1,0:T(8,128)(2,1)S(1)}, bf16[2,48,8,256]{3,2,1,0:T(8,128)(2,1)S(1)}, u32[]{:S(2)}, u32[]{:S(2)}) collective-permute-start(bf16[2,48,8,256]{3,2,1,0:T(8,128)(2,1)S(1)} %pad_maximum_fusion.3), channel_id=1, source_target_pairs={{0,1},{1,2},{2,3},{3,4},{4,5},{5,6},{6,7},{8,9},{9,10},{10,11},{11... | collective-permute-start | bytes 1179656 | tf_op jit(solution)/shard_map/ppermute | solution.py:30
  249.9 0.1 pad_maximum_fusion.4
  250.0 1.9 collective-permute-start.3
  251.9 0.1 constant_dynamic-update-slice_fusion.1
  252.1 0.0 copy-start.1
  252.2 2.5 collective-permute-done.2
  254.6 1.2 fusion.9
  255.8 1.1 fusion.7
  256.9 1.2 fusion.6
  258.1 1.2 fusion.5
  259.3 1.2 fusion.4
  260.5 1.2 fusion.3
  261.6 1.2 fusion.2
  262.8 0.0 collective-permute-done.3
  262.8 0.0 copy-done.1
  262.8 0.0 copy-start.3
  262.8 1.3 fusion.1
  264.1 0.0 all-to-all-done.notes.queries
  264.1 18.5 %shard_map.46 = s16[128,88,128]{2,1,0:T(8,128)(2,1)} custom-call(bf16[128,136,256]{2,1,0:T(8,128)(2,1)} %all-to-all-done.notes.queries, bf16[128,128,256]{2,1,0:T(8,128)(2,1)} %all_to_all.20.queries, bf16[640,16,256]{2,1,0:T(8,128)(2,1)} %bitcast.13.strips), custom_call_target="tpu_custom_call" | custom-call | tf_op jit(solution)/shard_map/pallas_call | solution.py:300
  282.7 0.0 copy-done.3
  282.7 10.3 %all-to-all-start.2 = ((s16[128,88,128]{2,1,0:T(8,128)(2,1)}), s16[128,88,128]{2,1,0:T(8,128)(2,1)S(1)}, u32[]{:S(2)}, u32[]{:S(2)}) async-start(s16[128,88,128]{2,1,0:T(8,128)(2,1)} %shard_map.46), calls=%async_computation.2 | async-start | bytes 5767168 | tf_op jit(solution)/shard_map/all_to_all | solution.py:283
  293.0 5.1 %maximum_convert_fusion = f32[2,48,80,256]{3,2,1,0:T(8,128)} fusion(bf16[2,48,8,256]{3,2,1,0:T(8,128)(2,1)} %copy-done.3, bf16[2,48,64,256]{3,2,1,0:T(8,128)(2,1)} %copy-done.1, bf16[2,48,8,256]{3,2,1,0:T(8,128)(2,1)S(1)} %collective-permute-done.2), kind=kLoop, calls=%fused_computation | loop fusion | flops 11796480 | bytes 11796480 | tf_op jit(solution)/shard_map/convert_element_type | solution.py:40
  298.1 9.9 %reshape.24 = f32[2,24,2,40,2,256]{5,4,3,2,1,0:T(2,128)} reshape(f32[2,48,80,256]{3,2,1,0:T(8,128)} %maximum_convert_fusion) | data formatting | bytes 15728640 | tf_op jit(solution)/shard_map/convert_element_type | solution.py:40
  308.0 10.7 %reduce_sum.9 = f32[2,24,40,256]{3,2,1,0:T(8,128)} reduce(f32[2,24,2,40,2,256]{5,4,3,2,1,0:T(2,128)} %reshape.24, f32[]{:T(128)} %constant.1.clone.1), dimensions={2,4}, to_apply=%region_0.0 | reduce | flops 1474560 | bytes 9830404 | tf_op jit(solution)/shard_map/reduce_sum | solution.py:43
  318.7 1.7 multiply_convert_fusion
  320.4 0.2 slice_bitcast_fusion.9
  320.6 1.3 pad_maximum_fusion
  321.9 17.5 %shard_map.47 = s16[128,88,128]{2,1,0:T(8,128)(2,1)} custom-call(bf16[128,136,256]{2,1,0:T(8,128)(2,1)} %all-to-all-done.notes.queries, bf16[128,136,256]{2,1,0:T(8,128)(2,1)} %all-to-all-done.notes.queries, bf16[192,16,256]{2,1,0:T(8,128)(2,1)} %bitcast.55), custom_call_target="tpu_custom_call" | custom-call | tf_op jit(solution)/shard_map/pallas_call | solution.py:300
  339.4 0.0 copy-start
  339.4 0.0 all-to-all-done.2.reply0
  339.4 48.2 %all_to_all.21.reply1 = s16[128,88,128]{2,1,0:T(8,128)(2,1)S(1)} all-to-all(s16[128,88,128]{2,1,0:T(8,128)(2,1)} %shard_map.47), channel_id=1, replica_groups=mesh['rows'=16,'cols'=8] {'rows','cols'}, dimensions={0} | all-to-all | bytes 5767168 | tf_op jit(solution)/shard_map/all_to_all | solution.py:283
  387.6 0.0 copy-done
  387.6 4.4 %finish.1 = f32[81,2,4096]{2,1,0:T(2,128)} custom-call(s32[128]{0:T(128)S(1)} %copy-done, s16[128,88,128]{2,1,0:T(8,128)(2,1)S(1)} %all-to-all-done.2.reply0, s16[128,88,128]{2,1,0:T(8,128)(2,1)S(1)} %all_to_all.21.reply1), custom_call_target="tpu_custom_call" | custom-call | tf_op jit(solution)/shard_map/finish/pallas_call | solution.py:322
  (5 shorter events, 0.1 us)
Async XLA Ops:
  120.8 7.8 %copy-start.2 = (bf16[2,32,64,256]{3,2,1,0:T(8,128)(2,1)S(1)}, bf16[2,32,64,256]{3,2,1,0:T(8,128)(2,1)}, u32[]{:S(2)}) copy-start(bf16[2,32,64,256]{3,2,1,0:T(8,128)(2,1)} %param.5) | copy-start | bytes 6291460
  120.8 143.4 %all-to-all-start = ((bf16[128,136,256]{2,1,0:T(8,128)(2,1)}), bf16[128,136,256]{2,1,0:T(8,128)(2,1)}, u32[]{:S(2)}, u32[]{:S(2)}) async-start(bf16[128,136,256]{2,1,0:T(8,128)(2,1)} %bitcast.52), calls=%async_computation | async-start | bytes 17825792 | tf_op jit(solution)/shard_map/all_to_all | solution.py:283
  128.7 111.3 %collective-permute-start.1 = (bf16[2,8,64,256]{3,2,1,0:T(8,128)(2,1)S(1)}, bf16[2,8,64,256]{3,2,1,0:T(8,128)(2,1)S(1)}, u32[]{:S(2)}, u32[]{:S(2)}) collective-permute-start(bf16[2,8,64,256]{3,2,1,0:T(8,128)(2,1)S(1)} %get-tuple-element.11), channel_id=1, source_target_pairs={{8,0},{16,8},{24,16},{32,24},{40,32},{48,40},{56,48},{64,56},{72,6... | collective-permute-start | bytes 1572872 | tf_op jit(solution)/shard_map/ppermute | solution.py:30
  130.0 110.0 %collective-permute-start = (bf16[2,8,64,256]{3,2,1,0:T(8,128)(2,1)S(1)}, bf16[2,8,64,256]{3,2,1,0:T(8,128)(2,1)S(1)}, u32[]{:S(2)}, u32[]{:S(2)}) collective-permute-start(bf16[2,8,64,256]{3,2,1,0:T(8,128)(2,1)S(1)} %get-tuple-element.12), channel_id=1, source_target_pairs={{0,8},{8,16},{16,24},{24,32},{32,40},{40,48},{48,56},{56,64},{64,7... | collective-permute-start | bytes 1572872 | tf_op jit(solution)/shard_map/ppermute | solution.py:30
  240.1 14.5 %collective-permute-start.2 = (bf16[2,48,8,256]{3,2,1,0:T(8,128)(2,1)S(1)}, bf16[2,48,8,256]{3,2,1,0:T(8,128)(2,1)S(1)}, u32[]{:S(2)}, u32[]{:S(2)}) collective-permute-start(bf16[2,48,8,256]{3,2,1,0:T(8,128)(2,1)S(1)} %pad_maximum_fusion.3), channel_id=1, source_target_pairs={{0,1},{1,2},{2,3},{3,4},{4,5},{5,6},{6,7},{8,9},{9,10},{10,11},{11... | collective-permute-start | bytes 1179656 | tf_op jit(solution)/shard_map/ppermute | solution.py:30
  250.0 12.8 %collective-permute-start.3 = (bf16[2,48,8,256]{3,2,1,0:T(8,128)(2,1)S(1)}, bf16[2,48,8,256]{3,2,1,0:T(8,128)(2,1)S(1)}, u32[]{:S(2)}, u32[]{:S(2)}) collective-permute-start(bf16[2,48,8,256]{3,2,1,0:T(8,128)(2,1)S(1)} %pad_maximum_fusion.4), channel_id=1, source_target_pairs={{1,0},{2,1},{3,2},{4,3},{5,4},{6,5},{7,6},{9,8},{10,9},{11,10},{12... | collective-permute-start | bytes 1179656 | tf_op jit(solution)/shard_map/ppermute | solution.py:30
  252.1 10.7 %copy-start.1 = (bf16[2,48,64,256]{3,2,1,0:T(8,128)(2,1)}, bf16[2,48,64,256]{3,2,1,0:T(8,128)(2,1)S(1)}, u32[]{:S(2)}) copy-start(bf16[2,48,64,256]{3,2,1,0:T(8,128)(2,1)S(1)} %constant_dynamic-update-slice_fusion) | copy-start | bytes 9437188
  262.8 19.8 %copy-start.3 = (bf16[2,48,8,256]{3,2,1,0:T(8,128)(2,1)}, bf16[2,48,8,256]{3,2,1,0:T(8,128)(2,1)S(1)}, u32[]{:S(2)}) copy-start(bf16[2,48,8,256]{3,2,1,0:T(8,128)(2,1)S(1)} %collective-permute-done.3) | copy-start | bytes 1179652
  282.7 56.7 %all-to-all-start.2 = ((s16[128,88,128]{2,1,0:T(8,128)(2,1)}), s16[128,88,128]{2,1,0:T(8,128)(2,1)S(1)}, u32[]{:S(2)}, u32[]{:S(2)}) async-start(s16[128,88,128]{2,1,0:T(8,128)(2,1)} %shard_map.46), calls=%async_computation.2 | async-start | bytes 5767168 | tf_op jit(solution)/shard_map/all_to_all | solution.py:283
  339.4 48.2 %copy-start = (s32[128]{0:T(128)S(1)}, s32[128]{0:T(128)}, u32[]{:S(2)}) copy-start(s32[128]{0:T(128)} %get-tuple-element.7.slots) | copy-start | bytes 1540
